TPU v7x, 32 devices: a whole 2x2x4 slice. The times are simulated.
32 devices in a mesh: wide: 8 (over y, x, core), narrow: 4 (over z).
Axes of the slice: x: 2, y: 2, z: 4, core: 2. Of those that a mesh axis runs over, the one named last changes fastest.
Arguments:
- schur_matrix: bfloat16 [8, 4, 3, 1024, 1024], P('wide', 'narrow')
- face_inverse: bfloat16 [8, 4, 3, 8, 128, 128], P('wide', 'narrow')
- deluxe: bfloat16 [8, 4, 3, 8, 128, 128], P('wide', 'narrow')
- primal_weight: float32 [8, 4, 3, 8, 128], P('wide', 'narrow'), may hold values from 0.05 to 0.3
- coarse_group: float32 [8, 96, 96], P('wide', 'narrow')
- coarse_map: float32 [8, 96, 8], P('wide', 'narrow'), may hold values from -0.625 to 0.625
- coarse_top: float32 [64, 64], P('wide')
- load_vector: bfloat16 [8, 4, 3, 8, 128, 128], P('wide', 'narrow'), may hold values from -6 to 6
- previous: bfloat16 [8, 4, 3, 8, 128, 128], P('wide', 'narrow'), may hold values from -3 to 3
- slot_count: int32 [8, 4], P('wide', 'narrow'), may hold values from 1 to 3, as said below
- partner: int32 [8, 4, 3, 8], P('wide', 'narrow'), may hold values from -1 to 2, as said below
- face_size: int32 [8, 4, 3, 8], P('wide', 'narrow'), may hold values from 0 to 128, as said below
Outputs:
- solution: float32 [8, 4, 3, 8, 128, 128], P('wide', 'narrow')
- residual: float32 [8, 4, 3, 8, 128, 128], P('wide', 'narrow')
Inputs may be any that keep to these rules, and one draw needn't show every extreme that they name: Slots of a device below its slot_count hold subdomains; the others are empty. `face_size`: both sides of a face with a partner have the same size; faces of empty slots have size 0, all other faces at least 32.
All inputs are finite; a program needn't handle non-finite values.
Results may differ from a plain program's by a relative error of at most 0.00355.
The roundings to bfloat16 on the way count: a program that leaves them out, or rounds other values in their place, can miss the bound.
Values may be sent and summed in bfloat16 or wider, within the bound.
No kernel may reach another device: no remote copies, remote signals or barrier semaphores. Data moves between devices by JAX's collectives and lax.ppermute only.
A program may use at most 128 MiB of HBM per device.

v0:
```python
import jax
import jax.numpy as jnp
from jax import lax
from jax.sharding import PartitionSpec as P

ITERS = 2


precise = lax.Precision.HIGHEST


def with_halo(block, sides, width, periodic):
    for axis, dim in sides:
        count = lax.axis_size(axis)
        forward = [(i, i + 1) for i in range(count - 1)]
        if periodic:
            forward.append((count - 1, 0))
        backward = [(target, source) for source, target in forward]
        low = lax.ppermute(
            lax.slice_in_dim(block, block.shape[dim] - width, None, axis=dim), axis, forward
        )
        high = lax.ppermute(lax.slice_in_dim(block, 0, width, axis=dim), axis, backward)
        block = jnp.concatenate([low, block, high], axis=dim)
    return block


def pick_partner(sources, partner):
    slot_total = sources.shape[1]
    chosen = partner[:, :, None] == jnp.arange(slot_total, dtype=jnp.int32)[None, None, :]
    spread = jnp.where(chosen[:, :, :, None, None], sources[None], jnp.zeros((), sources.dtype))
    return jnp.sum(spread, axis=2)


def face_sources(values, wide_got, narrow_got):
    return jnp.stack(
        [
            narrow_got[0],
            narrow_got[3],
            wide_got[0],
            wide_got[3],
            values[:, 5],
            values[:, 4],
            values[:, 7],
            values[:, 6],
        ],
        axis=0,
    )


def partner_full(values, partner):
    wide_got = with_halo(jnp.stack([values[:, 2], values[:, 3]], axis=0), (("wide", 0),), 1, True)
    narrow_got = with_halo(
        jnp.stack([values[:, 0], values[:, 1]], axis=0), (("narrow", 0),), 1, False
    )
    return pick_partner(face_sources(values, wide_got, narrow_got), partner)


def partner_half(values, partner):
    wide_got = with_halo(jnp.stack([values[:, 2], values[:, 3]], axis=0), (("wide", 0),), 1, True)
    narrow_got = with_halo(
        jnp.stack([values[:, 0], values[:, 1]], axis=0), (("narrow", 0),), 1, False
    )
    return pick_partner(face_sources(values, wide_got, narrow_got), partner)


def body(
    schur_matrix,
    face_inverse,
    deluxe,
    primal_weight,
    coarse_group,
    coarse_map,
    coarse_top,
    load_vector,
    previous,
    slot_count,
    partner,
    face_size,
):
    schur_matrix = schur_matrix[0, 0]
    face_inverse = face_inverse[0, 0]
    deluxe = deluxe[0, 0]
    primal_weight = primal_weight[0, 0]
    coarse_group = coarse_group[0]
    coarse_map = coarse_map[0]
    load_vector = load_vector[0, 0]
    previous = previous[0, 0]
    live_count = slot_count[0, 0]
    partner = partner[0, 0]
    face_size = face_size[0, 0]
    slot_total, face_total, face_width, columns = load_vector.shape
    block_order = schur_matrix.shape[1]
    slot_alive = jnp.arange(slot_total, dtype=jnp.int32)[:, None, None] < live_count
    inside = jnp.arange(face_width, dtype=jnp.int32)[None, None, :] < face_size[:, :, None]
    live_mask = jnp.where(jnp.logical_and(slot_alive, inside), 1.0, 0.0).astype(jnp.float32)[
        ..., None
    ]
    linked = (partner >= 0)[:, :, None, None]

    def global_inner(first_vec, second_vec, weights):
        return lax.psum(
            jnp.sum(weights * first_vec * second_vec, axis=(0, 1, 2)), ("wide", "narrow")
        )

    def operator(values):
        direction_half = values.astype(jnp.bfloat16)
        stacked = direction_half.reshape(slot_total, block_order, columns)
        result = jnp.einsum(
            "sij,sjr->sir", schur_matrix, stacked, preferred_element_type=jnp.float32
        )
        return live_mask * result.reshape(values.shape)

    def precondition(values):
        res_half = values.astype(jnp.bfloat16)
        scaled = live_mask * jnp.einsum(
            "sfkj,sfkr->sfjr", deluxe, res_half, preferred_element_type=jnp.float32
        )
        scaled_half = scaled.astype(jnp.bfloat16)
        local_part = jnp.einsum(
            "sfjk,sfkr->sfjr", face_inverse, scaled_half, preferred_element_type=jnp.float32
        )
        coarse_in = jnp.sum(primal_weight[..., None] * scaled, axis=2).reshape(
            slot_total * face_total, columns
        )
        group_vec = lax.all_gather(coarse_in, "narrow", axis=0, tiled=True)
        group_part = jnp.dot(coarse_group, group_vec, precision=precise)
        restricted = lax.psum(jnp.dot(coarse_map.T, coarse_in, precision=precise), "narrow")
        everyone = lax.all_gather(restricted, "wide", axis=0, tiled=True)
        top_part = jnp.dot(coarse_top, everyone, precision=precise)
        coarse_out = group_part + jnp.dot(coarse_map, top_part, precision=precise)
        correction = local_part + primal_weight[..., None] * coarse_out.reshape(
            slot_total, face_total, 1, columns
        )
        corr_half = (live_mask * correction).astype(jnp.bfloat16)
        weighted = live_mask * jnp.einsum(
            "sfjk,sfkr->sfjr", deluxe, corr_half, preferred_element_type=jnp.float32
        )
        assembled = weighted + partner_full(weighted, partner)
        return (assembled, weighted)

    def norm_of(values, weighted):
        return global_inner(values, weighted, 1.0)

    prev_full = previous.astype(jnp.float32)
    prev_partner = partner_half(previous, partner).astype(jnp.float32)
    averaged = live_mask * jnp.where(linked, 0.5 * (prev_full + prev_partner), prev_full)
    start_local = live_mask * load_vector.astype(jnp.float32) - operator(averaged)
    residual = start_local + partner_full(start_local, partner)
    solution = averaged
    precond, weighted = precondition(residual)
    precond_norm = norm_of(residual, weighted)
    direction = precond
    for iteration in range(ITERS):
        image_local = operator(direction)
        curvature = global_inner(direction, image_local, 1.0)
        image_full = image_local + partner_full(image_local, partner)
        step_size = precond_norm / curvature
        solution = solution + step_size * direction
        residual = residual - step_size * image_full
        if iteration + 1 < ITERS:
            precond, weighted = precondition(residual)
            next_norm = norm_of(residual, weighted)
            direction = precond + next_norm / precond_norm * direction
            precond_norm = next_norm
    return (solution[None, None], residual[None, None])


def solution(mesh):
    in_specs = (
        P("wide", "narrow", None, None, None),
        P("wide", "narrow", None, None, None, None),
        P("wide", "narrow", None, None, None, None),
        P("wide", "narrow", None, None, None),
        P("wide", "narrow", None),
        P("wide", "narrow", None),
        P("wide", None),
        P("wide", "narrow", None, None, None, None),
        P("wide", "narrow", None, None, None, None),
        P("wide", "narrow"),
        P("wide", "narrow", None, None),
        P("wide", "narrow", None, None),
    )
    out_specs = (
        P("wide", "narrow", None, None, None, None),
        P("wide", "narrow", None, None, None, None),
    )
    return jax.shard_map(body, mesh=mesh, in_specs=in_specs, out_specs=out_specs, check_vma=False)
```

profile of v0, /device:TPU:0, one launch (start us, length us, event | category | flops | bytes accessed | tf_op | source)
XLA Modules:
  0.0 334.1 jit_solution(3498991599465272584)
XLA Ops:
  0.6 1.1 slice_bitcast_fusion.44
  1.8 3.4 %collective-permute-start.3 = (bf16[1,3,128,128]{3,2,1,0:T(8,128)(2,1)S(1)}, bf16[1,3,128,128]{3,2,1,0:T(8,128)(2,1)}, u32[]{:S(2)}, u32[]{:S(2)}) collective-permute-start(bf16[1,3,128,128]{3,2,1,0:T(8,128)(2,1)S(1)} %get-tuple-element.33), channel_id=1, source_target_pairs={{4,0},{8,4},{12,8},{16,12},{20,16},{24,20},{28,24},{0,28},{5,1},{9... | collective-permute-start | bytes 294920 | tf_op jit(solution)/shard_map/ppermute | solution.py:22
  5.2 1.3 collective-permute-start.1
  6.5 5.2 %collective-permute-start = (bf16[1,3,128,128]{3,2,1,0:T(8,128)(2,1)S(1)}, bf16[1,3,128,128]{3,2,1,0:T(8,128)(2,1)}, u32[]{:S(2)}, u32[]{:S(2)}) collective-permute-start(bf16[1,3,128,128]{3,2,1,0:T(8,128)(2,1)S(1)} %get-tuple-element.36), channel_id=1, source_target_pairs={{0,1},{1,2},{2,3},{4,5},{5,6},{6,7},{8,9},{9,10},{10,11},{12,13},{... | collective-permute-start | bytes 294920 | tf_op jit(solution)/shard_map/ppermute | solution.py:19
  16.0 1.5 copy.131
  18.4 0.9 constant_dynamic-update-slice_fusion.6
  21.9 1.4 copy.132
  23.3 6.6 %fusion.23 = f32[3,1024,128]{1,2,0:T(8,128)} fusion(bf16[1,1,3,1024,1024]{4,3,2,1,0:T(8,128)(2,1)} %param.12, f32[3,1024,128]{1,2,0:T(8,128)S(1)} %copy.131, f32[3,1024,128]{1,2,0:T(8,128)} %copy.132, f32[3,1024]{1,0:T(4,128)S(1)} %copy-done.29, pred[3,1024]{1,0:T(4,128)(4,1)S(1)} %bitcast.426), kind=kOutput, calls=%fused_computation.50 | convolution fusion | flops 807272448 | bytes 11025408 | tf_op jit(solution)/shard_map/sij,sjr->sir/dot_general | solution.py:108
  29.9 1.9 copy.191
  33.1 2.9 collective-permute-start.4
  35.9 1.3 collective-permute-start.5
  37.2 1.9 collective-permute-start.7
  39.5 4.6 %collective-permute-done.5 = f32[1,3,128,128]{3,2,1,0:T(8,128)S(1)} collective-permute-done((f32[1,3,128,128]{3,2,1,0:T(8,128)S(1)}, f32[1,3,128,128]{3,2,1,0:T(8,128)S(1)}, u32[]{:S(2)}, u32[]{:S(2)}) %collective-permute-start.5) | collective-permute-done | bytes 196640 | tf_op jit(solution)/shard_map/ppermute | solution.py:22
  44.1 1.0 collective-permute-done.6
  46.0 1.0 copy-done.10
  47.0 2.0 multiply_reduce_fusion.5
  49.2 12.1 %psum.42 = f32[8,128]{1,0:T(8,128)S(1)} all-reduce(f32[8,128]{1,0:T(8,128)S(1)} %convolution_bitcast_fusion.1), channel_id=1, replica_groups=mesh['wide'=8,'narrow'=4] {'narrow'}, use_global_device_ids=true, to_apply=%region_3.4 | all-reduce | flops 1024 | bytes 8192 | tf_op jit(solution)/shard_map/psum | solution.py:127
  61.3 8.1 %all_gather.13 = f32[64,128]{1,0:T(8,128)S(1)} all-gather(f32[8,128]{1,0:T(8,128)S(1)} %psum.42), channel_id=1, replica_groups=mesh['wide'=8,'narrow'=4] {'wide'}, dimensions={0}, use_global_device_ids=true | all-gather | bytes 36864 | tf_op jit(solution)/shard_map/all_gather | solution.py:128
  69.4 13.1 %all_gather.12 = f32[96,128]{1,0:T(8,128)S(1)} all-gather(f32[24,128]{1,0:T(8,128)S(1)} %bitcast.423), channel_id=1, replica_groups=mesh['wide'=8,'narrow'=4] {'narrow'}, dimensions={0}, use_global_device_ids=true | all-gather | bytes 61440 | tf_op jit(solution)/shard_map/all_gather | solution.py:125
  83.0 2.5 multiply_bitcast_fusion.1
  85.5 1.6 collective-permute-start.8
  87.1 1.4 collective-permute-start.9
  89.1 1.2 collective-permute-done.8
  90.3 4.5 %collective-permute-done.9 = f32[1,3,128,128]{3,2,1,0:T(8,128)S(1)} collective-permute-done((f32[1,3,128,128]{3,2,1,0:T(8,128)S(1)}, f32[1,3,128,128]{3,2,1,0:T(8,128)S(1)}, u32[]{:S(2)}, u32[]{:S(2)}) %collective-permute-start.9) | collective-permute-done | bytes 196640 | tf_op jit(solution)/shard_map/ppermute | solution.py:22
  94.8 1.0 collective-permute-done.10
  97.3 2.0 fusion.93
  99.4 3.4 %fusion.26 = f32[3,1024,128]{1,2,0:T(8,128)} fusion(bf16[3,1024,128]{2,1,0:T(8,128)(2,1)S(1)} %bitcast.416, bf16[1,1,3,1024,1024]{4,3,2,1,0:T(8,128)(2,1)S(1)} %bitcast.400), kind=kOutput, calls=%fused_computation.51 | convolution fusion | flops 805306368 | bytes 8650752 | tf_op jit(solution)/shard_map/sij,sjr->sir/dot_general | solution.py:108
  102.8 3.0 copy.153
  105.8 1.9 multiply_reduce_fusion.3
  107.7 1.2 copy-done.17
  109.8 5.4 %collective-permute-start.12 = (f32[1,3,128,128]{3,2,1,0:T(8,128)}, f32[1,3,128,128]{3,2,1,0:T(8,128)}, u32[]{:S(2)}, u32[]{:S(2)}) collective-permute-start(f32[1,3,128,128]{3,2,1,0:T(8,128)} %get-tuple-element.24), channel_id=1, source_target_pairs={{0,1},{1,2},{2,3},{4,5},{5,6},{6,7},{8,9},{9,10},{10,11},{12,13},{... | collective-permute-start | bytes 589832 | tf_op jit(solution)/shard_map/ppermute | solution.py:19
  115.2 1.3 collective-permute-start.13
  117.0 40.9 %all-reduce = (f32[128]{0:T(128)S(1)}, f32[128]{0:T(128)S(1)}) all-reduce(f32[128]{0:T(128)S(1)} %get-tuple-element.20, f32[128]{0:T(128)S(1)} %get-tuple-element.8), channel_id=1, replica_groups=mesh['wide'=8,'narrow'=4] {'wide','narrow'}, use_global_device_ids=true, to_apply=%region_5.6 | all-reduce | flops 256 | bytes 2048 | tf_op jit(solution)/shard_map/psum | solution.py:101
  158.0 0.9 constant_dynamic-update-slice_fusion.19
  158.9 0.9 constant_dynamic-update-slice_fusion.18
  159.9 0.9 constant_dynamic-update-slice_fusion.17
  160.8 0.9 constant_dynamic-update-slice_fusion.16
  164.5 1.3 multiply_reduce_fusion.2
  165.9 10.2 %psum.45 = f32[8,128]{1,0:T(8,128)S(1)} all-reduce(f32[8,128]{1,0:T(8,128)S(1)} %convolution_bitcast_fusion), channel_id=1, replica_groups=mesh['wide'=8,'narrow'=4] {'narrow'}, use_global_device_ids=true, to_apply=%region_11.12 | all-reduce | flops 1024 | bytes 8192 | tf_op jit(solution)/shard_map/psum | solution.py:127
  176.1 9.9 %all_gather.15 = f32[64,128]{1,0:T(8,128)S(1)} all-gather(f32[8,128]{1,0:T(8,128)S(1)} %psum.45), channel_id=1, replica_groups=mesh['wide'=8,'narrow'=4] {'wide'}, dimensions={0}, use_global_device_ids=true | all-gather | bytes 36864 | tf_op jit(solution)/shard_map/all_gather | solution.py:128
  186.1 13.1 %all_gather.14 = f32[96,128]{1,0:T(8,128)S(1)} all-gather(f32[24,128]{1,0:T(8,128)S(1)} %bitcast.422), channel_id=1, replica_groups=mesh['wide'=8,'narrow'=4] {'narrow'}, dimensions={0}, use_global_device_ids=true | all-gather | bytes 61440 | tf_op jit(solution)/shard_map/all_gather | solution.py:125
  199.6 4.4 %multiply_reduce_fusion.1 = (f32[128]{0:T(128)}, f32[3,8,128,128]{3,2,1,0:T(8,128)}) fusion(f32[3,8,128,128]{3,2,1,0:T(8,128)} %copy-done.20, bf16[1,1,3,8,128,128]{5,4,3,2,1,0:T(8,128)(2,1)S(1)} %copy-done.25, f32[3,8,128]{2,1,0:T(8,128)S(1)} %fusion.32, bf16[3,8,128,128]{2,3,1,0:T(8,128)(2,1)S(1)} %get-tuple-element.40, f32[3,8,128]{2,1,0:T(8,128)S(1)} %bitcast.421, ...), kind=kOutput, calls=%fused_computation.39 | convolution fusion | flops 204078976 | bytes 5542400 | tf_op jit(solution)/shard_map/sfjk,sfkr->sfjr/dot_general | solution.py:135
  204.0 2.1 slice_bitcast_fusion.12
  206.1 2.0 collective-permute-start.16
  208.1 1.3 collective-permute-start.17
  209.4 40.3 %psum.46 = f32[128]{0:T(128)S(1)} all-reduce(f32[128]{0:T(128)S(1)} %copy-done.38), channel_id=1, replica_groups=mesh['wide'=8,'narrow'=4] {'wide','narrow'}, use_global_device_ids=true, to_apply=%region_13.14 | all-reduce | flops 128 | bytes 1024 | tf_op jit(solution)/shard_map/psum | solution.py:101
  249.8 1.0 collective-permute-start.19
  250.7 0.9 constant_dynamic-update-slice_fusion.23
  251.7 0.9 constant_dynamic-update-slice_fusion.22
  252.6 5.5 %collective-permute-done.18 = f32[1,3,128,128]{3,2,1,0:T(8,128)S(1)} collective-permute-done((f32[1,3,128,128]{3,2,1,0:T(8,128)S(1)}, f32[1,3,128,128]{3,2,1,0:T(8,128)S(1)}, u32[]{:S(2)}, u32[]{:S(2)}) %collective-permute-start.18) | collective-permute-done | bytes 196640 | tf_op jit(solution)/shard_map/ppermute | solution.py:19
  258.2 0.9 fusion.64
  259.1 0.9 fusion.63
  261.5 1.6 fusion.92
  263.1 3.4 %fusion.29 = f32[3,1024,128]{1,2,0:T(8,128)} fusion(bf16[3,1024,128]{2,1,0:T(8,128)(2,1)S(1)} %bitcast.417, bf16[1,1,3,1024,1024]{4,3,2,1,0:T(8,128)(2,1)S(1)} %bitcast.402), kind=kOutput, calls=%fused_computation.52 | convolution fusion | flops 805306368 | bytes 8650752 | tf_op jit(solution)/shard_map/sij,sjr->sir/dot_general | solution.py:108
  266.5 1.9 copy.172
  268.4 1.2 copy-done.15
  269.5 3.2 multiply_reduce_fusion
  272.7 38.1 %psum.47 = f32[128]{0:T(128)S(1)} all-reduce(f32[128]{0:T(128)S(1)} %get-tuple-element.4), channel_id=1, replica_groups=mesh['wide'=8,'narrow'=4] {'wide','narrow'}, use_global_device_ids=true, to_apply=%region_16.17 | all-reduce | flops 128 | bytes 1024 | tf_op jit(solution)/shard_map/psum | solution.py:101
  310.8 1.3 slice_bitcast_fusion.4
  312.1 1.3 collective-permute-start.21
  313.4 4.6 %collective-permute-start.20 = (f32[1,3,128,128]{3,2,1,0:T(8,128)S(1)}, f32[1,3,128,128]{3,2,1,0:T(8,128)S(1)}, u32[]{:S(2)}, u32[]{:S(2)}) collective-permute-start(f32[1,3,128,128]{3,2,1,0:T(8,128)S(1)} %get-tuple-element.15), channel_id=1, source_target_pairs={{0,1},{1,2},{2,3},{4,5},{5,6},{6,7},{8,9},{9,10},{10,11},{12,13},{... | collective-permute-start | bytes 589832 | tf_op jit(solution)/shard_map/ppermute | solution.py:19
  318.1 3.1 fusion.10
  321.8 7.8 %collective-permute-done.22 = f32[1,3,128,128]{3,2,1,0:T(8,128)S(1)} collective-permute-done((f32[1,3,128,128]{3,2,1,0:T(8,128)S(1)}, f32[1,3,128,128]{3,2,1,0:T(8,128)S(1)}, u32[]{:S(2)}, u32[]{:S(2)}) %collective-permute-start.22) | collective-permute-done | bytes 196640 | tf_op jit(solution)/shard_map/ppermute | solution.py:19
  332.0 2.2 fusion.16
  (192 shorter events, 21.3 us)
Async XLA Ops:
  0.6 46.3 %copy-start = (bf16[1,1,3,8,128,128]{5,4,3,2,1,0:T(8,128)(2,1)S(1)}, bf16[1,1,3,8,128,128]{5,4,3,2,1,0:T(8,128)(2,1)}, u32[]{:S(2)}) copy-start(bf16[1,1,3,8,128,128]{5,4,3,2,1,0:T(8,128)(2,1)} %param.14) | copy-start | bytes 2359300
  1.8 18.4 %collective-permute-start.3 = (bf16[1,3,128,128]{3,2,1,0:T(8,128)(2,1)S(1)}, bf16[1,3,128,128]{3,2,1,0:T(8,128)(2,1)}, u32[]{:S(2)}, u32[]{:S(2)}) collective-permute-start(bf16[1,3,128,128]{3,2,1,0:T(8,128)(2,1)S(1)} %get-tuple-element.33), channel_id=1, source_target_pairs={{4,0},{8,4},{12,8},{16,12},{20,16},{24,20},{28,24},{0,28},{5,1},{9... | collective-permute-start | bytes 294920 | tf_op jit(solution)/shard_map/ppermute | solution.py:22
  5.2 14.1 %collective-permute-start.2 = (bf16[1,3,128,128]{3,2,1,0:T(8,128)(2,1)S(1)}, bf16[1,3,128,128]{3,2,1,0:T(8,128)(2,1)}, u32[]{:S(2)}, u32[]{:S(2)}) collective-permute-start(bf16[1,3,128,128]{3,2,1,0:T(8,128)(2,1)S(1)} %get-tuple-element.34), channel_id=1, source_target_pairs={{0,4},{4,8},{8,12},{12,16},{16,20},{20,24},{24,28},{28,0},{1,5},{5... | collective-permute-start | bytes 294920 | tf_op jit(solution)/shard_map/ppermute | solution.py:19
  5.2 13.2 %collective-permute-start.1 = (bf16[1,3,128,128]{3,2,1,0:T(8,128)(2,1)S(1)}, bf16[1,3,128,128]{3,2,1,0:T(8,128)(2,1)}, u32[]{:S(2)}, u32[]{:S(2)}) collective-permute-start(bf16[1,3,128,128]{3,2,1,0:T(8,128)(2,1)S(1)} %get-tuple-element.35), channel_id=1, source_target_pairs={{1,0},{2,1},{3,2},{5,4},{6,5},{7,6},{9,8},{10,9},{11,10},{13,12},{... | collective-permute-start | bytes 294920 | tf_op jit(solution)/shard_map/ppermute | solution.py:22
  6.5 11.0 %collective-permute-start = (bf16[1,3,128,128]{3,2,1,0:T(8,128)(2,1)S(1)}, bf16[1,3,128,128]{3,2,1,0:T(8,128)(2,1)}, u32[]{:S(2)}, u32[]{:S(2)}) collective-permute-start(bf16[1,3,128,128]{3,2,1,0:T(8,128)(2,1)S(1)} %get-tuple-element.36), channel_id=1, source_target_pairs={{0,1},{1,2},{2,3},{4,5},{5,6},{6,7},{8,9},{9,10},{10,11},{12,13},{... | collective-permute-start | bytes 294920 | tf_op jit(solution)/shard_map/ppermute | solution.py:19
  12.4 3.6 %copy-start.36 = (pred[3,8]{1,0:T(4,128)(4,1)}, pred[3,8]{1,0:T(4,128)(4,1)S(1)}, u32[]{:S(2)}) copy-start(pred[3,8]{1,0:T(4,128)(4,1)S(1)} %broadcast_compare_fusion) | copy-start | bytes 76
  16.0 5.2 %copy-start.21 = (bf16[1,1,3,8,128,128]{5,4,3,2,1,0:T(8,128)(2,1)S(1)}, bf16[1,1,3,8,128,128]{5,4,3,2,1,0:T(8,128)(2,1)}, u32[]{:S(2)}) copy-start(bf16[1,1,3,8,128,128]{5,4,3,2,1,0:T(8,128)(2,1)} %param.20) | copy-start | bytes 2359300
  21.8 1.5 copy-start.23
  21.8 1.5 copy-start.29
  21.8 1.4 copy-start.31
  29.9 2.0 copy-start.26
  33.1 6.4 %collective-permute-start.4 = (f32[1,3,128,128]{3,2,1,0:T(8,128)S(1)}, f32[1,3,128,128]{3,2,1,0:T(8,128)S(1)}, u32[]{:S(2)}, u32[]{:S(2)}) collective-permute-start(f32[1,3,128,128]{3,2,1,0:T(8,128)S(1)} %get-tuple-element.32), channel_id=1, source_target_pairs={{0,1},{1,2},{2,3},{4,5},{5,6},{6,7},{8,9},{9,10},{10,11},{12,13},{... | collective-permute-start | bytes 589832 | tf_op jit(solution)/shard_map/ppermute | solution.py:19
  35.9 8.1 %collective-permute-start.5 = (f32[1,3,128,128]{3,2,1,0:T(8,128)S(1)}, f32[1,3,128,128]{3,2,1,0:T(8,128)S(1)}, u32[]{:S(2)}, u32[]{:S(2)}) collective-permute-start(f32[1,3,128,128]{3,2,1,0:T(8,128)S(1)} %get-tuple-element.31), channel_id=1, source_target_pairs={{1,0},{2,1},{3,2},{5,4},{6,5},{7,6},{9,8},{10,9},{11,10},{13,12},{... | collective-permute-start | bytes 589832 | tf_op jit(solution)/shard_map/ppermute | solution.py:22
  37.2 7.9 %collective-permute-start.7 = (f32[1,3,128,128]{3,2,1,0:T(8,128)S(1)}, f32[1,3,128,128]{3,2,1,0:T(8,128)S(1)}, u32[]{:S(2)}, u32[]{:S(2)}) collective-permute-start(f32[1,3,128,128]{3,2,1,0:T(8,128)S(1)} %get-tuple-element.29), channel_id=1, source_target_pairs={{4,0},{8,4},{12,8},{16,12},{20,16},{24,20},{28,24},{0,28},{5,1},{9... | collective-permute-start | bytes 589832 | tf_op jit(solution)/shard_map/ppermute | solution.py:22
  39.1 6.0 %collective-permute-start.6 = (f32[1,3,128,128]{3,2,1,0:T(8,128)S(1)}, f32[1,3,128,128]{3,2,1,0:T(8,128)S(1)}, u32[]{:S(2)}, u32[]{:S(2)}) collective-permute-start(f32[1,3,128,128]{3,2,1,0:T(8,128)S(1)} %get-tuple-element.30), channel_id=1, source_target_pairs={{0,4},{4,8},{8,12},{12,16},{16,20},{20,24},{24,28},{28,0},{1,5},{5... | collective-permute-start | bytes 589832 | tf_op jit(solution)/shard_map/ppermute | solution.py:19
  47.0 2.1 copy-start.4
  47.0 2.1 copy-start.33
  47.0 35.5 %copy-start.32 = (f32[8,64]{1,0:T(8,128)S(1)}, f32[8,64]{1,0:T(8,128)}, u32[]{:S(2)}) copy-start(f32[8,64]{1,0:T(8,128)} %param.18) | copy-start | bytes 6148
  47.0 35.6 %copy-start.30 = (f32[1,24,96]{2,1,0:T(8,128)S(1)}, f32[1,24,96]{2,1,0:T(8,128)}, u32[]{:S(2)}) copy-start(f32[1,24,96]{2,1,0:T(8,128)} %param.16) | copy-start | bytes 27652
  47.0 36.0 %copy-start.25 = (bf16[1,1,3,8,128,128]{5,4,3,2,1,0:T(8,128)(2,1)S(1)}, bf16[1,1,3,8,128,128]{5,4,3,2,1,0:T(8,128)(2,1)}, u32[]{:S(2)}) copy-start(bf16[1,1,3,8,128,128]{5,4,3,2,1,0:T(8,128)(2,1)} %param.13) | copy-start | bytes 2359300
  85.4 10.5 %copy-start.9 = (f32[3,8,128,128]{3,2,1,0:T(8,128)}, f32[3,8,128,128]{3,2,1,0:T(8,128)S(1)}, u32[]{:S(2)}) copy-start(f32[3,8,128,128]{3,2,1,0:T(8,128)S(1)} %multiply_bitcast_fusion.1) | copy-start | bytes 4718596
  85.4 13.9 %slice-start = ((s8[6291456]{0:T(1024)(128)(4,1)}), s8[4194304]{0:T(1024)(128)(4,1)S(1)}, s32[]{:S(2)}) async-start(s8[6291456]{0:T(1024)(128)(4,1)} %bitcast.399), calls=%async_computation | async-start | bytes 8388608
  85.5 4.7 %collective-permute-start.8 = (f32[1,3,128,128]{3,2,1,0:T(8,128)S(1)}, f32[1,3,128,128]{3,2,1,0:T(8,128)S(1)}, u32[]{:S(2)}, u32[]{:S(2)}) collective-permute-start(f32[1,3,128,128]{3,2,1,0:T(8,128)S(1)} %get-tuple-element.28), channel_id=1, source_target_pairs={{0,1},{1,2},{2,3},{4,5},{5,6},{6,7},{8,9},{9,10},{10,11},{12,13},{... | collective-permute-start | bytes 589832 | tf_op jit(solution)/shard_map/ppermute | solution.py:19
  87.1 7.7 %collective-permute-start.9 = (f32[1,3,128,128]{3,2,1,0:T(8,128)S(1)}, f32[1,3,128,128]{3,2,1,0:T(8,128)S(1)}, u32[]{:S(2)}, u32[]{:S(2)}) collective-permute-start(f32[1,3,128,128]{3,2,1,0:T(8,128)S(1)} %get-tuple-element.27), channel_id=1, source_target_pairs={{1,0},{2,1},{3,2},{5,4},{6,5},{7,6},{9,8},{10,9},{11,10},{13,12},{... | collective-permute-start | bytes 589832 | tf_op jit(solution)/shard_map/ppermute | solution.py:22
  88.5 7.3 %collective-permute-start.11 = (f32[1,3,128,128]{3,2,1,0:T(8,128)S(1)}, f32[1,3,128,128]{3,2,1,0:T(8,128)S(1)}, u32[]{:S(2)}, u32[]{:S(2)}) collective-permute-start(f32[1,3,128,128]{3,2,1,0:T(8,128)S(1)} %get-tuple-element.25), channel_id=1, source_target_pairs={{4,0},{8,4},{12,8},{16,12},{20,16},{24,20},{28,24},{0,28},{5,1},{9... | collective-permute-start | bytes 589832 | tf_op jit(solution)/shard_map/ppermute | solution.py:22
  88.6 7.2 %collective-permute-start.10 = (f32[1,3,128,128]{3,2,1,0:T(8,128)S(1)}, f32[1,3,128,128]{3,2,1,0:T(8,128)S(1)}, u32[]{:S(2)}, u32[]{:S(2)}) collective-permute-start(f32[1,3,128,128]{3,2,1,0:T(8,128)S(1)} %get-tuple-element.26), channel_id=1, source_target_pairs={{0,4},{4,8},{8,12},{12,16},{16,20},{20,24},{24,28},{28,0},{1,5},{5... | collective-permute-start | bytes 589832 | tf_op jit(solution)/shard_map/ppermute | solution.py:19
  95.9 1.4 copy-start.5
  96.0 3.4 %slice-start.1 = ((s8[6291456]{0:T(1024)(128)(4,1)}), s8[2097152]{0:T(1024)(128)(4,1)S(1)}, s32[]{:S(2)}) async-start(s8[6291456]{0:T(1024)(128)(4,1)} %bitcast.399), calls=%async_computation.1 | async-start | bytes 4194304
  99.3 6.5 %copy-start.1 = (f32[3,8,128,128]{3,2,1,0:T(8,128)}, f32[3,8,128,128]{3,2,1,0:T(8,128)S(1)}, u32[]{:S(2)}) copy-start(f32[3,8,128,128]{3,2,1,0:T(8,128)S(1)} %get-tuple-element.11) | copy-start | bytes 4718596
  109.8 52.0 %copy-start.18 = (f32[3,8,128,128]{3,2,1,0:T(8,128)S(1)}, f32[3,8,128,128]{3,2,1,0:T(8,128)}, u32[]{:S(2)}) copy-start(f32[3,8,128,128]{3,2,1,0:T(8,128)} %copy-done.17) | copy-start | bytes 4718596
  109.8 48.2 %collective-permute-start.12 = (f32[1,3,128,128]{3,2,1,0:T(8,128)}, f32[1,3,128,128]{3,2,1,0:T(8,128)}, u32[]{:S(2)}, u32[]{:S(2)}) collective-permute-start(f32[1,3,128,128]{3,2,1,0:T(8,128)} %get-tuple-element.24), channel_id=1, source_target_pairs={{0,1},{1,2},{2,3},{4,5},{5,6},{6,7},{8,9},{9,10},{10,11},{12,13},{... | collective-permute-start | bytes 589832 | tf_op jit(solution)/shard_map/ppermute | solution.py:19
  115.2 43.8 %collective-permute-start.13 = (f32[1,3,128,128]{3,2,1,0:T(8,128)}, f32[1,3,128,128]{3,2,1,0:T(8,128)}, u32[]{:S(2)}, u32[]{:S(2)}) collective-permute-start(f32[1,3,128,128]{3,2,1,0:T(8,128)} %get-tuple-element.23), channel_id=1, source_target_pairs={{1,0},{2,1},{3,2},{5,4},{6,5},{7,6},{9,8},{10,9},{11,10},{13,12},{... | collective-permute-start | bytes 589832 | tf_op jit(solution)/shard_map/ppermute | solution.py:22
  116.4 44.4 %collective-permute-start.15 = (f32[1,3,128,128]{3,2,1,0:T(8,128)S(1)}, f32[1,3,128,128]{3,2,1,0:T(8,128)}, u32[]{:S(2)}, u32[]{:S(2)}) collective-permute-start(f32[1,3,128,128]{3,2,1,0:T(8,128)S(1)} %get-tuple-element.21), channel_id=1, source_target_pairs={{4,0},{8,4},{12,8},{16,12},{20,16},{24,20},{28,24},{0,28},{5,1},{9... | collective-permute-start | bytes 589832 | tf_op jit(solution)/shard_map/ppermute | solution.py:22
  116.5 43.4 %collective-permute-start.14 = (f32[1,3,128,128]{3,2,1,0:T(8,128)}, f32[1,3,128,128]{3,2,1,0:T(8,128)}, u32[]{:S(2)}, u32[]{:S(2)}) collective-permute-start(f32[1,3,128,128]{3,2,1,0:T(8,128)} %get-tuple-element.22), channel_id=1, source_target_pairs={{0,4},{4,8},{8,12},{12,16},{16,20},{20,24},{24,28},{28,0},{1,5},{5... | collective-permute-start | bytes 589832 | tf_op jit(solution)/shard_map/ppermute | solution.py:19
  157.9 3.9 %copy-start.39 = (f32[128]{0:T(128)}, f32[128]{0:T(128)S(1)}, u32[]{:S(2)}) copy-start(f32[128]{0:T(128)S(1)} %get-tuple-element.2) | copy-start | bytes 1540
  158.0 4.5 %copy-start.34 = (f32[128]{0:T(128)}, f32[128]{0:T(128)S(1)}, u32[]{:S(2)}) copy-start(f32[128]{0:T(128)S(1)} %div.9) | copy-start | bytes 1540
  161.9 1.4 copy-start.6
  204.0 5.4 %copy-start.38 = (f32[128]{0:T(128)S(1)}, f32[128]{0:T(128)}, u32[]{:S(2)}) copy-start(f32[128]{0:T(128)} %get-tuple-element.41) | copy-start | bytes 1540
  204.0 45.7 %copy-start.40 = (f32[128]{0:T(128)S(1)}, f32[128]{0:T(128)}, u32[]{:S(2)}) copy-start(f32[128]{0:T(128)} %copy-done.39) | copy-start | bytes 1540
  204.0 59.0 %slice-start.2 = ((s8[6291456]{0:T(1024)(128)(4,1)}), s8[2097152]{0:T(1024)(128)(4,1)S(1)}, s32[]{:S(2)}) async-start(s8[6291456]{0:T(1024)(128)(4,1)} %bitcast.401), calls=%async_computation.2 | async-start | bytes 4194304
  206.1 44.6 %collective-permute-start.16 = (f32[1,3,128,128]{3,2,1,0:T(8,128)}, f32[1,3,128,128]{3,2,1,0:T(8,128)}, u32[]{:S(2)}, u32[]{:S(2)}) collective-permute-start(f32[1,3,128,128]{3,2,1,0:T(8,128)} %get-tuple-element.19), channel_id=1, source_target_pairs={{0,1},{1,2},{2,3},{4,5},{5,6},{6,7},{8,9},{9,10},{10,11},{12,13},{... | collective-permute-start | bytes 589832 | tf_op jit(solution)/shard_map/ppermute | solution.py:19
  208.1 43.6 %collective-permute-start.17 = (f32[1,3,128,128]{3,2,1,0:T(8,128)S(1)}, f32[1,3,128,128]{3,2,1,0:T(8,128)}, u32[]{:S(2)}, u32[]{:S(2)}) collective-permute-start(f32[1,3,128,128]{3,2,1,0:T(8,128)S(1)} %get-tuple-element.18), channel_id=1, source_target_pairs={{1,0},{2,1},{3,2},{5,4},{6,5},{7,6},{9,8},{10,9},{11,10},{13,12},{... | collective-permute-start | bytes 589832 | tf_op jit(solution)/shard_map/ppermute | solution.py:22
  249.7 10.4 %copy-start.41 = (f32[128]{0:T(128)}, f32[128]{0:T(128)S(1)}, u32[]{:S(2)}) copy-start(f32[128]{0:T(128)S(1)} %psum.46) | copy-start | bytes 1540
  249.7 10.3 %copy-start.19 = (f32[3,8,128,128]{3,2,1,0:T(8,128)S(1)}, f32[3,8,128,128]{3,2,1,0:T(8,128)}, u32[]{:S(2)}) copy-start(f32[3,8,128,128]{3,2,1,0:T(8,128)} %get-tuple-element.42) | copy-start | bytes 4718596
  249.8 8.4 %collective-permute-start.19 = (f32[1,3,128,128]{3,2,1,0:T(8,128)S(1)}, f32[1,3,128,128]{3,2,1,0:T(8,128)S(1)}, u32[]{:S(2)}, u32[]{:S(2)}) collective-permute-start(f32[1,3,128,128]{3,2,1,0:T(8,128)S(1)} %get-tuple-element.16), channel_id=1, source_target_pairs={{4,0},{8,4},{12,8},{16,12},{20,16},{24,20},{28,24},{0,28},{5,1},{9... | collective-permute-start | bytes 589832 | tf_op jit(solution)/shard_map/ppermute | solution.py:22
  250.7 7.4 %collective-permute-start.18 = (f32[1,3,128,128]{3,2,1,0:T(8,128)S(1)}, f32[1,3,128,128]{3,2,1,0:T(8,128)S(1)}, u32[]{:S(2)}, u32[]{:S(2)}) collective-permute-start(f32[1,3,128,128]{3,2,1,0:T(8,128)S(1)} %get-tuple-element.17), channel_id=1, source_target_pairs={{0,4},{4,8},{8,12},{12,16},{16,20},{20,24},{24,28},{28,0},{1,5},{5... | collective-permute-start | bytes 589832 | tf_op jit(solution)/shard_map/ppermute | solution.py:19
  260.1 1.4 copy-start.2
  260.2 2.9 slice-start.3
  269.5 41.3 %copy-start.42 = (f32[128]{0:T(128)S(1)}, f32[128]{0:T(128)}, u32[]{:S(2)}) copy-start(f32[128]{0:T(128)} %copy-done.41) | copy-start | bytes 1540
  269.5 48.5 %copy-start.22 = (bf16[1,1,3,8,128,128]{5,4,3,2,1,0:T(8,128)(2,1)S(1)}, bf16[1,1,3,8,128,128]{5,4,3,2,1,0:T(8,128)(2,1)}, u32[]{:S(2)}) copy-start(bf16[1,1,3,8,128,128]{5,4,3,2,1,0:T(8,128)(2,1)} %param.20) | copy-start | bytes 2359300
  272.7 45.3 %copy-start.3 = (f32[3,8,128,128]{3,2,1,0:T(8,128)S(1)}, f32[3,8,128,128]{3,2,1,0:T(8,128)}, u32[]{:S(2)}) copy-start(f32[3,8,128,128]{3,2,1,0:T(8,128)} %copy-done.1) | copy-start | bytes 4718596
  272.7 45.3 %copy-start.35 = (f32[128]{0:T(128)S(1)}, f32[128]{0:T(128)}, u32[]{:S(2)}) copy-start(f32[128]{0:T(128)} %copy-done.34) | copy-start | bytes 1540
  272.7 45.3 %copy-start.37 = (pred[3,8]{1,0:T(4,128)(4,1)S(1)}, pred[3,8]{1,0:T(4,128)(4,1)}, u32[]{:S(2)}) copy-start(pred[3,8]{1,0:T(4,128)(4,1)} %copy-done.36) | copy-start | bytes 76
  312.1 9.6 %collective-permute-start.21 = (f32[1,3,128,128]{3,2,1,0:T(8,128)S(1)}, f32[1,3,128,128]{3,2,1,0:T(8,128)S(1)}, u32[]{:S(2)}, u32[]{:S(2)}) collective-permute-start(f32[1,3,128,128]{3,2,1,0:T(8,128)S(1)} %get-tuple-element.14), channel_id=1, source_target_pairs={{1,0},{2,1},{3,2},{5,4},{6,5},{7,6},{9,8},{10,9},{11,10},{13,12},{... | collective-permute-start | bytes 589832 | tf_op jit(solution)/shard_map/ppermute | solution.py:22
  313.4 8.3 %collective-permute-start.20 = (f32[1,3,128,128]{3,2,1,0:T(8,128)S(1)}, f32[1,3,128,128]{3,2,1,0:T(8,128)S(1)}, u32[]{:S(2)}, u32[]{:S(2)}) collective-permute-start(f32[1,3,128,128]{3,2,1,0:T(8,128)S(1)} %get-tuple-element.15), channel_id=1, source_target_pairs={{0,1},{1,2},{2,3},{4,5},{5,6},{6,7},{8,9},{9,10},{10,11},{12,13},{... | collective-permute-start | bytes 589832 | tf_op jit(solution)/shard_map/ppermute | solution.py:19
  318.0 11.6 %copy-start.24 = (f32[3,8,128,128]{3,2,1,0:T(8,128)S(1)}, f32[3,8,128,128]{3,2,1,0:T(8,128)}, u32[]{:S(2)}) copy-start(f32[3,8,128,128]{3,2,1,0:T(8,128)} %get-tuple-element.5) | copy-start | bytes 4718596
  318.0 12.2 %copy-start.16 = (f32[3,1024,128]{2,1,0:T(8,128)S(1)}, f32[3,1024,128]{2,1,0:T(8,128)}, u32[]{:S(2)}) copy-start(f32[3,1024,128]{2,1,0:T(8,128)} %copy-done.15) | copy-start | bytes 4718596
  318.0 12.2 %copy-start.27 = (bf16[1,1,3,8,128,128]{5,4,3,2,1,0:T(8,128)(2,1)S(1)}, bf16[1,1,3,8,128,128]{5,4,3,2,1,0:T(8,128)(2,1)}, u32[]{:S(2)}) copy-start(bf16[1,1,3,8,128,128]{5,4,3,2,1,0:T(8,128)(2,1)} %param.19) | copy-start | bytes 2359300
  321.2 8.3 %collective-permute-start.23 = (f32[1,3,128,128]{3,2,1,0:T(8,128)S(1)}, f32[1,3,128,128]{3,2,1,0:T(8,128)S(1)}, u32[]{:S(2)}, u32[]{:S(2)}) collective-permute-start(f32[1,3,128,128]{3,2,1,0:T(8,128)S(1)} %get-tuple-element.12), channel_id=1, source_target_pairs={{4,0},{8,4},{12,8},{16,12},{20,16},{24,20},{28,24},{0,28},{5,1},{9... | collective-permute-start | bytes 589832 | tf_op jit(solution)/shard_map/ppermute | solution.py:22
  321.5 8.0 %collective-permute-start.22 = (f32[1,3,128,128]{3,2,1,0:T(8,128)S(1)}, f32[1,3,128,128]{3,2,1,0:T(8,128)S(1)}, u32[]{:S(2)}, u32[]{:S(2)}) collective-permute-start(f32[1,3,128,128]{3,2,1,0:T(8,128)S(1)} %get-tuple-element.13), channel_id=1, source_target_pairs={{0,4},{4,8},{8,12},{12,16},{16,20},{20,24},{24,28},{28,0},{1,5},{5... | collective-permute-start | bytes 589832 | tf_op jit(solution)/shard_map/ppermute | solution.py:19
  321.7 8.5 %copy-start.14 = (f32[3,8,128,128]{3,2,1,0:T(8,128)S(1)}, f32[3,8,128,128]{3,2,1,0:T(8,128)}, u32[]{:S(2)}) copy-start(f32[3,8,128,128]{3,2,1,0:T(8,128)} %copy-done.13) | copy-start | bytes 4718596
  329.6 1.4 copy-start.12
  329.7 1.8 copy-start.8
  329.7 2.3 copy-start.11
  (7 other events, 8.4 us)
where the time goes:
time: 336 us; the launch traced here: 334 us
  blocking collectives  186 us (55%)
  local copies, waits for them, and re-layouts  38.2 us (11%)
  starting transfers between devices  37.2 us (11%)
  waiting for transfers between devices  25.9 us (8%)
  matrix products  24.9 us (7%)
  other arithmetic  19.7 us (6%)
    psum x3, blocking collectives, global_inner(): lax.psum(jnp.sum(weights * first_vec * second_vec, axis=(0, 1, 2)), ('wid...  119 us
    all_gather x2, blocking collectives, precondition(): group_vec = lax.all_gather(coarse_in, 'narrow', axis=0, tiled=True)  26.2 us
    unnamed x141, local copies, waits for them, and re-layouts  23 us
    ppermute x12, starting transfers between devices, with_halo(): lax.ppermute(lax.slice_in_dim(block, block.shape[dim] - width, None, axis...  22.7 us
    psum x2, blocking collectives, precondition(): lax.psum(jnp.dot(coarse_map.T, coarse_in, precision=precise), 'narrow')  22.3 us
    all_gather x2, blocking collectives, precondition(): everyone = lax.all_gather(restricted, 'wide', axis=0, tiled=True)  18 us
    ppermute x12, waiting for transfers between devices, with_halo(): lax.ppermute(lax.slice_in_dim(block, block.shape[dim] - width, None, axis...  16.8 us
    ppermute x12, starting transfers between devices, with_halo(): lax.ppermute(lax.slice_in_dim(block, 0, width, axis=dim), axis, backward)  14.5 us
  transfers between devices with their start and end apart: 24, of which 8 were waited for; matrix products, arithmetic and copies ran while one was open for 5% of the time, Pallas kernels for 0%

commit v1 on v0

v1 whole, which is shorter than its diff:
```python
import jax
import jax.numpy as jnp
from jax import lax
from jax.experimental import pallas as pl
from jax.experimental.pallas import tpu as pltpu
from jax.sharding import PartitionSpec as P

precise = lax.Precision.HIGHEST
F32 = jnp.float32
BF16 = jnp.bfloat16
AXES = ("wide", "narrow")
VMEM = pl.BlockSpec(memory_space=pltpu.VMEM)
SMEM = pl.BlockSpec(memory_space=pltpu.SMEM)


def call(kernel, name, scalars, arrays, outs, scratch=()):
    return pl.pallas_call(
        kernel,
        name=name,
        in_specs=[SMEM] * len(scalars) + [VMEM] * len(arrays),
        out_specs=[VMEM] * len(outs),
        out_shape=[jax.ShapeDtypeStruct(shape, dtype) for shape, dtype in outs],
        scratch_shapes=list(scratch),
        compiler_params=pltpu.CompilerParams(vmem_limit_bytes=40 * 1024 * 1024),
    )(*scalars, *arrays)


def odd(axis):
    return lax.axis_index(axis) % 2 == 1


def from_face(own, got, slot, face):
    if face >= 4:
        return own[slot, face ^ 1]
    near, far = (got[0], got[1]) if face < 2 else (got[2], got[3])
    first = near[slot]
    second = far[slot]
    is_odd = odd("narrow") if face < 2 else odd("wide")
    if face % 2:
        return jnp.where(is_odd, second, first)
    return jnp.where(is_odd, first, second)


def send_faces(sends, slot, faces):
    odd_n = odd("narrow")
    odd_w = odd("wide")
    kind = sends[0].dtype
    sends[0][slot] = jnp.where(odd_n, faces[0], faces[1]).astype(kind)
    sends[1][slot] = jnp.where(odd_n, faces[1], faces[0]).astype(kind)
    sends[2][slot] = jnp.where(odd_w, faces[2], faces[3]).astype(kind)
    sends[3][slot] = jnp.where(odd_w, faces[3], faces[2]).astype(kind)


def live_rows(count, size, slot, face, shape):
    rows = lax.broadcasted_iota(jnp.int32, shape, 0)
    return rows < jnp.where(slot < count[0, 0], size[slot, face], 0)


def fold(values):
    rows, columns = values.shape
    return jnp.sum(values.reshape(rows // 8, 8, columns), axis=0)


def total_rows(gathered):
    return jnp.sum(gathered[...], axis=0)


def multiply(schur, vec, slot, width):
    span = 2 * width
    order = vec.shape[0]
    parts = []
    for start in range(0, order, span):
        block = jnp.dot(
            schur[slot, start : start + span], vec[...], preferred_element_type=F32
        )
        parts += [block[:width], block[width:]]
    return parts


def start_kernel(partner, size, count, previous, load, schur, g0, g1, g2, g3, averaged, local, s0, s1, s2, s3, vec):
    got = (g0, g1, g2, g3)
    slots, faces, width, columns = previous.shape

    def one_slot(slot, carry):
        for face in range(faces):
            other = partner[slot, face]
            mine = previous[slot, face].astype(F32)
            theirs = from_face(previous, got, jnp.maximum(other, 0), face).astype(F32)
            value = jnp.where(other >= 0, 0.5 * (mine + theirs), mine)
            value = jnp.where(live_rows(count, size, slot, face, mine.shape), value, 0.0)
            averaged[slot, face] = value
            vec[face * width : (face + 1) * width] = value.astype(BF16)
        products = multiply(schur, vec, slot, width)
        sent = []
        for face in range(faces):
            value = load[slot, face].astype(F32) - products[face]
            value = jnp.where(live_rows(count, size, slot, face, value.shape), value, 0.0)
            local[slot, face] = value
            if face < 4:
                sent.append(value)
        send_faces((s0, s1, s2, s3), slot, sent)
        return carry

    lax.fori_loop(0, slots, one_slot, 0)


def scale_slot(slot, values, partner_size, deluxe, spread_weight, scaled, coarse_in):
    count, size = partner_size
    rows = []
    for face, value in enumerate(values):
        part = lax.dot_general(
            deluxe[slot, face],
            value.astype(BF16),
            (((0,), (0,)), ((), ())),
            preferred_element_type=F32,
        )
        part = jnp.where(live_rows(count, size, slot, face, part.shape), part, 0.0)
        scaled[slot, face] = part.astype(BF16)
        rows.append(jnp.sum(spread_weight[slot, face] * part, axis=0, keepdims=True))
    faces = len(values)
    coarse_in[pl.ds(pl.multiple_of(slot * faces, 8), faces)] = jnp.concatenate(rows, axis=0)


def spread_restricted(coarse_map_t, coarse_in, restricted):
    part = jnp.dot(coarse_map_t[...], coarse_in[...], precision=precise, preferred_element_type=F32)
    restricted[...] = jnp.broadcast_to(part[None], restricted.shape)


def first_scale_kernel(partner, size, count, local, deluxe, spread_weight, coarse_map_t, g0, g1, g2, g3, residual, scaled, coarse_in, restricted):
    got = (g0, g1, g2, g3)
    slots, faces = local.shape[:2]

    def one_slot(slot, carry):
        values = []
        for face in range(faces):
            other = partner[slot, face]
            theirs = from_face(local, got, jnp.maximum(other, 0), face)
            value = local[slot, face] + jnp.where(other >= 0, theirs, 0.0)
            residual[slot, face] = value
            values.append(value)
        scale_slot(slot, values, (count, size), deluxe, spread_weight, scaled, coarse_in)
        return carry

    lax.fori_loop(0, slots, one_slot, 0)
    spread_restricted(coarse_map_t, coarse_in, restricted)


def next_scale_kernel(partner, size, count, old_residual, image, sums, deluxe, spread_weight, coarse_map_t, g0, g1, g2, g3, residual, full_image, scaled, coarse_in, restricted):
    got = (g0, g1, g2, g3)
    slots, faces = image.shape[:2]
    totals = total_rows(sums)
    step = totals[0:1] / totals[1:2]

    def one_slot(slot, carry):
        values = []
        for face in range(faces):
            other = partner[slot, face]
            theirs = from_face(image, got, jnp.maximum(other, 0), face).astype(F32)
            full = image[slot, face] + jnp.where(other >= 0, theirs, 0.0)
            full_image[slot, face] = full
            value = old_residual[slot, face] - step * full
            residual[slot, face] = value
            values.append(value)
        scale_slot(slot, values, (count, size), deluxe, spread_weight, scaled, coarse_in)
        return carry

    lax.fori_loop(0, slots, one_slot, 0)
    spread_restricted(coarse_map_t, coarse_in, restricted)


def inverse_kernel(scaled, face_inverse, local_part):
    slots, faces = scaled.shape[:2]

    def one_slot(slot, carry):
        for face in range(faces):
            local_part[slot, face] = jnp.dot(
                face_inverse[slot, face], scaled[slot, face], preferred_element_type=F32
            )
        return carry

    lax.fori_loop(0, slots, one_slot, 0)


def coarse_kernel_body(coarse_rows, restricted, coarse_group, coarse_map, coarse_top, group_vec):
    narrow = len(coarse_rows)
    each, columns = coarse_rows[0].shape
    here = lax.axis_index("narrow")
    for back, rows in enumerate(coarse_rows):
        place = (here + narrow - back) % narrow
        group_vec[pl.ds(pl.multiple_of(place * each, 8), each)] = rows[...]
    gathered = restricted[...]
    everyone = jnp.sum(
        gathered.reshape(gathered.shape[0] // narrow, narrow, gathered.shape[1], columns), axis=1
    ).reshape(-1, columns)
    top = jnp.dot(coarse_top[...], everyone, precision=precise, preferred_element_type=F32)
    group_part = jnp.dot(
        coarse_group[...], group_vec[...], precision=precise, preferred_element_type=F32
    )
    return group_part + jnp.dot(
        coarse_map[...], top, precision=precise, preferred_element_type=F32
    )


def make_weight_kernel(narrow):
    def weight_kernel(size, count, *refs):
        coarse_rows = refs[:narrow]
        restricted, coarse_group, coarse_map, coarse_top, local_part, spread_weight, deluxe = refs[
            narrow : narrow + 7
        ]
        weighted, s0, s1, s2, s3, group_vec, coarse_out = refs[narrow + 7 :]
        slots, faces = weighted.shape[:2]
        coarse_out[...] = coarse_kernel_body(
            coarse_rows, restricted, coarse_group, coarse_map, coarse_top, group_vec
        )

        def one_slot(slot, carry):
            sent = []
            for face in range(faces):
                row = coarse_out[pl.ds(slot * faces + face, 1)]
                value = local_part[slot, face] + spread_weight[slot, face] * row
                live = live_rows(count, size, slot, face, value.shape)
                value = jnp.where(live, value, 0.0).astype(BF16)
                value = jnp.dot(deluxe[slot, face], value, preferred_element_type=F32)
                value = jnp.where(live, value, 0.0)
                weighted[slot, face] = value
                if face < 4:
                    sent.append(value)
            send_faces((s0, s1, s2, s3), slot, sent)
            return carry

        lax.fori_loop(0, slots, one_slot, 0)

    return weight_kernel


def make_operator_kernel(later):
    def operator_kernel(partner, size, count, weighted, residual, schur, g0, g1, g2, g3, *refs):
        if later:
            old_direction, old_image = refs[:2]
            refs = refs[2:]
        direction, image, sums, s0, s1, s2, s3, vec = refs
        got = (g0, g1, g2, g3)
        slots, faces, width, columns = weighted.shape

        def one_slot(slot, carry):
            norm, curve, cross = carry
            for face in range(faces):
                other = partner[slot, face]
                mine = weighted[slot, face]
                theirs = from_face(weighted, got, jnp.maximum(other, 0), face)
                value = mine + jnp.where(other >= 0, theirs, 0.0)
                direction[slot, face] = value
                vec[face * width : (face + 1) * width] = value.astype(BF16)
                norm = norm + fold(residual[slot, face] * mine)
            products = multiply(schur, vec, slot, width)
            sent = []
            for face in range(faces):
                live = live_rows(count, size, slot, face, products[face].shape)
                value = jnp.where(live, products[face], 0.0)
                image[slot, face] = value
                curve = curve + fold(direction[slot, face] * value)
                if later:
                    cross = cross + fold(
                        direction[slot, face] * old_image[slot, face]
                        + old_direction[slot, face] * value
                    )
                if face < 4:
                    sent.append(value)
            send_faces((s0, s1, s2, s3), slot, sent)
            return norm, curve, cross

        zero = jnp.zeros((8, columns), F32)
        found = lax.fori_loop(0, slots, one_slot, (zero, zero, zero))
        rows = [jnp.sum(one, axis=0, keepdims=True) for one in found]
        rows.append(jnp.zeros((5, columns), F32))
        sums[...] = jnp.broadcast_to(jnp.concatenate(rows, axis=0)[None], sums.shape)

    return operator_kernel


def finish_kernel(partner, averaged, direction, precond, residual, full_image, image, first_sums, later_sums, g0, g1, g2, g3, solution_out, residual_out):
    got = (g0, g1, g2, g3)
    slots, faces = image.shape[:2]
    first = total_rows(first_sums)
    later = total_rows(later_sums)
    first_step = first[0:1] / first[1:2]
    ratio = later[0:1] / first[0:1]
    curve = later[1:2] + ratio * (later[2:3] + ratio * first[1:2])
    step = later[0:1] / curve
    old_step = first_step + step * ratio

    def one_slot(slot, carry):
        for face in range(faces):
            other = partner[slot, face]
            theirs = from_face(image, got, jnp.maximum(other, 0), face).astype(F32)
            full = image[slot, face] + jnp.where(other >= 0, theirs, 0.0)
            full = full + ratio * full_image[slot, face]
            residual_out[slot, face] = residual[slot, face] - step * full
            solution_out[slot, face] = (
                averaged[slot, face]
                + old_step * direction[slot, face]
                + step * precond[slot, face]
            )
        return carry

    lax.fori_loop(0, slots, one_slot, 0)


def body(
    schur_matrix,
    face_inverse,
    deluxe,
    primal_weight,
    coarse_group,
    coarse_map,
    coarse_top,
    load_vector,
    previous,
    slot_count,
    partner,
    face_size,
):
    schur_matrix = schur_matrix[0, 0]
    face_inverse = face_inverse[0, 0]
    deluxe = deluxe[0, 0]
    coarse_group = coarse_group[0]
    coarse_map = coarse_map[0]
    load_vector = load_vector[0, 0]
    previous = previous[0, 0]
    partner = partner[0, 0]
    face_size = face_size[0, 0]
    shape = load_vector.shape
    slots, faces, width, columns = shape
    order = schur_matrix.shape[1]
    quotient = coarse_map.shape[1]
    wide = lax.axis_size("wide")
    narrow = lax.axis_size("narrow")
    devices = wide * narrow
    one_face = (slots, width, columns)

    narrow_near = [(i, i ^ 1) for i in range(narrow)]
    narrow_far = [(i, i + 1 if i % 2 else i - 1) for i in range(1, narrow - 1)]
    wide_near = [(i, i ^ 1) for i in range(wide)]
    wide_far = [(i, (i + 1 if i % 2 else i - 1) % wide) for i in range(wide)]

    def swap(sends):
        return (
            lax.ppermute(sends[0], "narrow", narrow_near),
            lax.ppermute(sends[1], "narrow", narrow_far),
            lax.ppermute(sends[2], "wide", wide_near),
            lax.ppermute(sends[3], "wide", wide_far),
        )

    def from_all(spread):
        return lax.all_to_all(spread, AXES, 0, 0, tiled=False)

    def of_group(rows):
        got = [rows]
        for back in range(1, narrow):
            ring = [(i, (i + back) % narrow) for i in range(narrow)]
            got.append(lax.ppermute(rows, "narrow", ring))
        return got

    odd_n = odd("narrow")
    odd_w = odd("wide")
    got = swap(
        (
            jnp.where(odd_n, previous[:, 0], previous[:, 1]),
            jnp.where(odd_n, previous[:, 1], previous[:, 0]),
            jnp.where(odd_w, previous[:, 2], previous[:, 3]),
            jnp.where(odd_w, previous[:, 3], previous[:, 2]),
        )
    )
    spread_weight = jnp.broadcast_to(primal_weight[0, 0][..., None], shape)
    coarse_map_t = coarse_map.T
    ids = (partner, face_size, slot_count)
    vec = pltpu.VMEM((order, columns), BF16)
    sends_f32 = [(one_face, F32)] * 4
    averaged, local, *sends = call(
        start_kernel,
        "start",
        ids,
        (previous, load_vector, schur_matrix) + got,
        [(shape, F32), (shape, F32)] + sends_f32,
        [vec],
    )
    scale_outs = [
        (shape, BF16),
        ((slots * faces, columns), F32),
        ((devices, quotient, columns), F32),
    ]

    def weigh(scaled, coarse_in, restricted):
        restricted = from_all(restricted)
        coarse_rows = of_group(coarse_in)
        (local_part,) = call(
            inverse_kernel, "inverse", (), (scaled, face_inverse), [(shape, F32)]
        )
        weighted, *sends = call(
            make_weight_kernel(narrow),
            "weight",
            (face_size, slot_count),
            (
                *coarse_rows,
                restricted,
                coarse_group,
                coarse_map,
                coarse_top,
                local_part,
                spread_weight,
                deluxe,
            ),
            [(shape, F32)] + sends_f32,
            [
                pltpu.VMEM((narrow * slots * faces, columns), F32),
                pltpu.VMEM((slots * faces, columns), F32),
            ],
        )
        return weighted, swap(sends)

    sum_out = ((devices, 8, columns), F32)
    residual, scaled, coarse_in, restricted = call(
        first_scale_kernel,
        "first_scale",
        ids,
        (local, deluxe, spread_weight, coarse_map_t) + swap(sends),
        [(shape, F32)] + scale_outs,
    )
    weighted, got = weigh(scaled, coarse_in, restricted)
    direction, image, first_sums, *sends = call(
        make_operator_kernel(False),
        "first_operator",
        ids,
        (weighted, residual, schur_matrix) + got,
        [(shape, F32), (shape, F32), sum_out] + sends_f32,
        [vec],
    )
    first_sums = from_all(first_sums)
    residual, full_image, scaled, coarse_in, restricted = call(
        next_scale_kernel,
        "next_scale",
        ids,
        (residual, image, first_sums, deluxe, spread_weight, coarse_map_t) + swap(sends),
        [(shape, F32), (shape, F32)] + scale_outs,
    )
    weighted, got = weigh(scaled, coarse_in, restricted)
    precond, later_image, later_sums, *sends = call(
        make_operator_kernel(True),
        "later_operator",
        ids,
        (weighted, residual, schur_matrix) + got + (direction, image),
        [(shape, F32), (shape, F32), sum_out] + [(one_face, BF16)] * 4,
        [vec],
    )
    later_sums = from_all(later_sums)
    solution, residual = call(
        finish_kernel,
        "finish",
        (partner,),
        (averaged, direction, precond, residual, full_image, later_image, first_sums, later_sums)
        + swap(sends),
        [(shape, F32), (shape, F32)],
    )
    return (solution[None, None], residual[None, None])


def solution(mesh):
    in_specs = (
        P("wide", "narrow", None, None, None),
        P("wide", "narrow", None, None, None, None),
        P("wide", "narrow", None, None, None, None),
        P("wide", "narrow", None, None, None),
        P("wide", "narrow", None),
        P("wide", "narrow", None),
        P("wide", None),
        P("wide", "narrow", None, None, None, None),
        P("wide", "narrow", None, None, None, None),
        P("wide", "narrow"),
        P("wide", "narrow", None, None),
        P("wide", "narrow", None, None),
    )
    out_specs = (
        P("wide", "narrow", None, None, None, None),
        P("wide", "narrow", None, None, None, None),
    )
    return jax.shard_map(body, mesh=mesh, in_specs=in_specs, out_specs=out_specs, check_vma=False)
```

time: 336 us -> 169 us (0.50)
  blocking collectives: 186 us -> 0 us
  matrix products: 24.9 us -> 0 us
  starting transfers between devices: 37.2 us -> 61.6 us
  Pallas kernels: 0 us -> 24.1 us
  other arithmetic: 19.7 us -> 0.03 us
  local copies, waits for them, and re-layouts: 38.2 us -> 52 us
    psum x5 -> x0, blocking collectives: 142 us -> none  [the longest x3 119 us: global_inner(): lax.psum(jnp.sum(weights * first_vec * second_vec, axis=(0, 1, 2)), ('wid...]
    all_gather x4 -> x0, blocking collectives: 44.1 us -> none  [the longest x2 26.2 us: precondition(): group_vec = lax.all_gather(coarse_in, 'narrow', axis=0, tiled=True)]
    unnamed x141 -> x131, local copies, waits for them, and re-layouts: 23 us -> 51.6 us
    dot_general x15 -> x0, matrix products: 24.9 us -> none  [the longest x3 13.5 us: operator(): jnp.einsum('sij,sjr->sir', schur_matrix, stacked, preferred_element_type=...]
    pallas_call x0 -> x10, Pallas kernels: none -> 24.1 us  [call(): pl.pallas_call(kernel, name=name, in_specs=[SMEM] * len(scalars) + [VMEM]...]
    all_to_all x0 -> x4, starting transfers between devices: none -> 21 us  [from_all(): return lax.all_to_all(spread, AXES, 0, 0, tiled=False)]
    reduce_sum x8 -> x0, other arithmetic: 8.15 us -> none  [the longest x2 5.06 us: global_inner(): jnp.sum(weights * first_vec * second_vec, axis=(0, 1, 2))]
    another operation x12 -> x0, local copies, waits for them, and re-layouts: 5.54 us -> none  [the longest x5 4.31 us: partner_full(): jnp.stack([values[:, 2], values[:, 3]], axis=0)]
  transfers between devices with their start and end apart: 24 -> 34, of which waited for: 8 -> 14; matrix products, arithmetic and copies ran while one was open for 5% -> 0% of each run, Pallas kernels for 0% -> 1%
where the time goes in v1:
time: 169 us; the launch traced here: 167 us
  starting transfers between devices  61.6 us (36%)
  local copies, waits for them, and re-layouts  52 us (31%)
  waiting for transfers between devices  27.2 us (16%)
  Pallas kernels  24.1 us (14%)
  between operations  1.77 us (1%)
    unnamed x131, local copies, waits for them, and re-layouts  51.6 us
    pallas_call x10, Pallas kernels, call(): pl.pallas_call(kernel, name=name, in_specs=[SMEM] * len(scalars) + [VMEM]...  24.1 us
    all_to_all x4, starting transfers between devices, from_all(): return lax.all_to_all(spread, AXES, 0, 0, tiled=False)  21 us
    ppermute x6, starting transfers between devices, swap(): lax.ppermute(sends[3], 'wide', wide_far)  14.7 us
    ppermute x6, waiting for transfers between devices, swap(): lax.ppermute(sends[0], 'narrow', narrow_near)  12.6 us
    ppermute x6, starting transfers between devices, swap(): lax.ppermute(sends[0], 'narrow', narrow_near)  12 us
    ppermute x6, waiting for transfers between devices, swap(): lax.ppermute(sends[3], 'wide', wide_far)  11.7 us
    ppermute x6, starting transfers between devices, of_group(): got.append(lax.ppermute(rows, 'narrow', ring))  9.5 us
  transfers between devices with their start and end apart: 34, of which 14 were waited for; matrix products, arithmetic and copies ran while one was open for 0% of the time, Pallas kernels for 1%

profile of v1, /device:TPU:0, one launch (start us, length us, event | category | flops | bytes accessed | tf_op | source)
XLA Modules:
  0.0 166.8 jit_solution(3655828426115353990)
XLA Ops:
  0.7 1.3 copy.26
  2.0 3.4 %collective-permute-start.3 = (bf16[3,128,128]{2,1,0:T(8,128)(2,1)S(1)}, bf16[3,128,128]{2,1,0:T(8,128)(2,1)S(1)}, u32[]{:S(2)}, u32[]{:S(2)}) collective-permute-start(bf16[3,128,128]{2,1,0:T(8,128)(2,1)S(1)} %get-tuple-element.84), channel_id=1, source_target_pairs={{0,28},{4,8},{8,4},{12,16},{16,12},{20,24},{24,20},{28,0},{1,29},{... | collective-permute-start | bytes 294920 | tf_op jit(solution)/shard_map/ppermute | solution.py:351
  5.5 1.6 collective-permute-start
  8.5 1.6 collective-permute-done.g0
  10.1 2.8 %copy-done = bf16[1,1,3,1024,1024]{4,3,2,1,0:T(8,128)(2,1)S(1)} copy-done((bf16[1,1,3,1024,1024]{4,3,2,1,0:T(8,128)(2,1)S(1)}, bf16[1,1,3,1024,1024]{4,3,2,1,0:T(8,128)(2,1)}, u32[]{:S(2)}) %copy-start) | copy-done | bytes 6291480
  12.9 3.2 %start.1 = (f32[3,8,128,128]{3,2,1,0:T(8,128)S(1)}, f32[3,8,128,128]{3,2,1,0:T(8,128)S(1)}, f32[3,128,128]{2,1,0:T(8,128)S(1)}, f32[3,128,128]{2,1,0:T(8,128)S(1...) custom-call(s32[3,8]{1,0:T(4,128)S(1)} %get-tuple-element.89.partner, s32[3,8]{1,0:T(4,128)S(1)} %get-tuple-element.88.size, ...), custom_call_target="tpu_custom_call" | custom-call | tf_op jit(solution)/shard_map/start/pallas_call | solution.py:17
  16.1 4.7 %collective-permute-start.4 = (f32[3,128,128]{2,1,0:T(8,128)S(1)}, f32[3,128,128]{2,1,0:T(8,128)S(1)}, u32[]{:S(2)}, u32[]{:S(2)}) collective-permute-start(f32[3,128,128]{2,1,0:T(8,128)S(1)} %get-tuple-element.45), channel_id=1, source_target_pairs={{0,1},{1,0},{2,3},{3,2},{4,5},{5,4},{6,7},{7,6},{8,9},{9,8},{10,11... | collective-permute-start | bytes 589832 | tf_op jit(solution)/shard_map/ppermute | solution.py:348
  21.5 1.3 collective-permute-start.7
  22.8 1.9 %collective-permute-done.4.g0 = f32[3,128,128]{2,1,0:T(8,128)S(1)} collective-permute-done((f32[3,128,128]{2,1,0:T(8,128)S(1)}, f32[3,128,128]{2,1,0:T(8,128)S(1)}, u32[]{:S(2)}, u32[]{:S(2)}) %collective-permute-start.4) | collective-permute-done | bytes 196640 | tf_op jit(solution)/shard_map/ppermute | solution.py:348
  24.8 4.4 %collective-permute-done.7.g3 = f32[3,128,128]{2,1,0:T(8,128)S(1)} collective-permute-done((f32[3,128,128]{2,1,0:T(8,128)S(1)}, f32[3,128,128]{2,1,0:T(8,128)S(1)}, u32[]{:S(2)}, u32[]{:S(2)}) %collective-permute-start.7) | collective-permute-done | bytes 196640 | tf_op jit(solution)/shard_map/ppermute | solution.py:351
  29.7 2.3 %first_scale.1 = (f32[3,8,128,128]{3,2,1,0:T(8,128)S(1)}, bf16[3,8,128,128]{3,2,1,0:T(8,128)(2,1)S(1)}, f32[24,128]{1,0:T(8,128)S(1)}, f32[32,8,128]{2,1,0:T(8,128)}) custom-call(s32[3,8]{1,0:T(4,128)S(1)} %get-tuple-element.89.partner, s32[3,8]{1,0:T(4,128)S(1)} %get-tuple-element.88.size, s32[1,1]{1,0:T(1,128)S(6)} %copy.27.count, ...), custom_call_target="tpu_custom_call" | custom-call | tf_op jit(solution)/shard_map/first_scale/pallas_call | solution.py:17
  32.0 1.1 copy-done.6
  34.0 4.6 %all-to-all-start = ((f32[32,8,128]{2,1,0:T(8,128)}), f32[32,8,128]{2,1,0:T(8,128)S(1)}, u32[]{:S(2)}, u32[]{:S(2)}) async-start(f32[32,8,128]{2,1,0:T(8,128)} %get-tuple-element.50), calls=%async_computation | async-start | bytes 262144 | tf_op jit(solution)/shard_map/all_to_all | solution.py:355
  38.6 3.7 %collective-permute-start.10 = (f32[24,128]{1,0:T(8,128)S(1)}, f32[24,128]{1,0:T(8,128)S(1)}, u32[]{:S(2)}, u32[]{:S(2)}) collective-permute-start(f32[24,128]{1,0:T(8,128)S(1)} %get-tuple-element.49.refs_0_), channel_id=1, source_target_pairs={{0,3},{1,0},{2,1},{3,2},{4,7},{5,4},{6,5},{7,6},{8,11},{9,8},{10,9... | collective-permute-start | bytes 36872 | tf_op jit(solution)/shard_map/ppermute | solution.py:361
  42.3 1.1 collective-permute-start.8
  43.4 1.1 copy-done.30
  45.2 1.1 copy-done.11
  47.8 1.4 copy-done.12
  49.2 1.7 %weight.2 = (f32[3,8,128,128]{3,2,1,0:T(8,128)S(1)}, f32[3,128,128]{2,1,0:T(8,128)S(1)}, f32[3,128,128]{2,1,0:T(8,128)S(1)}, f32[3,128,128]{2,1,0:T(8,128)S(1)}, f32[3,128,128]{2,1,0:T(8,128)S(1)}) custom-call(s32[3,8]{1,0:T(4,128)S(1)} %get-tuple-element.88.size, s32[1,1]{1,0:T(1,128)S(6)} %copy.27.count, f32[24,128]{1,0:T(8,128)S(1)} %get-tuple-element.49.refs_0_, ...), custom_call_target="tpu_custom_call" | custom-call | tf_op jit(solution)/shard_map/weight/pallas_call | solution.py:17
  50.9 1.1 collective-permute-start.11
  52.8 2.5 %collective-permute-start.14 = (f32[3,128,128]{2,1,0:T(8,128)S(1)}, f32[3,128,128]{2,1,0:T(8,128)S(1)}, u32[]{:S(2)}, u32[]{:S(2)}) collective-permute-start(f32[3,128,128]{2,1,0:T(8,128)S(1)} %get-tuple-element.57), channel_id=1, source_target_pairs={{0,28},{4,8},{8,4},{12,16},{16,12},{20,24},{24,20},{28,0},{1,29},{... | collective-permute-start | bytes 589832 | tf_op jit(solution)/shard_map/ppermute | solution.py:351
  55.3 1.5 collective-permute-done.11.g0
  56.8 3.5 %collective-permute-done.14.g3 = f32[3,128,128]{2,1,0:T(8,128)S(1)} collective-permute-done((f32[3,128,128]{2,1,0:T(8,128)S(1)}, f32[3,128,128]{2,1,0:T(8,128)S(1)}, u32[]{:S(2)}, u32[]{:S(2)}) %collective-permute-start.14) | collective-permute-done | bytes 196640 | tf_op jit(solution)/shard_map/ppermute | solution.py:351
  60.3 2.8 %copy-done.1 = bf16[1,1,3,1024,1024]{4,3,2,1,0:T(8,128)(2,1)S(1)} copy-done((bf16[1,1,3,1024,1024]{4,3,2,1,0:T(8,128)(2,1)S(1)}, bf16[1,1,3,1024,1024]{4,3,2,1,0:T(8,128)(2,1)}, u32[]{:S(2)}) %copy-start.1) | copy-done | bytes 6291480
  63.1 3.7 %first_operator.1 = (f32[3,8,128,128]{3,2,1,0:T(8,128)S(1)}, f32[3,8,128,128]{3,2,1,0:T(8,128)S(1)}, f32[32,8,128]{2,1,0:T(8,128)}, f32[3,128,128]{2,1,0:T(8,128...) custom-call(s32[3,8]{1,0:T(4,128)S(1)} %get-tuple-element.89.partner, ...), custom_call_target="tpu_custom_call" | custom-call | tf_op jit(solution)/shard_map/first_operator/pallas_call | solution.py:17
  66.8 1.1 copy-done.3
  67.9 1.1 copy-done.13
  71.8 5.3 %all-to-all-start.1 = ((f32[32,8,128]{2,1,0:T(8,128)}), f32[32,8,128]{2,1,0:T(8,128)S(1)}, u32[]{:S(2)}, u32[]{:S(2)}) async-start(f32[32,8,128]{2,1,0:T(8,128)} %get-tuple-element.60), calls=%async_computation.1 | async-start | bytes 262144 | tf_op jit(solution)/shard_map/all_to_all | solution.py:355
  77.1 1.8 %collective-permute-start.15 = (f32[3,128,128]{2,1,0:T(8,128)}, f32[3,128,128]{2,1,0:T(8,128)S(1)}, u32[]{:S(2)}, u32[]{:S(2)}) collective-permute-start(f32[3,128,128]{2,1,0:T(8,128)} %copy-done.56), channel_id=1, source_target_pairs={{0,1},{1,0},{2,3},{3,2},{4,5},{5,4},{6,7},{7,6},{8,9},{9,8},{10,11... | collective-permute-start | bytes 589832 | tf_op jit(solution)/shard_map/ppermute | solution.py:348
  79.7 2.5 %collective-permute-start.18 = (f32[3,128,128]{2,1,0:T(8,128)}, f32[3,128,128]{2,1,0:T(8,128)S(1)}, u32[]{:S(2)}, u32[]{:S(2)}) collective-permute-start(f32[3,128,128]{2,1,0:T(8,128)} %copy-done.53), channel_id=1, source_target_pairs={{0,28},{4,8},{8,4},{12,16},{16,12},{20,24},{24,20},{28,0},{1,29},{... | collective-permute-start | bytes 589832 | tf_op jit(solution)/shard_map/ppermute | solution.py:351
  82.2 4.1 %collective-permute-done.15.g0 = f32[3,128,128]{2,1,0:T(8,128)S(1)} collective-permute-done((f32[3,128,128]{2,1,0:T(8,128)}, f32[3,128,128]{2,1,0:T(8,128)S(1)}, u32[]{:S(2)}, u32[]{:S(2)}) %collective-permute-start.15) | collective-permute-done | bytes 196640 | tf_op jit(solution)/shard_map/ppermute | solution.py:348
  88.7 1.4 copy-done.4
  90.1 1.4 copy-done.8
  91.5 0.9 copy-done.35
  92.4 0.9 copy-done.37
  93.4 0.9 copy-done.39
  94.3 1.7 %next_scale.1 = (f32[3,8,128,128]{3,2,1,0:T(8,128)S(1)}, f32[3,8,128,128]{3,2,1,0:T(8,128)S(1)}, bf16[3,8,128,128]{3,2,1,0:T(8,128)(2,1)S(1)}, f32[24,128]{1,0:T(8,128)S(1)}, f32[32,8,128]{2,1,0:T(8,128)S(1)}) custom-call(s32[3,8]{1,0:T(4,128)S(1)} %get-tuple-element.89.partner, s32[3,8]{1,0:T(4,128)S(1)} %get-tuple-element.88.size, s32[1,1]{1,0:T(1,128)S(6)} %copy.27.count, ...), custom_call_target="tpu_custom_call" | custom-call | tf_op jit(solution)/shard_map/next_scale/pallas_call | solution.py:17
  96.0 1.1 copy-done.16
  97.1 1.2 copy-done.23
  98.3 0.9 copy-done.31
  99.9 5.7 %all-to-all-start.2 = ((f32[32,8,128]{2,1,0:T(8,128)}), f32[32,8,128]{2,1,0:T(8,128)S(1)}, u32[]{:S(2)}, u32[]{:S(2)}) async-start(f32[32,8,128]{2,1,0:T(8,128)} %copy-done.41), calls=%async_computation.2 | async-start | bytes 262144 | tf_op jit(solution)/shard_map/all_to_all | solution.py:355
  105.6 3.7 %collective-permute-start.21 = (f32[24,128]{1,0:T(8,128)S(1)}, f32[24,128]{1,0:T(8,128)S(1)}, u32[]{:S(2)}, u32[]{:S(2)}) collective-permute-start(f32[24,128]{1,0:T(8,128)S(1)} %get-tuple-element.65.refs_0_), channel_id=1, source_target_pairs={{0,3},{1,0},{2,1},{3,2},{4,7},{5,4},{6,5},{7,6},{8,11},{9,8},{10,9... | collective-permute-start | bytes 36872 | tf_op jit(solution)/shard_map/ppermute | solution.py:361
  109.2 1.1 collective-permute-start.19
  110.3 1.1 copy-done.32
  112.1 1.1 copy-done.9
  114.7 1.4 copy-done.10
  116.1 1.8 %weight.3 = (f32[3,8,128,128]{3,2,1,0:T(8,128)S(1)}, f32[3,128,128]{2,1,0:T(8,128)S(1)}, f32[3,128,128]{2,1,0:T(8,128)S(1)}, f32[3,128,128]{2,1,0:T(8,128)S(1)}, f32[3,128,128]{2,1,0:T(8,128)S(1)}) custom-call(s32[3,8]{1,0:T(4,128)S(1)} %get-tuple-element.88.size, s32[1,1]{1,0:T(1,128)S(6)} %copy.27.count, f32[24,128]{1,0:T(8,128)S(1)} %get-tuple-element.65.refs_0_, ...), custom_call_target="tpu_custom_call" | custom-call | tf_op jit(solution)/shard_map/weight/pallas_call | solution.py:17
  117.9 1.0 collective-permute-start.22
  119.7 2.5 %collective-permute-start.25 = (f32[3,128,128]{2,1,0:T(8,128)S(1)}, f32[3,128,128]{2,1,0:T(8,128)S(1)}, u32[]{:S(2)}, u32[]{:S(2)}) collective-permute-start(f32[3,128,128]{2,1,0:T(8,128)S(1)} %get-tuple-element.73), channel_id=1, source_target_pairs={{0,28},{4,8},{8,4},{12,16},{16,12},{20,24},{24,20},{28,0},{1,29},{... | collective-permute-start | bytes 589832 | tf_op jit(solution)/shard_map/ppermute | solution.py:351
  122.2 1.6 collective-permute-done.22.g0
  123.8 3.4 %collective-permute-done.25.g3 = f32[3,128,128]{2,1,0:T(8,128)S(1)} collective-permute-done((f32[3,128,128]{2,1,0:T(8,128)S(1)}, f32[3,128,128]{2,1,0:T(8,128)S(1)}, u32[]{:S(2)}, u32[]{:S(2)}) %collective-permute-start.25) | collective-permute-done | bytes 196640 | tf_op jit(solution)/shard_map/ppermute | solution.py:351
  127.2 1.4 copy-done.17
  128.6 5.4 %later_operator.1 = (f32[3,8,128,128]{3,2,1,0:T(8,128)S(1)}, f32[3,8,128,128]{3,2,1,0:T(8,128)S(1)}, f32[32,8,128]{2,1,0:T(8,128)S(1)}, bf16[3,128,128]{2,1,0:T(...) custom-call(s32[3,8]{1,0:T(4,128)S(1)} %get-tuple-element.89.partner, ...), custom_call_target="tpu_custom_call" | custom-call | tf_op jit(solution)/shard_map/later_operator/pallas_call | solution.py:17
  134.0 1.1 copy-done.25
  135.1 1.1 copy-done.27
  139.5 5.4 %all-to-all-start.3 = ((f32[32,8,128]{2,1,0:T(8,128)}), f32[32,8,128]{2,1,0:T(8,128)S(1)}, u32[]{:S(2)}, u32[]{:S(2)}) async-start(f32[32,8,128]{2,1,0:T(8,128)} %copy-done.40), calls=%async_computation.3 | async-start | bytes 262144 | tf_op jit(solution)/shard_map/all_to_all | solution.py:355
  144.9 1.8 %collective-permute-start.26 = (bf16[3,128,128]{2,1,0:T(8,128)(2,1)}, bf16[3,128,128]{2,1,0:T(8,128)(2,1)S(1)}, u32[]{:S(2)}, u32[]{:S(2)}) collective-permute-start(bf16[3,128,128]{2,1,0:T(8,128)(2,1)} %copy-done.60), channel_id=1, source_target_pairs={{0,1},{1,0},{2,3},{3,2},{4,5},{5,4},{6,7},{7,6},{8,9},{9,8},{10,11... | collective-permute-start | bytes 294920 | tf_op jit(solution)/shard_map/ppermute | solution.py:348
  147.5 2.5 %collective-permute-start.29 = (bf16[3,128,128]{2,1,0:T(8,128)(2,1)}, bf16[3,128,128]{2,1,0:T(8,128)(2,1)S(1)}, u32[]{:S(2)}, u32[]{:S(2)}) collective-permute-start(bf16[3,128,128]{2,1,0:T(8,128)(2,1)} %copy-done.57), channel_id=1, source_target_pairs={{0,28},{4,8},{8,4},{12,16},{16,12},{20,24},{24,20},{28,0},{1,29},{... | collective-permute-start | bytes 294920 | tf_op jit(solution)/shard_map/ppermute | solution.py:351
  150.0 1.9 %collective-permute-done.26.g0 = bf16[3,128,128]{2,1,0:T(8,128)(2,1)S(1)} collective-permute-done((bf16[3,128,128]{2,1,0:T(8,128)(2,1)}, bf16[3,128,128]{2,1,0:T(8,128)(2,1)S(1)}, u32[]{:S(2)}, u32[]{:S(2)}) %collective-permute-start.26) | collective-permute-done | bytes 98336 | tf_op jit(solution)/shard_map/ppermute | solution.py:348
  154.5 1.4 copy-done.22
  155.9 1.4 copy-done.24
  157.3 1.4 copy-done.26
  158.7 1.4 copy-done.28
  163.7 3.1 %finish.1 = (f32[3,8,128,128]{3,2,1,0:T(8,128)}, f32[3,8,128,128]{3,2,1,0:T(8,128)}) custom-call(s32[3,8]{1,0:T(4,128)S(1)} %get-tuple-element.89.partner, f32[3,8,128,128]{3,2,1,0:T(8,128)S(1)} %copy-done.22, f32[3,8,128,128]{3,2,1,0:T(8,128)S(1)} %copy-done.15, f32[3,8,128,128]{3,2,1,0:T(8,128)S(1)} %copy-done.26, f32[3,8,128,128]{3,2,1,0:T(8,128)S(1)} %copy-done.18, ...), custom_call_target="tpu_custom_call" | custom-call | tf_op jit(solution)/shard_map/finish/pallas_call | solution.py:17
  (147 shorter events, 25.3 us)
Async XLA Ops:
  0.6 9.5 %copy-start.20 = (bf16[1,1,3,8,128,128]{5,4,3,2,1,0:T(8,128)(2,1)S(1)}, bf16[1,1,3,8,128,128]{5,4,3,2,1,0:T(8,128)(2,1)}, u32[]{:S(2)}) copy-start(bf16[1,1,3,8,128,128]{5,4,3,2,1,0:T(8,128)(2,1)} %param.20) | copy-start | bytes 2359300
  0.6 7.2 %copy-start.62 = (s32[1,1,3,8]{3,1,2,0:T(1,128)S(1)}, s32[1,1,3,8]{3,1,2,0:T(1,128)}, u32[]{:S(2)}) copy-start(s32[1,1,3,8]{3,1,2,0:T(1,128)} %param.23) | copy-start | bytes 292
  0.7 7.2 %copy-start.63 = (s32[1,1,3,8]{3,1,2,0:T(1,128)S(1)}, s32[1,1,3,8]{3,1,2,0:T(1,128)}, u32[]{:S(2)}) copy-start(s32[1,1,3,8]{3,1,2,0:T(1,128)} %param.22) | copy-start | bytes 292
  0.7 9.4 %copy-start.33 = (bf16[1,1,3,8,128,128]{5,4,3,2,1,0:T(8,128)(2,1)S(1)}, bf16[1,1,3,8,128,128]{5,4,3,2,1,0:T(8,128)(2,1)}, u32[]{:S(2)}) copy-start(bf16[1,1,3,8,128,128]{5,4,3,2,1,0:T(8,128)(2,1)} %param.19) | copy-start | bytes 2359300
  2.0 6.4 %collective-permute-start.3 = (bf16[3,128,128]{2,1,0:T(8,128)(2,1)S(1)}, bf16[3,128,128]{2,1,0:T(8,128)(2,1)S(1)}, u32[]{:S(2)}, u32[]{:S(2)}) collective-permute-start(bf16[3,128,128]{2,1,0:T(8,128)(2,1)S(1)} %get-tuple-element.84), channel_id=1, source_target_pairs={{0,28},{4,8},{8,4},{12,16},{16,12},{20,24},{24,20},{28,0},{1,29},{... | collective-permute-start | bytes 294920 | tf_op jit(solution)/shard_map/ppermute | solution.py:351
  5.5 4.6 %collective-permute-start = (bf16[3,128,128]{2,1,0:T(8,128)(2,1)S(1)}, bf16[3,128,128]{2,1,0:T(8,128)(2,1)S(1)}, u32[]{:S(2)}, u32[]{:S(2)}) collective-permute-start(bf16[3,128,128]{2,1,0:T(8,128)(2,1)S(1)} %get-tuple-element.85), channel_id=1, source_target_pairs={{0,1},{1,0},{2,3},{3,2},{4,5},{5,4},{6,7},{7,6},{8,9},{9,8},{10,11... | collective-permute-start | bytes 294920 | tf_op jit(solution)/shard_map/ppermute | solution.py:348
  7.1 3.0 %collective-permute-start.1 = (bf16[3,128,128]{2,1,0:T(8,128)(2,1)S(1)}, bf16[3,128,128]{2,1,0:T(8,128)(2,1)S(1)}, u32[]{:S(2)}, u32[]{:S(2)}) collective-permute-start(bf16[3,128,128]{2,1,0:T(8,128)(2,1)S(1)} %get-tuple-element.86), channel_id=1, source_target_pairs={{1,2},{2,1},{5,6},{6,5},{9,10},{10,9},{13,14},{14,13},{17,18},{18,... | collective-permute-start | bytes 294920 | tf_op jit(solution)/shard_map/ppermute | solution.py:349
  7.7 2.4 %collective-permute-start.2 = (bf16[3,128,128]{2,1,0:T(8,128)(2,1)S(1)}, bf16[3,128,128]{2,1,0:T(8,128)(2,1)S(1)}, u32[]{:S(2)}, u32[]{:S(2)}) collective-permute-start(bf16[3,128,128]{2,1,0:T(8,128)(2,1)S(1)} %get-tuple-element.87), channel_id=1, source_target_pairs={{0,4},{4,0},{8,12},{12,8},{16,20},{20,16},{24,28},{28,24},{1,5},{5... | collective-permute-start | bytes 294920 | tf_op jit(solution)/shard_map/ppermute | solution.py:350
  10.1 2.8 %copy-start = (bf16[1,1,3,1024,1024]{4,3,2,1,0:T(8,128)(2,1)S(1)}, bf16[1,1,3,1024,1024]{4,3,2,1,0:T(8,128)(2,1)}, u32[]{:S(2)}) copy-start(bf16[1,1,3,1024,1024]{4,3,2,1,0:T(8,128)(2,1)} %param.12) | copy-start | bytes 18874372
  12.9 16.3 %copy-start.61 = (f32[1,1,3,8,128]{4,3,2,1,0:T(8,128)S(1)}, f32[1,1,3,8,128]{4,3,2,1,0:T(8,128)}, u32[]{:S(2)}) copy-start(f32[1,1,3,8,128]{4,3,2,1,0:T(8,128)} %param.15) | copy-start | bytes 36868
  16.1 15.9 %copy-start.21 = (f32[3,8,128,128]{3,2,1,0:T(8,128)}, f32[3,8,128,128]{3,2,1,0:T(8,128)S(1)}, u32[]{:S(2)}) copy-start(f32[3,8,128,128]{3,2,1,0:T(8,128)S(1)} %get-tuple-element.43.averaged) | copy-start | bytes 4718596
  16.1 13.6 %copy-start.2 = (bf16[1,1,3,8,128,128]{5,4,3,2,1,0:T(8,128)(2,1)S(1)}, bf16[1,1,3,8,128,128]{5,4,3,2,1,0:T(8,128)(2,1)}, u32[]{:S(2)}) copy-start(bf16[1,1,3,8,128,128]{5,4,3,2,1,0:T(8,128)(2,1)} %param.14) | copy-start | bytes 2359300
  16.1 13.6 %copy-start.51 = (f32[1,24,8]{1,2,0:T(8,128)S(1)}, f32[1,24,8]{1,2,0:T(8,128)}, u32[]{:S(2)}) copy-start(f32[1,24,8]{1,2,0:T(8,128)} %param.17) | copy-start | bytes 2308
  16.1 8.6 %collective-permute-start.4 = (f32[3,128,128]{2,1,0:T(8,128)S(1)}, f32[3,128,128]{2,1,0:T(8,128)S(1)}, u32[]{:S(2)}, u32[]{:S(2)}) collective-permute-start(f32[3,128,128]{2,1,0:T(8,128)S(1)} %get-tuple-element.45), channel_id=1, source_target_pairs={{0,1},{1,0},{2,3},{3,2},{4,5},{5,4},{6,7},{7,6},{8,9},{9,8},{10,11... | collective-permute-start | bytes 589832 | tf_op jit(solution)/shard_map/ppermute | solution.py:348
  20.8 4.0 %collective-permute-start.5 = (f32[3,128,128]{2,1,0:T(8,128)S(1)}, f32[3,128,128]{2,1,0:T(8,128)S(1)}, u32[]{:S(2)}, u32[]{:S(2)}) collective-permute-start(f32[3,128,128]{2,1,0:T(8,128)S(1)} %get-tuple-element.46), channel_id=1, source_target_pairs={{1,2},{2,1},{5,6},{6,5},{9,10},{10,9},{13,14},{14,13},{17,18},{18,... | collective-permute-start | bytes 589832 | tf_op jit(solution)/shard_map/ppermute | solution.py:349
  21.4 3.3 %collective-permute-start.6 = (f32[3,128,128]{2,1,0:T(8,128)S(1)}, f32[3,128,128]{2,1,0:T(8,128)S(1)}, u32[]{:S(2)}, u32[]{:S(2)}) collective-permute-start(f32[3,128,128]{2,1,0:T(8,128)S(1)} %get-tuple-element.47), channel_id=1, source_target_pairs={{0,4},{4,0},{8,12},{12,8},{16,20},{20,16},{24,28},{28,24},{1,5},{5... | collective-permute-start | bytes 589832 | tf_op jit(solution)/shard_map/ppermute | solution.py:350
  21.5 7.7 %collective-permute-start.7 = (f32[3,128,128]{2,1,0:T(8,128)S(1)}, f32[3,128,128]{2,1,0:T(8,128)S(1)}, u32[]{:S(2)}, u32[]{:S(2)}) collective-permute-start(f32[3,128,128]{2,1,0:T(8,128)S(1)} %get-tuple-element.48), channel_id=1, source_target_pairs={{0,28},{4,8},{8,4},{12,16},{16,12},{20,24},{24,20},{28,0},{1,29},{... | collective-permute-start | bytes 589832 | tf_op jit(solution)/shard_map/ppermute | solution.py:351
  29.7 13.8 %copy-start.19 = (bf16[1,1,3,8,128,128]{5,4,3,2,1,0:T(8,128)(2,1)S(1)}, bf16[1,1,3,8,128,128]{5,4,3,2,1,0:T(8,128)(2,1)}, u32[]{:S(2)}) copy-start(bf16[1,1,3,8,128,128]{5,4,3,2,1,0:T(8,128)(2,1)} %param.13) | copy-start | bytes 2359300
  34.0 13.8 %all-to-all-start = ((f32[32,8,128]{2,1,0:T(8,128)}), f32[32,8,128]{2,1,0:T(8,128)S(1)}, u32[]{:S(2)}, u32[]{:S(2)}) async-start(f32[32,8,128]{2,1,0:T(8,128)} %get-tuple-element.50), calls=%async_computation | async-start | bytes 262144 | tf_op jit(solution)/shard_map/all_to_all | solution.py:355
  38.6 7.8 %collective-permute-start.10 = (f32[24,128]{1,0:T(8,128)S(1)}, f32[24,128]{1,0:T(8,128)S(1)}, u32[]{:S(2)}, u32[]{:S(2)}) collective-permute-start(f32[24,128]{1,0:T(8,128)S(1)} %get-tuple-element.49.refs_0_), channel_id=1, source_target_pairs={{0,3},{1,0},{2,1},{3,2},{4,7},{5,4},{6,5},{7,6},{8,11},{9,8},{10,9... | collective-permute-start | bytes 36872 | tf_op jit(solution)/shard_map/ppermute | solution.py:361
  42.3 4.6 %collective-permute-start.9 = (f32[24,128]{1,0:T(8,128)S(1)}, f32[24,128]{1,0:T(8,128)S(1)}, u32[]{:S(2)}, u32[]{:S(2)}) collective-permute-start(f32[24,128]{1,0:T(8,128)S(1)} %get-tuple-element.49.refs_0_), channel_id=1, source_target_pairs={{0,2},{1,3},{2,0},{3,1},{4,6},{5,7},{6,4},{7,5},{8,10},{9,11},{10,... | collective-permute-start | bytes 36872 | tf_op jit(solution)/shard_map/ppermute | solution.py:361
  42.3 5.5 %collective-permute-start.8 = (f32[24,128]{1,0:T(8,128)S(1)}, f32[24,128]{1,0:T(8,128)S(1)}, u32[]{:S(2)}, u32[]{:S(2)}) collective-permute-start(f32[24,128]{1,0:T(8,128)S(1)} %get-tuple-element.49.refs_0_), channel_id=1, source_target_pairs={{0,1},{1,2},{2,3},{3,0},{4,5},{5,6},{6,7},{7,4},{8,9},{9,10},{10,1... | collective-permute-start | bytes 36872 | tf_op jit(solution)/shard_map/ppermute | solution.py:361
  44.6 3.2 %copy-start.50 = (f32[1,24,96]{2,1,0:T(8,128)S(1)}, f32[1,24,96]{2,1,0:T(8,128)}, u32[]{:S(2)}) copy-start(f32[1,24,96]{2,1,0:T(8,128)} %param.16) | copy-start | bytes 27652
  44.6 3.2 %copy-start.52 = (f32[8,64]{1,0:T(8,128)S(1)}, f32[8,64]{1,0:T(8,128)}, u32[]{:S(2)}) copy-start(f32[8,64]{1,0:T(8,128)} %refs_7_.3) | copy-start | bytes 6148
  47.8 1.4 copy-start.12
  49.2 11.1 %copy-start.7 = (f32[3,8,128,128]{3,2,1,0:T(8,128)S(1)}, f32[3,8,128,128]{3,2,1,0:T(8,128)}, u32[]{:S(2)}) copy-start(f32[3,8,128,128]{3,2,1,0:T(8,128)} %copy-done.6) | copy-start | bytes 4718596
  50.9 5.9 %collective-permute-start.11 = (f32[3,128,128]{2,1,0:T(8,128)S(1)}, f32[3,128,128]{2,1,0:T(8,128)S(1)}, u32[]{:S(2)}, u32[]{:S(2)}) collective-permute-start(f32[3,128,128]{2,1,0:T(8,128)S(1)} %get-tuple-element.54), channel_id=1, source_target_pairs={{0,1},{1,0},{2,3},{3,2},{4,5},{5,4},{6,7},{7,6},{8,9},{9,8},{10,11... | collective-permute-start | bytes 589832 | tf_op jit(solution)/shard_map/ppermute | solution.py:348
  52.0 4.8 %collective-permute-start.12 = (f32[3,128,128]{2,1,0:T(8,128)S(1)}, f32[3,128,128]{2,1,0:T(8,128)S(1)}, u32[]{:S(2)}, u32[]{:S(2)}) collective-permute-start(f32[3,128,128]{2,1,0:T(8,128)S(1)} %get-tuple-element.55), channel_id=1, source_target_pairs={{1,2},{2,1},{5,6},{6,5},{9,10},{10,9},{13,14},{14,13},{17,18},{18,... | collective-permute-start | bytes 589832 | tf_op jit(solution)/shard_map/ppermute | solution.py:349
  52.7 4.1 %collective-permute-start.13 = (f32[3,128,128]{2,1,0:T(8,128)S(1)}, f32[3,128,128]{2,1,0:T(8,128)S(1)}, u32[]{:S(2)}, u32[]{:S(2)}) collective-permute-start(f32[3,128,128]{2,1,0:T(8,128)S(1)} %get-tuple-element.56), channel_id=1, source_target_pairs={{0,4},{4,0},{8,12},{12,8},{16,20},{20,16},{24,28},{28,24},{1,5},{5... | collective-permute-start | bytes 589832 | tf_op jit(solution)/shard_map/ppermute | solution.py:350
  52.8 7.5 %collective-permute-start.14 = (f32[3,128,128]{2,1,0:T(8,128)S(1)}, f32[3,128,128]{2,1,0:T(8,128)S(1)}, u32[]{:S(2)}, u32[]{:S(2)}) collective-permute-start(f32[3,128,128]{2,1,0:T(8,128)S(1)} %get-tuple-element.57), channel_id=1, source_target_pairs={{0,28},{4,8},{8,4},{12,16},{16,12},{20,24},{24,20},{28,0},{1,29},{... | collective-permute-start | bytes 589832 | tf_op jit(solution)/shard_map/ppermute | solution.py:351
  60.3 2.8 %copy-start.1 = (bf16[1,1,3,1024,1024]{4,3,2,1,0:T(8,128)(2,1)S(1)}, bf16[1,1,3,1024,1024]{4,3,2,1,0:T(8,128)(2,1)}, u32[]{:S(2)}) copy-start(bf16[1,1,3,1024,1024]{4,3,2,1,0:T(8,128)(2,1)} %param.12) | copy-start | bytes 18874372
  71.8 16.9 %all-to-all-start.1 = ((f32[32,8,128]{2,1,0:T(8,128)}), f32[32,8,128]{2,1,0:T(8,128)S(1)}, u32[]{:S(2)}, u32[]{:S(2)}) async-start(f32[32,8,128]{2,1,0:T(8,128)} %get-tuple-element.60), calls=%async_computation.1 | async-start | bytes 262144 | tf_op jit(solution)/shard_map/all_to_all | solution.py:355
  77.1 9.2 %collective-permute-start.15 = (f32[3,128,128]{2,1,0:T(8,128)}, f32[3,128,128]{2,1,0:T(8,128)S(1)}, u32[]{:S(2)}, u32[]{:S(2)}) collective-permute-start(f32[3,128,128]{2,1,0:T(8,128)} %copy-done.56), channel_id=1, source_target_pairs={{0,1},{1,0},{2,3},{3,2},{4,5},{5,4},{6,7},{7,6},{8,9},{9,8},{10,11... | collective-permute-start | bytes 589832 | tf_op jit(solution)/shard_map/ppermute | solution.py:348
  78.9 7.3 %collective-permute-start.16 = (f32[3,128,128]{2,1,0:T(8,128)}, f32[3,128,128]{2,1,0:T(8,128)S(1)}, u32[]{:S(2)}, u32[]{:S(2)}) collective-permute-start(f32[3,128,128]{2,1,0:T(8,128)} %copy-done.55), channel_id=1, source_target_pairs={{1,2},{2,1},{5,6},{6,5},{9,10},{10,9},{13,14},{14,13},{17,18},{18,... | collective-permute-start | bytes 589832 | tf_op jit(solution)/shard_map/ppermute | solution.py:349
  79.6 7.3 %collective-permute-start.17 = (f32[3,128,128]{2,1,0:T(8,128)}, f32[3,128,128]{2,1,0:T(8,128)S(1)}, u32[]{:S(2)}, u32[]{:S(2)}) collective-permute-start(f32[3,128,128]{2,1,0:T(8,128)} %copy-done.54), channel_id=1, source_target_pairs={{0,4},{4,0},{8,12},{12,8},{16,20},{20,16},{24,28},{28,24},{1,5},{5... | collective-permute-start | bytes 589832 | tf_op jit(solution)/shard_map/ppermute | solution.py:350
  79.7 8.3 %collective-permute-start.18 = (f32[3,128,128]{2,1,0:T(8,128)}, f32[3,128,128]{2,1,0:T(8,128)S(1)}, u32[]{:S(2)}, u32[]{:S(2)}) collective-permute-start(f32[3,128,128]{2,1,0:T(8,128)} %copy-done.53), channel_id=1, source_target_pairs={{0,28},{4,8},{8,4},{12,16},{16,12},{20,24},{24,20},{28,0},{1,29},{... | collective-permute-start | bytes 589832 | tf_op jit(solution)/shard_map/ppermute | solution.py:351
  88.7 1.4 copy-start.4
  90.1 1.4 copy-start.8
  97.1 1.2 copy-start.23
  99.9 14.9 %all-to-all-start.2 = ((f32[32,8,128]{2,1,0:T(8,128)}), f32[32,8,128]{2,1,0:T(8,128)S(1)}, u32[]{:S(2)}, u32[]{:S(2)}) async-start(f32[32,8,128]{2,1,0:T(8,128)} %copy-done.41), calls=%async_computation.2 | async-start | bytes 262144 | tf_op jit(solution)/shard_map/all_to_all | solution.py:355
  105.6 7.7 %collective-permute-start.21 = (f32[24,128]{1,0:T(8,128)S(1)}, f32[24,128]{1,0:T(8,128)S(1)}, u32[]{:S(2)}, u32[]{:S(2)}) collective-permute-start(f32[24,128]{1,0:T(8,128)S(1)} %get-tuple-element.65.refs_0_), channel_id=1, source_target_pairs={{0,3},{1,0},{2,1},{3,2},{4,7},{5,4},{6,5},{7,6},{8,11},{9,8},{10,9... | collective-permute-start | bytes 36872 | tf_op jit(solution)/shard_map/ppermute | solution.py:361
  109.2 4.6 %collective-permute-start.20 = (f32[24,128]{1,0:T(8,128)S(1)}, f32[24,128]{1,0:T(8,128)S(1)}, u32[]{:S(2)}, u32[]{:S(2)}) collective-permute-start(f32[24,128]{1,0:T(8,128)S(1)} %get-tuple-element.65.refs_0_), channel_id=1, source_target_pairs={{0,2},{1,3},{2,0},{3,1},{4,6},{5,7},{6,4},{7,5},{8,10},{9,11},{10,... | collective-permute-start | bytes 36872 | tf_op jit(solution)/shard_map/ppermute | solution.py:361
  109.2 5.5 %collective-permute-start.19 = (f32[24,128]{1,0:T(8,128)S(1)}, f32[24,128]{1,0:T(8,128)S(1)}, u32[]{:S(2)}, u32[]{:S(2)}) collective-permute-start(f32[24,128]{1,0:T(8,128)S(1)} %get-tuple-element.65.refs_0_), channel_id=1, source_target_pairs={{0,1},{1,2},{2,3},{3,0},{4,5},{5,6},{6,7},{7,4},{8,9},{9,10},{10,1... | collective-permute-start | bytes 36872 | tf_op jit(solution)/shard_map/ppermute | solution.py:361
  112.1 1.2 copy-start.9
  114.7 1.4 copy-start.10
  116.1 11.1 %copy-start.5 = (f32[3,8,128,128]{3,2,1,0:T(8,128)S(1)}, f32[3,8,128,128]{3,2,1,0:T(8,128)}, u32[]{:S(2)}) copy-start(f32[3,8,128,128]{3,2,1,0:T(8,128)} %copy-done.3) | copy-start | bytes 4718596
  116.1 11.1 %copy-start.14 = (f32[3,8,128,128]{3,2,1,0:T(8,128)S(1)}, f32[3,8,128,128]{3,2,1,0:T(8,128)}, u32[]{:S(2)}) copy-start(f32[3,8,128,128]{3,2,1,0:T(8,128)} %copy-done.13) | copy-start | bytes 4718596
  117.9 5.9 %collective-permute-start.22 = (f32[3,128,128]{2,1,0:T(8,128)S(1)}, f32[3,128,128]{2,1,0:T(8,128)S(1)}, u32[]{:S(2)}, u32[]{:S(2)}) collective-permute-start(f32[3,128,128]{2,1,0:T(8,128)S(1)} %get-tuple-element.70), channel_id=1, source_target_pairs={{0,1},{1,0},{2,3},{3,2},{4,5},{5,4},{6,7},{7,6},{8,9},{9,8},{10,11... | collective-permute-start | bytes 589832 | tf_op jit(solution)/shard_map/ppermute | solution.py:348
  118.9 4.8 %collective-permute-start.23 = (f32[3,128,128]{2,1,0:T(8,128)S(1)}, f32[3,128,128]{2,1,0:T(8,128)S(1)}, u32[]{:S(2)}, u32[]{:S(2)}) collective-permute-start(f32[3,128,128]{2,1,0:T(8,128)S(1)} %get-tuple-element.71), channel_id=1, source_target_pairs={{1,2},{2,1},{5,6},{6,5},{9,10},{10,9},{13,14},{14,13},{17,18},{18,... | collective-permute-start | bytes 589832 | tf_op jit(solution)/shard_map/ppermute | solution.py:349
  119.6 4.2 %collective-permute-start.24 = (f32[3,128,128]{2,1,0:T(8,128)S(1)}, f32[3,128,128]{2,1,0:T(8,128)S(1)}, u32[]{:S(2)}, u32[]{:S(2)}) collective-permute-start(f32[3,128,128]{2,1,0:T(8,128)S(1)} %get-tuple-element.72), channel_id=1, source_target_pairs={{0,4},{4,0},{8,12},{12,8},{16,20},{20,16},{24,28},{28,24},{1,5},{5... | collective-permute-start | bytes 589832 | tf_op jit(solution)/shard_map/ppermute | solution.py:350
  119.7 7.5 %collective-permute-start.25 = (f32[3,128,128]{2,1,0:T(8,128)S(1)}, f32[3,128,128]{2,1,0:T(8,128)S(1)}, u32[]{:S(2)}, u32[]{:S(2)}) collective-permute-start(f32[3,128,128]{2,1,0:T(8,128)S(1)} %get-tuple-element.73), channel_id=1, source_target_pairs={{0,28},{4,8},{8,4},{12,16},{16,12},{20,24},{24,20},{28,0},{1,29},{... | collective-permute-start | bytes 589832 | tf_op jit(solution)/shard_map/ppermute | solution.py:351
  127.2 1.4 copy-start.17
  128.6 25.9 %copy-start.15 = (f32[3,8,128,128]{3,2,1,0:T(8,128)S(1)}, f32[3,8,128,128]{3,2,1,0:T(8,128)}, u32[]{:S(2)}) copy-start(f32[3,8,128,128]{3,2,1,0:T(8,128)} %copy-done.13) | copy-start | bytes 4718596
  128.6 25.9 %copy-start.18 = (f32[3,8,128,128]{3,2,1,0:T(8,128)S(1)}, f32[3,8,128,128]{3,2,1,0:T(8,128)}, u32[]{:S(2)}) copy-start(f32[3,8,128,128]{3,2,1,0:T(8,128)} %copy-done.16) | copy-start | bytes 4718596
  135.1 1.1 copy-start.27
  139.5 15.0 %all-to-all-start.3 = ((f32[32,8,128]{2,1,0:T(8,128)}), f32[32,8,128]{2,1,0:T(8,128)S(1)}, u32[]{:S(2)}, u32[]{:S(2)}) async-start(f32[32,8,128]{2,1,0:T(8,128)} %copy-done.40), calls=%async_computation.3 | async-start | bytes 262144 | tf_op jit(solution)/shard_map/all_to_all | solution.py:355
  144.9 7.0 %collective-permute-start.26 = (bf16[3,128,128]{2,1,0:T(8,128)(2,1)}, bf16[3,128,128]{2,1,0:T(8,128)(2,1)S(1)}, u32[]{:S(2)}, u32[]{:S(2)}) collective-permute-start(bf16[3,128,128]{2,1,0:T(8,128)(2,1)} %copy-done.60), channel_id=1, source_target_pairs={{0,1},{1,0},{2,3},{3,2},{4,5},{5,4},{6,7},{7,6},{8,9},{9,8},{10,11... | collective-permute-start | bytes 294920 | tf_op jit(solution)/shard_map/ppermute | solution.py:348
  146.8 5.8 %collective-permute-start.27 = (bf16[3,128,128]{2,1,0:T(8,128)(2,1)}, bf16[3,128,128]{2,1,0:T(8,128)(2,1)S(1)}, u32[]{:S(2)}, u32[]{:S(2)}) collective-permute-start(bf16[3,128,128]{2,1,0:T(8,128)(2,1)} %copy-done.59), channel_id=1, source_target_pairs={{1,2},{2,1},{5,6},{6,5},{9,10},{10,9},{13,14},{14,13},{17,18},{18,... | collective-permute-start | bytes 294920 | tf_op jit(solution)/shard_map/ppermute | solution.py:349
  147.4 5.8 %collective-permute-start.28 = (bf16[3,128,128]{2,1,0:T(8,128)(2,1)}, bf16[3,128,128]{2,1,0:T(8,128)(2,1)S(1)}, u32[]{:S(2)}, u32[]{:S(2)}) collective-permute-start(bf16[3,128,128]{2,1,0:T(8,128)(2,1)} %copy-done.58), channel_id=1, source_target_pairs={{0,4},{4,0},{8,12},{12,8},{16,20},{20,16},{24,28},{28,24},{1,5},{5... | collective-permute-start | bytes 294920 | tf_op jit(solution)/shard_map/ppermute | solution.py:350
  147.5 6.3 %collective-permute-start.29 = (bf16[3,128,128]{2,1,0:T(8,128)(2,1)}, bf16[3,128,128]{2,1,0:T(8,128)(2,1)S(1)}, u32[]{:S(2)}, u32[]{:S(2)}) collective-permute-start(bf16[3,128,128]{2,1,0:T(8,128)(2,1)} %copy-done.57), channel_id=1, source_target_pairs={{0,28},{4,8},{8,4},{12,16},{16,12},{20,24},{24,20},{28,0},{1,29},{... | collective-permute-start | bytes 294920 | tf_op jit(solution)/shard_map/ppermute | solution.py:351
  154.5 1.4 copy-start.22
  155.9 1.4 copy-start.24
  157.3 1.4 copy-start.26
  158.7 1.4 copy-start.28
  (34 other events, 28.5 us)

commit v2 on v1

v2 whole, which is shorter than its diff:
```python
import functools

import jax
import jax.numpy as jnp
from jax import lax
from jax.experimental import pallas as pl
from jax.experimental.pallas import tpu as pltpu
from jax.sharding import PartitionSpec as P

precise = lax.Precision.HIGHEST
F32 = jnp.float32
BF16 = jnp.bfloat16
VMEM = pl.BlockSpec(memory_space=pltpu.VMEM)
SMEM = pl.BlockSpec(memory_space=pltpu.SMEM)


def call(kernel, scalars, arrays, outs, scratch=()):
    return pl.pallas_call(
        kernel,
        in_specs=[SMEM] * len(scalars) + [VMEM] * len(arrays),
        out_specs=[VMEM] * len(outs),
        out_shape=[jax.ShapeDtypeStruct(shape, dtype) for shape, dtype in outs],
        scratch_shapes=list(scratch),
        compiler_params=pltpu.CompilerParams(vmem_limit_bytes=16 * 1024 * 1024),
    )(*scalars, *arrays)


def odd(axis):
    return lax.axis_index(axis) % 2 == 1


def from_face(own, got, slot, face):
    if face >= 4:
        return own[slot, face ^ 1]
    return from_device(got, face, slot * own.shape[2], own.shape[2])


def from_device(got, face, start, count):
    near, far = (got[0], got[1]) if face < 2 else (got[2], got[3])
    rows = pl.ds(pl.multiple_of(start, 8), count)
    is_odd = odd("narrow") if face < 2 else odd("wide")
    if face % 2:
        return jnp.where(is_odd, far[rows], near[rows])
    return jnp.where(is_odd, near[rows], far[rows])


def send_faces(sends, slot, faces):
    odd_n = odd("narrow")
    odd_w = odd("wide")
    kind = sends[0].dtype
    width = faces[0].shape[0]
    rows = pl.ds(pl.multiple_of(slot * width, width), width)
    sends[0][rows] = jnp.where(odd_n, faces[0], faces[1]).astype(kind)
    sends[1][rows] = jnp.where(odd_n, faces[1], faces[0]).astype(kind)
    sends[2][rows] = jnp.where(odd_w, faces[2], faces[3]).astype(kind)
    sends[3][rows] = jnp.where(odd_w, faces[3], faces[2]).astype(kind)


def chunks(total, columns):
    return [(start, min(columns, total - start)) for start in range(0, total, columns)]


class Pack:
    def __init__(self, start, columns, weight, group, map_t, top):
        self.columns = columns
        self.sizes = [weight, group, map_t, top]
        self.starts = []
        for rows, lanes in self.sizes:
            self.starts.append(start)
            start += rows * len(chunks(lanes, columns))
        self.end = start

    def store(self, sends, refs):
        for start, (rows, lanes), ref in zip(self.starts, self.sizes, refs):
            for number, (lane, many) in enumerate(chunks(lanes, self.columns)):
                value = ref[:, lane : lane + many]
                if many < self.columns:
                    filler = jnp.zeros((rows, self.columns - many), F32)
                    value = jnp.concatenate([value, filler], axis=1)
                for send in sends:
                    send[start + number * rows : start + (number + 1) * rows] = value

    def read(self, got, face, part):
        rows, lanes = self.sizes[part]
        pieces = []
        for number, (lane, many) in enumerate(chunks(lanes, self.columns)):
            value = from_device(got, face, self.starts[part] + number * rows, rows)
            pieces.append(value[:, :many])
        return pieces[0] if len(pieces) == 1 else jnp.concatenate(pieces, axis=1)


def exact(first, second):
    return jnp.dot(first, second, precision=precise, preferred_element_type=F32)


def exact_t(first, second):
    return lax.dot_general(
        first,
        second,
        (((0,), (0,)), ((), ())),
        precision=precise,
        preferred_element_type=F32,
    )


def send_kernel(previous, deluxe, face_inverse, s0, s1, s2, s3, sems):
    odd_n = lax.axis_index("narrow") % 2
    odd_w = lax.axis_index("wide") % 2
    slots, _, width, _ = previous.shape
    copies = []
    for send, face in ((s0, 1 - odd_n), (s1, odd_n), (s2, 3 - odd_w), (s3, 2 + odd_w)):
        for part, source in enumerate((previous, deluxe, face_inverse)):
            for slot in range(slots):
                row = (part * slots + slot) * width
                copies.append(
                    pltpu.make_async_copy(
                        source.at[slot, face],
                        send.at[pl.ds(row, width)],
                        sems.at[len(copies)],
                    )
                )
    for copy in copies:
        copy.start()
    for copy in copies:
        copy.wait()


def live_rows(count, size, slot, face, shape):
    rows = lax.broadcasted_iota(jnp.int32, shape, 0)
    return rows < jnp.where(slot < count[0, 0], size[slot, face], 0)


def fold(values):
    rows, columns = values.shape
    return jnp.sum(values.reshape(rows // 8, 8, columns), axis=0)


def multiply(schur, vec, slot, width):
    span = 2 * width
    order = vec.shape[0]
    parts = []
    for start in range(0, order, span):
        block = jnp.dot(
            schur[slot, start : start + span], vec[...], preferred_element_type=F32
        )
        parts += [block[:width], block[width:]]
    return parts


def start_kernel(pack, partner, size, count, previous, load, schur, weight, group, map_t, top, g0, g1, g2, g3, averaged, local, s0, s1, s2, s3, vec):
    got = (g0, g1, g2, g3)
    pack.store((s0, s1, s2, s3), (weight, group, map_t, top))
    slots, faces, width, _ = previous.shape

    def one_slot(slot, carry):
        for face in range(faces):
            other = partner[slot, face]
            mine = previous[slot, face].astype(F32)
            theirs = from_face(previous, got, jnp.maximum(other, 0), face).astype(F32)
            value = jnp.where(other >= 0, 0.5 * (mine + theirs), mine)
            value = jnp.where(live_rows(count, size, slot, face, mine.shape), value, 0.0)
            averaged[slot, face] = value
            vec[face * width : (face + 1) * width] = value.astype(BF16)
        products = multiply(schur, vec, slot, width)
        sent = []
        for face in range(faces):
            value = load[slot, face].astype(F32) - products[face]
            value = jnp.where(live_rows(count, size, slot, face, value.shape), value, 0.0)
            local[slot, face] = value
            if face < 4:
                sent.append(value)
        send_faces((s0, s1, s2, s3), slot, sent)
        return carry

    lax.fori_loop(0, slots, one_slot, 0)


def scale_slot(slot, values, ids, deluxe, spread_weight, given, scaled, coarse_in):
    partner, count, size = ids
    rows = []
    faces = len(values)
    slots, _, width, _ = deluxe.shape
    for face, value in enumerate(values):
        half = value.astype(BF16)
        blocks = [deluxe[slot, face]]
        if face < 4:
            other = jnp.maximum(partner[slot, face], 0)
            blocks.append(from_device(given, face, (slots + other) * width, width))
        for side, block in enumerate(blocks):
            part = lax.dot_general(
                block, half, (((0,), (0,)), ((), ())), preferred_element_type=F32
            )
            part = jnp.where(live_rows(count, size, slot, face, part.shape), part, 0.0)
            scaled[slot, face + side * faces] = part.astype(BF16)
            if side == 0:
                rows.append(jnp.sum(spread_weight[slot, face] * part, axis=0, keepdims=True))
    coarse_in[pl.ds(pl.multiple_of(slot * faces, 8), faces)] = jnp.concatenate(rows, axis=0)


def restrict(coarse_map_t, coarse_in):
    count = coarse_map_t.shape[1]
    coarse_in[count:] = jnp.dot(
        coarse_map_t[...], coarse_in[:count], precision=precise, preferred_element_type=F32
    )


def first_scale_kernel(partner, size, count, local, deluxe, spread_weight, coarse_map_t, *refs):
    got, given = refs[:4], refs[4:8]
    residual, scaled, coarse_in = refs[8:]
    slots, faces = local.shape[:2]

    def one_slot(slot, carry):
        values = []
        for face in range(faces):
            other = partner[slot, face]
            theirs = from_face(local, got, jnp.maximum(other, 0), face)
            value = local[slot, face] + jnp.where(other >= 0, theirs, 0.0)
            residual[slot, face] = value
            values.append(value)
        scale_slot(slot, values, (partner, count, size), deluxe, spread_weight, given, scaled, coarse_in)
        return carry

    lax.fori_loop(0, slots, one_slot, 0)
    restrict(coarse_map_t, coarse_in)


def next_scale_kernel(partner, size, count, old_residual, image, sums, deluxe, spread_weight, coarse_map_t, *refs):
    got, given = refs[:4], refs[4:8]
    residual, full_image, scaled, coarse_in = refs[8:]
    slots, faces = image.shape[:2]
    totals = sums[...]
    step = totals[0:1] / totals[1:2]

    def one_slot(slot, carry):
        values = []
        for face in range(faces):
            other = partner[slot, face]
            theirs = from_face(image, got, jnp.maximum(other, 0), face).astype(F32)
            full = image[slot, face] + jnp.where(other >= 0, theirs, 0.0)
            full_image[slot, face] = full
            value = old_residual[slot, face] - step * full
            residual[slot, face] = value
            values.append(value)
        scale_slot(slot, values, (partner, count, size), deluxe, spread_weight, given, scaled, coarse_in)
        return carry

    lax.fori_loop(0, slots, one_slot, 0)
    restrict(coarse_map_t, coarse_in)


def inverse_kernel(partner, scaled, face_inverse, g0, g1, g2, g3, local_part):
    given = (g0, g1, g2, g3)
    slots, faces, width, _ = face_inverse.shape

    def one_slot(slot, carry):
        for face in range(faces + 4):
            if face < faces:
                block = face_inverse[slot, face]
            else:
                other = jnp.maximum(partner[slot, face - faces], 0)
                block = from_device(given, face - faces, (2 * slots + other) * width, width)
            local_part[slot, face] = jnp.dot(
                block, scaled[slot, face], preferred_element_type=F32
            )
        return carry

    lax.fori_loop(0, slots, one_slot, 0)


def across_weight_kernel(pack, partner, g0, g1, g2, g3, spread):
    got = (g0, g1, g2, g3)
    slots, faces, width, columns = spread.shape
    for face in range(faces):
        rows = pack.read(got, face, 0)
        for slot in range(slots):
            other = partner[slot, face]
            row = jnp.zeros((1, width), F32)
            for place in range(slots):
                number = place * (pack.sizes[0][0] // slots) + (face ^ 1)
                row = jnp.where(other == place, rows[number : number + 1], row)
            spread[slot, face] = jnp.broadcast_to(row, (columns, width)).T


def make_group_kernel(pack, narrow, slots):
    def group_kernel(*refs):
        rows_of = refs[:narrow]
        coarse_group = refs[narrow]
        got = refs[narrow + 1 : narrow + 5]
        packed, group_part, group_vec = refs[narrow + 5 :]
        each = coarse_group.shape[0]
        faces = each // slots
        here = lax.axis_index("narrow")
        restricted = None
        for back, rows in enumerate(rows_of):
            place = (here + narrow - back) % narrow
            group_vec[pl.ds(pl.multiple_of(place * each, 8), each)] = rows[:each]
            part = rows[each:]
            restricted = part if restricted is None else restricted + part
        group = jnp.concatenate(
            [coarse_group[...], pack.read(got, 0, 1), pack.read(got, 1, 1)], axis=0
        )
        part = exact(group, group_vec[...])
        group_part[...] = part
        picked = [
            part[slot * faces + face : slot * faces + face + 1]
            for face in (2, 3)
            for slot in range(slots)
        ]
        quotient, columns = restricted.shape
        filler = packed.shape[0] - quotient - len(picked)
        packed[...] = jnp.concatenate(
            [restricted] + picked + [jnp.zeros((filler, columns), F32)], axis=0
        )

    return group_kernel


def make_apply_kernel(pack, halves, later):
    def apply_kernel(partner, size, count, *refs):
        pairs = refs[:halves]
        refs = refs[halves:]
        group_part, map_t, coarse_top, local_part, spread_weight, across_weight, deluxe = refs[:7]
        given, packs = refs[7:11], refs[11:15]
        residual, schur = refs[15:17]
        refs = refs[17:]
        if later:
            old_direction, old_image = refs[:2]
            refs = refs[2:]
        direction, image, sums, s0, s1, s2, s3 = refs[:7]
        weighted, everyone, every_pack, coarse_out, vec = refs[7:]
        slots, faces, width, columns = direction.shape
        quotient, each = map_t.shape
        here = lax.axis_index("wide")
        wide = 2 * halves
        packed = pairs[0].shape[0] // 2
        for half, rows in enumerate(pairs):
            for other in range(2):
                place = here ^ (2 * half + other)
                block = rows[other * packed : (other + 1) * packed]
                everyone[pl.ds(pl.multiple_of(place * quotient, 8), quotient)] = block[:quotient]
                every_pack[pl.ds(pl.multiple_of(place * packed, 8), packed)] = block
        tops = exact(
            jnp.concatenate(
                [coarse_top[...], pack.read(packs, 2, 3), pack.read(packs, 3, 3)], axis=0
            ),
            everyone[...],
        )
        own_top = tops[:quotient]
        coarse_out[:each] = group_part[:each] + exact_t(map_t[...], own_top)
        for face in range(4):
            top = own_top if face < 2 else tops[(face - 1) * quotient : face * quotient]
            value = exact_t(pack.read(packs, face, 2), top)
            start = (face + 1) * each
            if face < 2:
                value = value + group_part[start : start + each]
            coarse_out[start : start + each] = value

        def coarse_row(face, other):
            row = coarse_out[pl.ds((face + 1) * each + other * faces + (face ^ 1), 1)]
            if face < 2:
                return row
            side = here + wide - 1 if face == 2 else here + 1
            start = (side % wide) * packed + quotient + (slots if face == 2 else 0)
            return row + every_pack[pl.ds(start + other, 1)]

        def weigh(part, weight, row, block, live):
            value = part + weight * row
            value = jnp.where(live, value, 0.0).astype(BF16)
            value = jnp.dot(block, value, preferred_element_type=F32)
            return jnp.where(live, value, 0.0)

        def weigh_slot(slot, carry):
            for face in range(faces):
                live = live_rows(count, size, slot, face, (width, columns))
                weighted[slot, face] = weigh(
                    local_part[slot, face],
                    spread_weight[slot, face],
                    coarse_out[pl.ds(slot * faces + face, 1)],
                    deluxe[slot, face],
                    live,
                )
                if face < 4:
                    other = partner[slot, face]
                    place = jnp.maximum(other, 0)
                    theirs = weigh(
                        local_part[slot, faces + face],
                        across_weight[slot, face],
                        coarse_row(face, place),
                        from_device(given, face, (slots + place) * width, width),
                        live,
                    )
                    direction[slot, face] = jnp.where(other >= 0, theirs, 0.0)
            return carry

        lax.fori_loop(0, slots, weigh_slot, 0)

        def one_slot(slot, carry):
            norm, curve, cross = carry
            for face in range(faces):
                other = partner[slot, face]
                mine = weighted[slot, face]
                if face < 4:
                    value = mine + direction[slot, face]
                else:
                    theirs = weighted[jnp.maximum(other, 0), face ^ 1]
                    value = mine + jnp.where(other >= 0, theirs, 0.0)
                direction[slot, face] = value
                vec[face * width : (face + 1) * width] = value.astype(BF16)
                norm = norm + fold(residual[slot, face] * mine)
            products = multiply(schur, vec, slot, width)
            sent = []
            for face in range(faces):
                live = live_rows(count, size, slot, face, products[face].shape)
                value = jnp.where(live, products[face], 0.0)
                image[slot, face] = value
                curve = curve + fold(direction[slot, face] * value)
                if later:
                    cross = cross + fold(
                        direction[slot, face] * old_image[slot, face]
                        + old_direction[slot, face] * value
                    )
                if face < 4:
                    sent.append(value)
            send_faces((s0, s1, s2, s3), slot, sent)
            return norm, curve, cross

        zero = jnp.zeros((8, columns), F32)
        found = lax.fori_loop(0, slots, one_slot, (zero, zero, zero))
        rows = [jnp.sum(one, axis=0, keepdims=True) for one in found]
        rows.append(jnp.zeros((5, columns), F32))
        sums[...] = jnp.concatenate(rows, axis=0)

    return apply_kernel


def finish_kernel(partner, averaged, direction, precond, residual, full_image, image, first_sums, later_sums, g0, g1, g2, g3, solution_out, residual_out):
    got = (g0, g1, g2, g3)
    slots, faces = image.shape[:2]
    first = first_sums[...]
    later = later_sums[...]
    first_step = first[0:1] / first[1:2]
    ratio = later[0:1] / first[0:1]
    curve = later[1:2] + ratio * (later[2:3] + ratio * first[1:2])
    step = later[0:1] / curve
    old_step = first_step + step * ratio

    def one_slot(slot, carry):
        for face in range(faces):
            other = partner[slot, face]
            theirs = from_face(image, got, jnp.maximum(other, 0), face).astype(F32)
            full = image[slot, face] + jnp.where(other >= 0, theirs, 0.0)
            full = full + ratio * full_image[slot, face]
            residual_out[slot, face] = residual[slot, face] - step * full
            solution_out[slot, face] = (
                averaged[slot, face]
                + old_step * direction[slot, face]
                + step * precond[slot, face]
            )
        return carry

    lax.fori_loop(0, slots, one_slot, 0)


def body(
    schur_matrix,
    face_inverse,
    deluxe,
    primal_weight,
    coarse_group,
    coarse_map,
    coarse_top,
    load_vector,
    previous,
    slot_count,
    partner,
    face_size,
):
    schur_matrix = schur_matrix[0, 0]
    face_inverse = face_inverse[0, 0]
    deluxe = deluxe[0, 0]
    coarse_group = coarse_group[0]
    coarse_map = coarse_map[0]
    load_vector = load_vector[0, 0]
    previous = previous[0, 0]
    partner = partner[0, 0]
    face_size = face_size[0, 0]
    shape = load_vector.shape
    slots, faces, width, columns = shape
    order = schur_matrix.shape[1]
    quotient = coarse_map.shape[1]
    wide = lax.axis_size("wide")
    narrow = lax.axis_size("narrow")
    one_face = (slots * width, columns)
    each = slots * faces
    pack = Pack(
        slots * width,
        columns,
        (each, width),
        coarse_group.shape,
        (quotient, each),
        coarse_top.shape,
    )

    narrow_near = [(i, i ^ 1) for i in range(narrow)]
    narrow_far = [(i, i + 1 if i % 2 else i - 1) for i in range(1, narrow - 1)]
    wide_near = [(i, i ^ 1) for i in range(wide)]
    wide_far = [(i, (i + 1 if i % 2 else i - 1) % wide) for i in range(wide)]

    def swap(sends):
        return (
            lax.ppermute(sends[0], "narrow", narrow_near),
            lax.ppermute(sends[1], "narrow", narrow_far),
            lax.ppermute(sends[2], "wide", wide_near),
            lax.ppermute(sends[3], "wide", wide_far),
        )

    def of_group(rows):
        got = [rows]
        for back in range(1, narrow):
            ring = [(i, (i + back) % narrow) for i in range(narrow)]
            got.append(lax.ppermute(rows, "narrow", ring))
        return got

    def across(rows, step):
        return lax.ppermute(rows, "wide", [(i, i ^ step) for i in range(wide)])

    def total_and_swap(rows, sends):
        rows = sum(of_group(rows))
        got = swap(sends)
        rows = rows + across(rows, 1)
        rows = sum([rows] + [across(rows, step) for step in range(2, wide, 2)])
        return rows, got

    given = swap(
        pl.pallas_call(
            send_kernel,
            name="send",
            in_specs=[pl.BlockSpec(memory_space=pl.ANY)] * 3,
            out_specs=[VMEM] * 4,
            out_shape=[jax.ShapeDtypeStruct((3 * slots * width, columns), BF16)] * 4,
            scratch_shapes=[pltpu.SemaphoreType.DMA((12 * slots,))],
        )(previous, deluxe, face_inverse)
    )
    flat_weight = primal_weight[0, 0].reshape(each, width)
    spread_weight = jnp.broadcast_to(primal_weight[0, 0][..., None], shape)
    coarse_map_t = coarse_map.T
    ids = (partner, face_size, slot_count)
    vec = pltpu.VMEM((order, columns), BF16)
    averaged, local, *sends = call(
        functools.partial(start_kernel, pack),
        ids,
        (previous, load_vector, schur_matrix, flat_weight, coarse_group, coarse_map_t, coarse_top)
        + given,
        [(shape, F32), (shape, F32)] + [((pack.end, columns), F32)] * 4,
        [vec],
    )
    wider = (slots, faces + 4, width, columns)
    scale_outs = [(wider, BF16), ((each + quotient, columns), F32)]
    packed_rows = -(-(quotient + 2 * slots) // 8) * 8
    packs = swap(sends)
    (across_weight,) = call(
        functools.partial(across_weight_kernel, pack),
        (partner,),
        packs,
        [((slots, 4, width, columns), F32)],
    )

    def apply_to(later, scaled, coarse_in, more, send_type):
        rows_of = of_group(coarse_in)
        (local_part,) = call(
            inverse_kernel, (partner,), (scaled, face_inverse) + given, [(wider, F32)]
        )
        packed, group_part = call(
            make_group_kernel(pack, narrow, slots),
            (),
            (*rows_of, coarse_group) + packs,
            [((packed_rows, columns), F32), ((3 * each, columns), F32)],
            [pltpu.VMEM((narrow * each, columns), F32)],
        )
        pair = jnp.concatenate([packed, across(packed, 1)], axis=0)
        pairs = [pair] + [across(pair, step) for step in range(2, wide, 2)]
        return call(
            make_apply_kernel(pack, wide // 2, later),
            ids,
            (
                *pairs,
                group_part,
                coarse_map_t,
                coarse_top,
                local_part,
                spread_weight,
                across_weight,
                deluxe,
            )
            + given
            + packs
            + more,
            [(shape, F32), (shape, F32), ((8, columns), F32)] + [(one_face, send_type)] * 4,
            [
                pltpu.VMEM(shape, F32),
                pltpu.VMEM((wide * quotient, columns), F32),
                pltpu.VMEM((wide * packed_rows, columns), F32),
                pltpu.VMEM((5 * each, columns), F32),
                vec,
            ],
        )

    residual, scaled, coarse_in = call(
        first_scale_kernel,
        ids,
        (local, deluxe, spread_weight, coarse_map_t) + packs + given,
        [(shape, F32)] + scale_outs,
    )
    direction, image, first_sums, *sends = apply_to(
        False, scaled, coarse_in, (residual, schur_matrix), F32
    )
    first_sums, got = total_and_swap(first_sums, sends)
    residual, full_image, scaled, coarse_in = call(
        next_scale_kernel,
        ids,
        (residual, image, first_sums, deluxe, spread_weight, coarse_map_t) + got + given,
        [(shape, F32), (shape, F32)] + scale_outs,
    )
    precond, later_image, later_sums, *sends = apply_to(
        True, scaled, coarse_in, (residual, schur_matrix, direction, image), BF16
    )
    later_sums, got = total_and_swap(later_sums, sends)
    solution, residual = call(
        finish_kernel,
        (partner,),
        (averaged, direction, precond, residual, full_image, later_image, first_sums, later_sums)
        + got,
        [(shape, F32), (shape, F32)],
    )
    return (solution[None, None], residual[None, None])


def solution(mesh):
    in_specs = (
        P("wide", "narrow", None, None, None),
        P("wide", "narrow", None, None, None, None),
        P("wide", "narrow", None, None, None, None),
        P("wide", "narrow", None, None, None),
        P("wide", "narrow", None),
        P("wide", "narrow", None),
        P("wide", None),
        P("wide", "narrow", None, None, None, None),
        P("wide", "narrow", None, None, None, None),
        P("wide", "narrow"),
        P("wide", "narrow", None, None),
        P("wide", "narrow", None, None),
    )
    out_specs = (
        P("wide", "narrow", None, None, None, None),
        P("wide", "narrow", None, None, None, None),
    )
    return jax.shard_map(body, mesh=mesh, in_specs=in_specs, out_specs=out_specs, check_vma=False)
```

time: 169 us -> 126 us (0.75); the launches traced: 167 us -> 126 us
  local copies, waits for them, and re-layouts: 52 us -> 3.3 us
  waiting for transfers between devices: 27.2 us -> 50.8 us
  starting transfers between devices: 61.6 us -> 45.1 us
    unnamed x131 -> x29, local copies, waits for them, and re-layouts: 51.6 us -> 2.84 us
    all_to_all x4 -> x0, starting transfers between devices: 21 us -> none  [from_all(): return lax.all_to_all(spread, AXES, 0, 0, tiled=False)]
    ppermute x6 -> x12, waiting for transfers between devices: 2.87 us -> 17.4 us  [of_group(): got.append(lax.ppermute(rows, 'narrow', ring))]
    ppermute x0 -> x16, starting transfers between devices: none -> 14.2 us  [across(): return lax.ppermute(rows, 'wide', [(i, i ^ step) for i in range(wide)])]
    ppermute x0 -> x16, waiting for transfers between devices: none -> 9.9 us  [across(): return lax.ppermute(rows, 'wide', [(i, i ^ step) for i in range(wide)])]
    ppermute x6 -> x4, starting transfers between devices: 14.7 us -> 6.34 us  [swap(): lax.ppermute(sends[3], 'wide', wide_far)]
    ppermute x6 -> x12, starting transfers between devices: 9.5 us -> 14.1 us  [of_group(): got.append(lax.ppermute(rows, 'narrow', ring))]
    ppermute x6 -> x4, starting transfers between devices: 12 us -> 7.65 us  [swap(): lax.ppermute(sends[0], 'narrow', narrow_near)]
  transfers between devices with their start and end apart: 34 -> 44, of which waited for: 14 -> 28; matrix products, arithmetic and copies ran while one was open for 0% -> 0% of each run, Pallas kernels for 1% -> 3%
where the time goes in v2:
time: 126 us
  waiting for transfers between devices  50.8 us (40%)
  starting transfers between devices  45.1 us (36%)
  Pallas kernels  25.1 us (20%)
  local copies, waits for them, and re-layouts  3.3 us (3%)
  between operations  1.65 us (1%)
    pallas_call x11, Pallas kernels, call(): pl.pallas_call(kernel, in_specs=[SMEM] * len(scalars) + [VMEM] * len(arra...  22.5 us
    ppermute x12, waiting for transfers between devices, of_group(): got.append(lax.ppermute(rows, 'narrow', ring))  17.4 us
    ppermute x16, starting transfers between devices, across(): return lax.ppermute(rows, 'wide', [(i, i ^ step) for i in range(wide)])  14.2 us
    ppermute x12, starting transfers between devices, of_group(): got.append(lax.ppermute(rows, 'narrow', ring))  14.1 us
    ppermute x4, waiting for transfers between devices, swap(): lax.ppermute(sends[3], 'wide', wide_far)  13.5 us
    ppermute x4, waiting for transfers between devices, swap(): lax.ppermute(sends[0], 'narrow', narrow_near)  9.98 us
    ppermute x16, waiting for transfers between devices, across(): return lax.ppermute(rows, 'wide', [(i, i ^ step) for i in range(wide)])  9.9 us
    ppermute x4, starting transfers between devices, swap(): lax.ppermute(sends[0], 'narrow', narrow_near)  7.65 us
  transfers between devices with their start and end apart: 44, of which 28 were waited for; matrix products, arithmetic and copies ran while one was open for 0% of the time, Pallas kernels for 3%

profile of v2, /device:TPU:0, one launch (start us, length us, event | category | flops | bytes accessed | tf_op | source)
XLA Modules:
  0.0 126.0 jit_solution(9473257508361494123)
XLA Ops:
  0.7 2.6 %send.1 = (bf16[1152,128]{1,0:T(8,128)(2,1)}, bf16[1152,128]{1,0:T(8,128)(2,1)}, bf16[1152,128]{1,0:T(8,128)(2,1)}, bf16[1152,128]{1,0:T(8,128)(2,1)}) custom-call(bf16[3,8,128,128]{3,2,1,0:T(8,128)(2,1)} %bitcast.30, bf16[3,8,128,128]{3,2,1,0:T(8,128)(2,1)} %bitcast.22, bf16[3,8,128,128]{3,2,1,0:T(8,128)(2,1)} %bitcast.27), custom_call_target="tpu_custom_call" | custom-call | tf_op jit(solution)/shard_map/send/pallas_call | solution.py:535
  3.3 3.1 %collective-permute-start = (bf16[1152,128]{1,0:T(8,128)(2,1)}, bf16[1152,128]{1,0:T(8,128)(2,1)S(1)}, u32[]{:S(2)}, u32[]{:S(2)}) collective-permute-start(bf16[1152,128]{1,0:T(8,128)(2,1)} %get-tuple-element.39), channel_id=1, source_target_pairs={{0,1},{1,0},{2,3},{3,2},{4,5},{5,4},{6,7},{7,6},{8,9},{9,8},{10,11... | collective-permute-start | bytes 884744 | tf_op jit(solution)/shard_map/ppermute | solution.py:511
  6.5 0.7 collective-permute-start.1
  7.2 2.5 %collective-permute-start.3 = (bf16[1152,128]{1,0:T(8,128)(2,1)}, bf16[1152,128]{1,0:T(8,128)(2,1)S(1)}, u32[]{:S(2)}, u32[]{:S(2)}) collective-permute-start(bf16[1152,128]{1,0:T(8,128)(2,1)} %get-tuple-element.42), channel_id=1, source_target_pairs={{0,28},{4,8},{8,4},{12,16},{16,12},{20,24},{24,20},{28,0},{1,29},{... | collective-permute-start | bytes 884744 | tf_op jit(solution)/shard_map/ppermute | solution.py:514
  10.5 3.2 %collective-permute-done.g0.refs_4_.refs_11_ = bf16[1152,128]{1,0:T(8,128)(2,1)S(1)} collective-permute-done((bf16[1152,128]{1,0:T(8,128)(2,1)}, bf16[1152,128]{1,0:T(8,128)(2,1)S(1)}, u32[]{:S(2)}, u32[]{:S(2)}) %collective-permute-start) | collective-permute-done | bytes 294944 | tf_op jit(solution)/shard_map/ppermute | solution.py:511
  13.7 3.3 %collective-permute-done.3.g3.refs_7_.refs_14_ = bf16[1152,128]{1,0:T(8,128)(2,1)S(1)} collective-permute-done((bf16[1152,128]{1,0:T(8,128)(2,1)}, bf16[1152,128]{1,0:T(8,128)(2,1)S(1)}, u32[]{:S(2)}, u32[]{:S(2)}) %collective-permute-start.3) | collective-permute-done | bytes 294944 | tf_op jit(solution)/shard_map/ppermute | solution.py:514
  17.1 2.8 %copy-done = bf16[1,1,3,1024,1024]{4,3,2,1,0:T(8,128)(2,1)S(1)} copy-done((bf16[1,1,3,1024,1024]{4,3,2,1,0:T(8,128)(2,1)S(1)}, bf16[1,1,3,1024,1024]{4,3,2,1,0:T(8,128)(2,1)}, u32[]{:S(2)}) %copy-start) | copy-done | bytes 6291480
  19.9 3.2 %shard_map.131 = (f32[3,8,128,128]{3,2,1,0:T(8,128)S(1)}, f32[3,8,128,128]{3,2,1,0:T(8,128)S(1)}, f32[448,128]{1,0:T(8,128)S(1)}, f32[448,128]{1,0:T(8,128)S(1)}...) custom-call(s32[3,8]{1,0:T(4,128)S(1)} %get-tuple-element.77.partner, s32[3,8]{1,0:T(4,128)S(1)} %get-tuple-element.76.size, ...), custom_call_target="tpu_custom_call" | custom-call | tf_op jit(solution)/shard_map/pallas_call | solution.py:18
  23.0 4.4 %collective-permute-start.4 = (f32[448,128]{1,0:T(8,128)S(1)}, f32[448,128]{1,0:T(8,128)S(1)}, u32[]{:S(2)}, u32[]{:S(2)}) collective-permute-start(f32[448,128]{1,0:T(8,128)S(1)} %get-tuple-element.45), channel_id=1, source_target_pairs={{0,1},{1,0},{2,3},{3,2},{4,5},{5,4},{6,7},{7,6},{8,9},{9,8},{10,11... | collective-permute-start | bytes 688136 | tf_op jit(solution)/shard_map/ppermute | solution.py:511
  27.5 0.7 collective-permute-start.5
  28.2 1.8 %collective-permute-start.7 = (f32[448,128]{1,0:T(8,128)S(1)}, f32[448,128]{1,0:T(8,128)S(1)}, u32[]{:S(2)}, u32[]{:S(2)}) collective-permute-start(f32[448,128]{1,0:T(8,128)S(1)} %get-tuple-element.48), channel_id=1, source_target_pairs={{0,28},{4,8},{8,4},{12,16},{16,12},{20,24},{24,20},{28,0},{1,29},{... | collective-permute-start | bytes 688136 | tf_op jit(solution)/shard_map/ppermute | solution.py:514
  30.0 3.4 %collective-permute-done.4.refs_0_.refs_5_.g0.refs_15_ = f32[448,128]{1,0:T(8,128)S(1)} collective-permute-done((f32[448,128]{1,0:T(8,128)S(1)}, f32[448,128]{1,0:T(8,128)S(1)}, u32[]{:S(2)}, u32[]{:S(2)}) %collective-permute-start.4) | collective-permute-done | bytes 229408 | tf_op jit(solution)/shard_map/ppermute | solution.py:511
  33.4 2.7 %collective-permute-done.7.refs_3_.refs_8_.g3.refs_18_ = f32[448,128]{1,0:T(8,128)S(1)} collective-permute-done((f32[448,128]{1,0:T(8,128)S(1)}, f32[448,128]{1,0:T(8,128)S(1)}, u32[]{:S(2)}, u32[]{:S(2)}) %collective-permute-start.7) | collective-permute-done | bytes 229408 | tf_op jit(solution)/shard_map/ppermute | solution.py:514
  36.6 1.7 %shard_map.132 = (f32[3,8,128,128]{3,2,1,0:T(8,128)S(1)}, bf16[3,12,128,128]{3,2,1,0:T(8,128)(2,1)S(1)}, f32[32,128]{1,0:T(8,128)S(1)}) custom-call(s32[3,8]{1,0:T(4,128)S(1)} %get-tuple-element.77.partner, s32[3,8]{1,0:T(4,128)S(1)} %get-tuple-element.76.size, s32[1,1]{1,0:T(1,128)S(6)} %copy.20.count, f32[3,8,128,128]{3,2,1,0:T(8,128)S(1)} %get-tuple-element.44.local, ...), custom_call_target="tpu_custom_call" | custom-call | tf_op jit(solution)/shard_map/pallas_call | solution.py:18
  38.3 0.9 collective-permute-start.10
  39.2 2.0 %collective-permute-start.9 = (f32[32,128]{1,0:T(8,128)S(1)}, f32[32,128]{1,0:T(8,128)S(1)}, u32[]{:S(2)}, u32[]{:S(2)}) collective-permute-start(f32[32,128]{1,0:T(8,128)S(1)} %get-tuple-element.49.refs_0_), channel_id=1, source_target_pairs={{0,2},{1,3},{2,0},{3,1},{4,6},{5,7},{6,4},{7,5},{8,10},{9,11},{10,... | collective-permute-start | bytes 49160 | tf_op jit(solution)/shard_map/ppermute | solution.py:521
  41.3 1.9 %collective-permute-start.8 = (f32[32,128]{1,0:T(8,128)S(1)}, f32[32,128]{1,0:T(8,128)S(1)}, u32[]{:S(2)}, u32[]{:S(2)}) collective-permute-start(f32[32,128]{1,0:T(8,128)S(1)} %get-tuple-element.49.refs_0_), channel_id=1, source_target_pairs={{0,1},{1,2},{2,3},{3,0},{4,5},{5,6},{6,7},{7,4},{8,9},{9,10},{10,1... | collective-permute-start | bytes 49160 | tf_op jit(solution)/shard_map/ppermute | solution.py:521
  43.2 0.7 collective-permute-done.9.refs_2_
  43.9 2.9 %collective-permute-done.8.refs_1_ = f32[32,128]{1,0:T(8,128)S(1)} collective-permute-done((f32[32,128]{1,0:T(8,128)S(1)}, f32[32,128]{1,0:T(8,128)S(1)}, u32[]{:S(2)}, u32[]{:S(2)}) %collective-permute-start.8) | collective-permute-done | bytes 16416 | tf_op jit(solution)/shard_map/ppermute | solution.py:521
  47.1 1.1 collective-permute-done.11
  48.3 1.4 %collective-permute-start.14 = (f32[32,128]{1,0:T(8,128)S(1)}, f32[32,128]{1,0:T(8,128)S(1)}, u32[]{:S(2)}, u32[]{:S(2)}) collective-permute-start(f32[32,128]{1,0:T(8,128)S(1)} %constant_dynamic-update-slice_fusion.refs_0_), channel_id=1, source_target_pairs={{0,24},{4,28},{8,16},{12,20},{16,8},{20,12},{24,0},{28,4},{1,25},{... | collective-permute-start | bytes 49160 | tf_op jit(solution)/shard_map/ppermute | solution.py:525
  49.7 1.7 %collective-permute-start.13 = (f32[32,128]{1,0:T(8,128)S(1)}, f32[32,128]{1,0:T(8,128)S(1)}, u32[]{:S(2)}, u32[]{:S(2)}) collective-permute-start(f32[32,128]{1,0:T(8,128)S(1)} %constant_dynamic-update-slice_fusion.refs_0_), channel_id=1, source_target_pairs={{0,16},{4,20},{8,24},{12,28},{16,0},{20,4},{24,8},{28,12},{1,17},{... | collective-permute-start | bytes 49160 | tf_op jit(solution)/shard_map/ppermute | solution.py:525
  51.9 0.8 shard_map.135.refs_9_
  52.7 1.3 %shard_map.134.refs_7_ = f32[3,12,128,128]{3,2,1,0:T(8,128)S(1)} custom-call(s32[3,8]{1,0:T(4,128)S(1)} %get-tuple-element.77.partner, bf16[3,12,128,128]{3,2,1,0:T(8,128)(2,1)S(1)} %get-tuple-element.52.scaled, bf16[3,8,128,128]{3,2,1,0:T(8,128)(2,1)S(1)} %bitcast.28, bf16[1152,128]{1,0:T(8,128)(2,1)S(1)} %collective-permute-done.g0.refs_4_.refs_11_, ...), custom_call_target="tpu_custom_call" | custom-call | tf_op jit(solution)/shard_map/pallas_call | solution.py:18
  54.1 1.0 collective-permute-done.12.refs_1_
  55.1 4.4 %shard_map.136 = (f32[3,8,128,128]{3,2,1,0:T(8,128)S(1)}, f32[3,8,128,128]{3,2,1,0:T(8,128)S(1)}, f32[8,128]{1,0:T(8,128)S(1)}, f32[384,128]{1,0:T(8,128)S(1)}, ...) custom-call(s32[3,8]{1,0:T(4,128)S(1)} %get-tuple-element.77.partner, ...), custom_call_target="tpu_custom_call" | custom-call | tf_op jit(solution)/shard_map/pallas_call | solution.py:18
  59.7 1.0 collective-permute-start.16
  60.7 0.9 collective-permute-start.15
  61.6 1.6 %collective-permute-done.17 = f32[8,128]{1,0:T(8,128)S(1)} collective-permute-done((f32[8,128]{1,0:T(8,128)S(1)}, f32[8,128]{1,0:T(8,128)S(1)}, u32[]{:S(2)}, u32[]{:S(2)}) %collective-permute-start.17) | collective-permute-done | bytes 4128 | tf_op jit(solution)/shard_map/ppermute | solution.py:521
  63.2 1.1 collective-permute-done.16
  64.2 1.9 %collective-permute-done.15 = f32[8,128]{1,0:T(8,128)S(1)} collective-permute-done((f32[8,128]{1,0:T(8,128)S(1)}, f32[8,128]{1,0:T(8,128)S(1)}, u32[]{:S(2)}, u32[]{:S(2)}) %collective-permute-start.15) | collective-permute-done | bytes 4128 | tf_op jit(solution)/shard_map/ppermute | solution.py:521
  66.1 1.2 collective-permute-done.18
  67.3 2.5 %collective-permute-start.21 = (f32[8,128]{1,0:T(8,128)S(1)}, f32[8,128]{1,0:T(8,128)S(1)}, u32[]{:S(2)}, u32[]{:S(2)}) collective-permute-start(f32[8,128]{1,0:T(8,128)S(1)} %add.45), channel_id=1, source_target_pairs={{0,24},{4,28},{8,16},{12,20},{16,8},{20,12},{24,0},{28,4},{1,25},{... | collective-permute-start | bytes 12296 | tf_op jit(solution)/shard_map/ppermute | solution.py:525
  69.8 1.0 collective-permute-start.19
  70.8 0.7 collective-permute-start.23
  71.8 1.5 %collective-permute-done.20 = f32[8,128]{1,0:T(8,128)S(1)} collective-permute-done((f32[8,128]{1,0:T(8,128)S(1)}, f32[8,128]{1,0:T(8,128)S(1)}, u32[]{:S(2)}, u32[]{:S(2)}) %collective-permute-start.20) | collective-permute-done | bytes 4128 | tf_op jit(solution)/shard_map/ppermute | solution.py:525
  73.3 1.0 collective-permute-start.25
  74.4 2.5 %collective-permute-done.22.refs_0_ = f32[384,128]{1,0:T(8,128)S(1)} collective-permute-done((f32[384,128]{1,0:T(8,128)S(1)}, f32[384,128]{1,0:T(8,128)S(1)}, u32[]{:S(2)}, u32[]{:S(2)}) %collective-permute-start.22) | collective-permute-done | bytes 196640 | tf_op jit(solution)/shard_map/ppermute | solution.py:511
  76.9 3.8 %collective-permute-done.25.refs_3_ = f32[384,128]{1,0:T(8,128)S(1)} collective-permute-done((f32[384,128]{1,0:T(8,128)S(1)}, f32[384,128]{1,0:T(8,128)S(1)}, u32[]{:S(2)}, u32[]{:S(2)}) %collective-permute-start.25) | collective-permute-done | bytes 196640 | tf_op jit(solution)/shard_map/ppermute | solution.py:514
  80.7 1.8 %shard_map.137 = (f32[3,8,128,128]{3,2,1,0:T(8,128)S(1)}, f32[3,8,128,128]{3,2,1,0:T(8,128)S(1)}, bf16[3,12,128,128]{3,2,1,0:T(8,128)(2,1)S(1)}, f32[32,128]{1,0:T(8,128)S(1)}) custom-call(s32[3,8]{1,0:T(4,128)S(1)} %get-tuple-element.77.partner, s32[3,8]{1,0:T(4,128)S(1)} %get-tuple-element.76.size, s32[1,1]{1,0:T(1,128)S(6)} %copy.20.count, ...), custom_call_target="tpu_custom_call" | custom-call | tf_op jit(solution)/shard_map/pallas_call | solution.py:18
  82.4 1.2 collective-permute-start.28
  83.7 2.9 %collective-permute-start.27 = (f32[32,128]{1,0:T(8,128)S(1)}, f32[32,128]{1,0:T(8,128)S(1)}, u32[]{:S(2)}, u32[]{:S(2)}) collective-permute-start(f32[32,128]{1,0:T(8,128)S(1)} %get-tuple-element.61.refs_0_), channel_id=1, source_target_pairs={{0,2},{1,3},{2,0},{3,1},{4,6},{5,7},{6,4},{7,5},{8,10},{9,11},{10,... | collective-permute-start | bytes 49160 | tf_op jit(solution)/shard_map/ppermute | solution.py:521
  86.5 0.9 collective-permute-start.26
  87.5 1.0 collective-permute-done.27.refs_2_
  88.5 3.6 %collective-permute-done.26.refs_1_ = f32[32,128]{1,0:T(8,128)S(1)} collective-permute-done((f32[32,128]{1,0:T(8,128)S(1)}, f32[32,128]{1,0:T(8,128)S(1)}, u32[]{:S(2)}, u32[]{:S(2)}) %collective-permute-start.26) | collective-permute-done | bytes 16416 | tf_op jit(solution)/shard_map/ppermute | solution.py:521
  92.4 1.1 collective-permute-done.29
  93.5 1.1 collective-permute-start.32
  94.7 2.3 %collective-permute-start.30 = (f32[32,128]{1,0:T(8,128)S(1)}, f32[32,128]{1,0:T(8,128)S(1)}, u32[]{:S(2)}, u32[]{:S(2)}) collective-permute-start(f32[32,128]{1,0:T(8,128)S(1)} %constant_dynamic-update-slice_fusion.2.refs_0_), channel_id=1, source_target_pairs={{0,8},{4,12},{8,0},{12,4},{16,24},{20,28},{24,16},{28,20},{1,9},{5... | collective-permute-start | bytes 49160 | tf_op jit(solution)/shard_map/ppermute | solution.py:525
  97.0 1.3 %shard_map.139.refs_7_ = f32[3,12,128,128]{3,2,1,0:T(8,128)S(1)} custom-call(s32[3,8]{1,0:T(4,128)S(1)} %get-tuple-element.77.partner, bf16[3,12,128,128]{3,2,1,0:T(8,128)(2,1)S(1)} %get-tuple-element.64.scaled, bf16[3,8,128,128]{3,2,1,0:T(8,128)(2,1)S(1)} %bitcast.29, bf16[1152,128]{1,0:T(8,128)(2,1)S(1)} %collective-permute-done.g0.refs_4_.refs_11_, ...), custom_call_target="tpu_custom_call" | custom-call | tf_op jit(solution)/shard_map/pallas_call | solution.py:18
  98.7 4.5 %shard_map.140 = (f32[3,8,128,128]{3,2,1,0:T(8,128)S(1)}, f32[3,8,128,128]{3,2,1,0:T(8,128)S(1)}, f32[8,128]{1,0:T(8,128)S(1)}, bf16[384,128]{1,0:T(8,128)(2,1)S...) custom-call(s32[3,8]{1,0:T(4,128)S(1)} %get-tuple-element.77.partner, ...), custom_call_target="tpu_custom_call" | custom-call | tf_op jit(solution)/shard_map/pallas_call | solution.py:18
  103.5 1.1 collective-permute-start.34
  104.6 0.7 collective-permute-start.33
  105.3 1.6 %collective-permute-done.35 = f32[8,128]{1,0:T(8,128)S(1)} collective-permute-done((f32[8,128]{1,0:T(8,128)S(1)}, f32[8,128]{1,0:T(8,128)S(1)}, u32[]{:S(2)}, u32[]{:S(2)}) %collective-permute-start.35) | collective-permute-done | bytes 4128 | tf_op jit(solution)/shard_map/ppermute | solution.py:521
  106.9 1.1 collective-permute-done.34
  108.0 2.0 %collective-permute-done.33 = f32[8,128]{1,0:T(8,128)S(1)} collective-permute-done((f32[8,128]{1,0:T(8,128)S(1)}, f32[8,128]{1,0:T(8,128)S(1)}, u32[]{:S(2)}, u32[]{:S(2)}) %collective-permute-start.33) | collective-permute-done | bytes 4128 | tf_op jit(solution)/shard_map/ppermute | solution.py:521
  110.0 1.2 collective-permute-done.36
  111.2 2.6 %collective-permute-start.39 = (f32[8,128]{1,0:T(8,128)S(1)}, f32[8,128]{1,0:T(8,128)S(1)}, u32[]{:S(2)}, u32[]{:S(2)}) collective-permute-start(f32[8,128]{1,0:T(8,128)S(1)} %add.52), channel_id=1, source_target_pairs={{0,24},{4,28},{8,16},{12,20},{16,8},{20,12},{24,0},{28,4},{1,25},{... | collective-permute-start | bytes 12296 | tf_op jit(solution)/shard_map/ppermute | solution.py:525
  114.0 0.7 collective-permute-start.37
  114.7 0.7 collective-permute-start.41
  115.7 1.7 %collective-permute-done.38 = f32[8,128]{1,0:T(8,128)S(1)} collective-permute-done((f32[8,128]{1,0:T(8,128)S(1)}, f32[8,128]{1,0:T(8,128)S(1)}, u32[]{:S(2)}, u32[]{:S(2)}) %collective-permute-start.38) | collective-permute-done | bytes 4128 | tf_op jit(solution)/shard_map/ppermute | solution.py:525
  117.4 1.0 collective-permute-start.43
  118.5 0.8 collective-permute-done.40.g0
  119.3 3.6 %collective-permute-done.43.g3 = bf16[384,128]{1,0:T(8,128)(2,1)S(1)} collective-permute-done((bf16[384,128]{1,0:T(8,128)(2,1)S(1)}, bf16[384,128]{1,0:T(8,128)(2,1)S(1)}, u32[]{:S(2)}, u32[]{:S(2)}) %collective-permute-start.43) | collective-permute-done | bytes 98336 | tf_op jit(solution)/shard_map/ppermute | solution.py:514
  123.0 3.0 %shard_map.141 = (f32[3,8,128,128]{3,2,1,0:T(8,128)}, f32[3,8,128,128]{3,2,1,0:T(8,128)}) custom-call(s32[3,8]{1,0:T(4,128)S(1)} %get-tuple-element.77.partner, f32[3,8,128,128]{3,2,1,0:T(8,128)S(1)} %get-tuple-element.43.averaged, f32[3,8,128,128]{3,2,1,0:T(8,128)S(1)} %get-tuple-element.54.refs_21_.direction, ...), custom_call_target="tpu_custom_call" | custom-call | tf_op jit(solution)/shard_map/pallas_call | solution.py:18
  (75 shorter events, 3.6 us)
Async XLA Ops:
  0.6 16.4 %copy-start.3 = (bf16[1,1,3,8,128,128]{5,4,3,2,1,0:T(8,128)(2,1)S(1)}, bf16[1,1,3,8,128,128]{5,4,3,2,1,0:T(8,128)(2,1)}, u32[]{:S(2)}) copy-start(bf16[1,1,3,8,128,128]{5,4,3,2,1,0:T(8,128)(2,1)} %param.20) | copy-start | bytes 2359300
  0.6 9.8 %copy-start.9 = (s32[1,1,3,8]{3,1,2,0:T(1,128)S(1)}, s32[1,1,3,8]{3,1,2,0:T(1,128)}, u32[]{:S(2)}) copy-start(s32[1,1,3,8]{3,1,2,0:T(1,128)} %param.23) | copy-start | bytes 292
  0.7 9.8 %copy-start.10 = (s32[1,1,3,8]{3,1,2,0:T(1,128)S(1)}, s32[1,1,3,8]{3,1,2,0:T(1,128)}, u32[]{:S(2)}) copy-start(s32[1,1,3,8]{3,1,2,0:T(1,128)} %param.22) | copy-start | bytes 292
  0.7 16.4 %copy-start.8 = (f32[8,64]{1,0:T(8,128)S(1)}, f32[8,64]{1,0:T(8,128)}, u32[]{:S(2)}) copy-start(f32[8,64]{1,0:T(8,128)} %refs_6_.3) | copy-start | bytes 6148
  0.7 16.4 %copy-start.7 = (f32[1,1,3,8,128]{4,3,2,1,0:T(8,128)S(1)}, f32[1,1,3,8,128]{4,3,2,1,0:T(8,128)}, u32[]{:S(2)}) copy-start(f32[1,1,3,8,128]{4,3,2,1,0:T(8,128)} %param.15) | copy-start | bytes 36868
  0.7 16.4 %copy-start.4 = (bf16[1,1,3,8,128,128]{5,4,3,2,1,0:T(8,128)(2,1)S(1)}, bf16[1,1,3,8,128,128]{5,4,3,2,1,0:T(8,128)(2,1)}, u32[]{:S(2)}) copy-start(bf16[1,1,3,8,128,128]{5,4,3,2,1,0:T(8,128)(2,1)} %param.19) | copy-start | bytes 2359300
  0.7 16.4 %copy-start.6 = (f32[1,24,8]{1,2,0:T(8,128)S(1)}, f32[1,24,8]{1,2,0:T(8,128)}, u32[]{:S(2)}) copy-start(f32[1,24,8]{1,2,0:T(8,128)} %param.17) | copy-start | bytes 2308
  0.7 16.4 %copy-start.5 = (f32[1,24,96]{2,1,0:T(8,128)S(1)}, f32[1,24,96]{2,1,0:T(8,128)}, u32[]{:S(2)}) copy-start(f32[1,24,96]{2,1,0:T(8,128)} %param.16) | copy-start | bytes 27652
  3.3 10.3 %collective-permute-start = (bf16[1152,128]{1,0:T(8,128)(2,1)}, bf16[1152,128]{1,0:T(8,128)(2,1)S(1)}, u32[]{:S(2)}, u32[]{:S(2)}) collective-permute-start(bf16[1152,128]{1,0:T(8,128)(2,1)} %get-tuple-element.39), channel_id=1, source_target_pairs={{0,1},{1,0},{2,3},{3,2},{4,5},{5,4},{6,7},{7,6},{8,9},{9,8},{10,11... | collective-permute-start | bytes 884744 | tf_op jit(solution)/shard_map/ppermute | solution.py:511
  6.5 7.2 %collective-permute-start.1 = (bf16[1152,128]{1,0:T(8,128)(2,1)}, bf16[1152,128]{1,0:T(8,128)(2,1)S(1)}, u32[]{:S(2)}, u32[]{:S(2)}) collective-permute-start(bf16[1152,128]{1,0:T(8,128)(2,1)} %get-tuple-element.40), channel_id=1, source_target_pairs={{1,2},{2,1},{5,6},{6,5},{9,10},{10,9},{13,14},{14,13},{17,18},{18,... | collective-permute-start | bytes 884744 | tf_op jit(solution)/shard_map/ppermute | solution.py:512
  7.1 6.5 %collective-permute-start.2 = (bf16[1152,128]{1,0:T(8,128)(2,1)}, bf16[1152,128]{1,0:T(8,128)(2,1)S(1)}, u32[]{:S(2)}, u32[]{:S(2)}) collective-permute-start(bf16[1152,128]{1,0:T(8,128)(2,1)} %get-tuple-element.41), channel_id=1, source_target_pairs={{0,4},{4,0},{8,12},{12,8},{16,20},{20,16},{24,28},{28,24},{1,5},{5... | collective-permute-start | bytes 884744 | tf_op jit(solution)/shard_map/ppermute | solution.py:513
  7.2 9.8 %collective-permute-start.3 = (bf16[1152,128]{1,0:T(8,128)(2,1)}, bf16[1152,128]{1,0:T(8,128)(2,1)S(1)}, u32[]{:S(2)}, u32[]{:S(2)}) collective-permute-start(bf16[1152,128]{1,0:T(8,128)(2,1)} %get-tuple-element.42), channel_id=1, source_target_pairs={{0,28},{4,8},{8,4},{12,16},{16,12},{20,24},{24,20},{28,0},{1,29},{... | collective-permute-start | bytes 884744 | tf_op jit(solution)/shard_map/ppermute | solution.py:514
  17.1 2.8 %copy-start = (bf16[1,1,3,1024,1024]{4,3,2,1,0:T(8,128)(2,1)S(1)}, bf16[1,1,3,1024,1024]{4,3,2,1,0:T(8,128)(2,1)}, u32[]{:S(2)}) copy-start(bf16[1,1,3,1024,1024]{4,3,2,1,0:T(8,128)(2,1)} %param.12) | copy-start | bytes 18874372
  23.0 13.5 %copy-start.1 = (bf16[1,1,3,8,128,128]{5,4,3,2,1,0:T(8,128)(2,1)S(1)}, bf16[1,1,3,8,128,128]{5,4,3,2,1,0:T(8,128)(2,1)}, u32[]{:S(2)}) copy-start(bf16[1,1,3,8,128,128]{5,4,3,2,1,0:T(8,128)(2,1)} %param.14) | copy-start | bytes 2359300
  23.0 10.3 %collective-permute-start.4 = (f32[448,128]{1,0:T(8,128)S(1)}, f32[448,128]{1,0:T(8,128)S(1)}, u32[]{:S(2)}, u32[]{:S(2)}) collective-permute-start(f32[448,128]{1,0:T(8,128)S(1)} %get-tuple-element.45), channel_id=1, source_target_pairs={{0,1},{1,0},{2,3},{3,2},{4,5},{5,4},{6,7},{7,6},{8,9},{9,8},{10,11... | collective-permute-start | bytes 688136 | tf_op jit(solution)/shard_map/ppermute | solution.py:511
  27.5 5.9 %collective-permute-start.5 = (f32[448,128]{1,0:T(8,128)S(1)}, f32[448,128]{1,0:T(8,128)S(1)}, u32[]{:S(2)}, u32[]{:S(2)}) collective-permute-start(f32[448,128]{1,0:T(8,128)S(1)} %get-tuple-element.46), channel_id=1, source_target_pairs={{1,2},{2,1},{5,6},{6,5},{9,10},{10,9},{13,14},{14,13},{17,18},{18,... | collective-permute-start | bytes 688136 | tf_op jit(solution)/shard_map/ppermute | solution.py:512
  28.2 5.2 %collective-permute-start.6 = (f32[448,128]{1,0:T(8,128)S(1)}, f32[448,128]{1,0:T(8,128)S(1)}, u32[]{:S(2)}, u32[]{:S(2)}) collective-permute-start(f32[448,128]{1,0:T(8,128)S(1)} %get-tuple-element.47), channel_id=1, source_target_pairs={{0,4},{4,0},{8,12},{12,8},{16,20},{20,16},{24,28},{28,24},{1,5},{5... | collective-permute-start | bytes 688136 | tf_op jit(solution)/shard_map/ppermute | solution.py:513
  28.2 7.9 %collective-permute-start.7 = (f32[448,128]{1,0:T(8,128)S(1)}, f32[448,128]{1,0:T(8,128)S(1)}, u32[]{:S(2)}, u32[]{:S(2)}) collective-permute-start(f32[448,128]{1,0:T(8,128)S(1)} %get-tuple-element.48), channel_id=1, source_target_pairs={{0,28},{4,8},{8,4},{12,16},{16,12},{20,24},{24,20},{28,0},{1,29},{... | collective-permute-start | bytes 688136 | tf_op jit(solution)/shard_map/ppermute | solution.py:514
  36.1 19.0 %slice-start = ((s8[6291456]{0:T(1024)(128)(4,1)}), s8[4194304]{0:T(1024)(128)(4,1)S(1)}, s32[]{:S(2)}) async-start(s8[6291456]{0:T(1024)(128)(4,1)} %bitcast.18), calls=%async_computation | async-start | bytes 8388608
  38.3 14.4 %copy-start.2 = (bf16[1,1,3,8,128,128]{5,4,3,2,1,0:T(8,128)(2,1)S(1)}, bf16[1,1,3,8,128,128]{5,4,3,2,1,0:T(8,128)(2,1)}, u32[]{:S(2)}) copy-start(bf16[1,1,3,8,128,128]{5,4,3,2,1,0:T(8,128)(2,1)} %param.13) | copy-start | bytes 2359300
  38.3 16.8 %slice-start.1 = ((s8[6291456]{0:T(1024)(128)(4,1)}), s8[2097152]{0:T(1024)(128)(4,1)S(1)}, s32[]{:S(2)}) async-start(s8[6291456]{0:T(1024)(128)(4,1)} %bitcast.18), calls=%async_computation.1 | async-start | bytes 4194304
  38.3 4.9 %collective-permute-start.10 = (f32[32,128]{1,0:T(8,128)S(1)}, f32[32,128]{1,0:T(8,128)S(1)}, u32[]{:S(2)}, u32[]{:S(2)}) collective-permute-start(f32[32,128]{1,0:T(8,128)S(1)} %get-tuple-element.49.refs_0_), channel_id=1, source_target_pairs={{0,3},{1,0},{2,1},{3,2},{4,7},{5,4},{6,5},{7,6},{8,11},{9,8},{10,9... | collective-permute-start | bytes 49160 | tf_op jit(solution)/shard_map/ppermute | solution.py:521
  39.2 4.6 %collective-permute-start.9 = (f32[32,128]{1,0:T(8,128)S(1)}, f32[32,128]{1,0:T(8,128)S(1)}, u32[]{:S(2)}, u32[]{:S(2)}) collective-permute-start(f32[32,128]{1,0:T(8,128)S(1)} %get-tuple-element.49.refs_0_), channel_id=1, source_target_pairs={{0,2},{1,3},{2,0},{3,1},{4,6},{5,7},{6,4},{7,5},{8,10},{9,11},{10,... | collective-permute-start | bytes 49160 | tf_op jit(solution)/shard_map/ppermute | solution.py:521
  41.3 5.5 %collective-permute-start.8 = (f32[32,128]{1,0:T(8,128)S(1)}, f32[32,128]{1,0:T(8,128)S(1)}, u32[]{:S(2)}, u32[]{:S(2)}) collective-permute-start(f32[32,128]{1,0:T(8,128)S(1)} %get-tuple-element.49.refs_0_), channel_id=1, source_target_pairs={{0,1},{1,2},{2,3},{3,0},{4,5},{5,6},{6,7},{7,4},{8,9},{9,10},{10,1... | collective-permute-start | bytes 49160 | tf_op jit(solution)/shard_map/ppermute | solution.py:521
  47.0 1.2 collective-permute-start.11
  48.3 5.8 %collective-permute-start.14 = (f32[32,128]{1,0:T(8,128)S(1)}, f32[32,128]{1,0:T(8,128)S(1)}, u32[]{:S(2)}, u32[]{:S(2)}) collective-permute-start(f32[32,128]{1,0:T(8,128)S(1)} %constant_dynamic-update-slice_fusion.refs_0_), channel_id=1, source_target_pairs={{0,24},{4,28},{8,16},{12,20},{16,8},{20,12},{24,0},{28,4},{1,25},{... | collective-permute-start | bytes 49160 | tf_op jit(solution)/shard_map/ppermute | solution.py:525
  49.7 4.4 %collective-permute-start.13 = (f32[32,128]{1,0:T(8,128)S(1)}, f32[32,128]{1,0:T(8,128)S(1)}, u32[]{:S(2)}, u32[]{:S(2)}) collective-permute-start(f32[32,128]{1,0:T(8,128)S(1)} %constant_dynamic-update-slice_fusion.refs_0_), channel_id=1, source_target_pairs={{0,16},{4,20},{8,24},{12,28},{16,0},{20,4},{24,8},{28,12},{1,17},{... | collective-permute-start | bytes 49160 | tf_op jit(solution)/shard_map/ppermute | solution.py:525
  51.4 3.7 %collective-permute-start.12 = (f32[32,128]{1,0:T(8,128)S(1)}, f32[32,128]{1,0:T(8,128)S(1)}, u32[]{:S(2)}, u32[]{:S(2)}) collective-permute-start(f32[32,128]{1,0:T(8,128)S(1)} %constant_dynamic-update-slice_fusion.refs_0_), channel_id=1, source_target_pairs={{0,8},{4,12},{8,0},{12,4},{16,24},{20,28},{24,16},{28,20},{1,9},{5... | collective-permute-start | bytes 49160 | tf_op jit(solution)/shard_map/ppermute | solution.py:525
  59.5 3.7 %collective-permute-start.17 = (f32[8,128]{1,0:T(8,128)S(1)}, f32[8,128]{1,0:T(8,128)S(1)}, u32[]{:S(2)}, u32[]{:S(2)}) collective-permute-start(f32[8,128]{1,0:T(8,128)S(1)} %get-tuple-element.56), channel_id=1, source_target_pairs={{0,3},{1,0},{2,1},{3,2},{4,7},{5,4},{6,5},{7,6},{8,11},{9,8},{10,9... | collective-permute-start | bytes 12296 | tf_op jit(solution)/shard_map/ppermute | solution.py:521
  59.7 4.5 %collective-permute-start.16 = (f32[8,128]{1,0:T(8,128)S(1)}, f32[8,128]{1,0:T(8,128)S(1)}, u32[]{:S(2)}, u32[]{:S(2)}) collective-permute-start(f32[8,128]{1,0:T(8,128)S(1)} %get-tuple-element.56), channel_id=1, source_target_pairs={{0,2},{1,3},{2,0},{3,1},{4,6},{5,7},{6,4},{7,5},{8,10},{9,11},{10,... | collective-permute-start | bytes 12296 | tf_op jit(solution)/shard_map/ppermute | solution.py:521
  60.7 5.4 %collective-permute-start.15 = (f32[8,128]{1,0:T(8,128)S(1)}, f32[8,128]{1,0:T(8,128)S(1)}, u32[]{:S(2)}, u32[]{:S(2)}) collective-permute-start(f32[8,128]{1,0:T(8,128)S(1)} %get-tuple-element.56), channel_id=1, source_target_pairs={{0,1},{1,2},{2,3},{3,0},{4,5},{5,6},{6,7},{7,4},{8,9},{9,10},{10,1... | collective-permute-start | bytes 12296 | tf_op jit(solution)/shard_map/ppermute | solution.py:521
  66.1 1.2 collective-permute-start.18
  67.3 4.5 %collective-permute-start.21 = (f32[8,128]{1,0:T(8,128)S(1)}, f32[8,128]{1,0:T(8,128)S(1)}, u32[]{:S(2)}, u32[]{:S(2)}) collective-permute-start(f32[8,128]{1,0:T(8,128)S(1)} %add.45), channel_id=1, source_target_pairs={{0,24},{4,28},{8,16},{12,20},{16,8},{20,12},{24,0},{28,4},{1,25},{... | collective-permute-start | bytes 12296 | tf_op jit(solution)/shard_map/ppermute | solution.py:525
  69.7 3.6 %collective-permute-start.20 = (f32[8,128]{1,0:T(8,128)S(1)}, f32[8,128]{1,0:T(8,128)S(1)}, u32[]{:S(2)}, u32[]{:S(2)}) collective-permute-start(f32[8,128]{1,0:T(8,128)S(1)} %add.45), channel_id=1, source_target_pairs={{0,16},{4,20},{8,24},{12,28},{16,0},{20,4},{24,8},{28,12},{1,17},{... | collective-permute-start | bytes 12296 | tf_op jit(solution)/shard_map/ppermute | solution.py:525
  69.8 4.6 %collective-permute-start.19 = (f32[8,128]{1,0:T(8,128)S(1)}, f32[8,128]{1,0:T(8,128)S(1)}, u32[]{:S(2)}, u32[]{:S(2)}) collective-permute-start(f32[8,128]{1,0:T(8,128)S(1)} %add.45), channel_id=1, source_target_pairs={{0,8},{4,12},{8,0},{12,4},{16,24},{20,28},{24,16},{28,20},{1,9},{5... | collective-permute-start | bytes 12296 | tf_op jit(solution)/shard_map/ppermute | solution.py:525
  70.8 6.1 %collective-permute-start.22 = (f32[384,128]{1,0:T(8,128)S(1)}, f32[384,128]{1,0:T(8,128)S(1)}, u32[]{:S(2)}, u32[]{:S(2)}) collective-permute-start(f32[384,128]{1,0:T(8,128)S(1)} %get-tuple-element.57), channel_id=1, source_target_pairs={{0,1},{1,0},{2,3},{3,2},{4,5},{5,4},{6,7},{7,6},{8,9},{9,8},{10,11... | collective-permute-start | bytes 589832 | tf_op jit(solution)/shard_map/ppermute | solution.py:511
  70.8 6.1 %collective-permute-start.23 = (f32[384,128]{1,0:T(8,128)S(1)}, f32[384,128]{1,0:T(8,128)S(1)}, u32[]{:S(2)}, u32[]{:S(2)}) collective-permute-start(f32[384,128]{1,0:T(8,128)S(1)} %get-tuple-element.58), channel_id=1, source_target_pairs={{1,2},{2,1},{5,6},{6,5},{9,10},{10,9},{13,14},{14,13},{17,18},{18,... | collective-permute-start | bytes 589832 | tf_op jit(solution)/shard_map/ppermute | solution.py:512
  71.8 5.1 %collective-permute-start.24 = (f32[384,128]{1,0:T(8,128)S(1)}, f32[384,128]{1,0:T(8,128)S(1)}, u32[]{:S(2)}, u32[]{:S(2)}) collective-permute-start(f32[384,128]{1,0:T(8,128)S(1)} %get-tuple-element.59), channel_id=1, source_target_pairs={{0,4},{4,0},{8,12},{12,8},{16,20},{20,16},{24,28},{28,24},{1,5},{5... | collective-permute-start | bytes 589832 | tf_op jit(solution)/shard_map/ppermute | solution.py:513
  73.3 7.4 %collective-permute-start.25 = (f32[384,128]{1,0:T(8,128)S(1)}, f32[384,128]{1,0:T(8,128)S(1)}, u32[]{:S(2)}, u32[]{:S(2)}) collective-permute-start(f32[384,128]{1,0:T(8,128)S(1)} %get-tuple-element.60), channel_id=1, source_target_pairs={{0,28},{4,8},{8,4},{12,16},{16,12},{20,24},{24,20},{28,0},{1,29},{... | collective-permute-start | bytes 589832 | tf_op jit(solution)/shard_map/ppermute | solution.py:514
  82.4 5.1 %collective-permute-start.28 = (f32[32,128]{1,0:T(8,128)S(1)}, f32[32,128]{1,0:T(8,128)S(1)}, u32[]{:S(2)}, u32[]{:S(2)}) collective-permute-start(f32[32,128]{1,0:T(8,128)S(1)} %get-tuple-element.61.refs_0_), channel_id=1, source_target_pairs={{0,3},{1,0},{2,1},{3,2},{4,7},{5,4},{6,5},{7,6},{8,11},{9,8},{10,9... | collective-permute-start | bytes 49160 | tf_op jit(solution)/shard_map/ppermute | solution.py:521
  83.7 4.9 %collective-permute-start.27 = (f32[32,128]{1,0:T(8,128)S(1)}, f32[32,128]{1,0:T(8,128)S(1)}, u32[]{:S(2)}, u32[]{:S(2)}) collective-permute-start(f32[32,128]{1,0:T(8,128)S(1)} %get-tuple-element.61.refs_0_), channel_id=1, source_target_pairs={{0,2},{1,3},{2,0},{3,1},{4,6},{5,7},{6,4},{7,5},{8,10},{9,11},{10,... | collective-permute-start | bytes 49160 | tf_op jit(solution)/shard_map/ppermute | solution.py:521
  86.5 5.5 %collective-permute-start.26 = (f32[32,128]{1,0:T(8,128)S(1)}, f32[32,128]{1,0:T(8,128)S(1)}, u32[]{:S(2)}, u32[]{:S(2)}) collective-permute-start(f32[32,128]{1,0:T(8,128)S(1)} %get-tuple-element.61.refs_0_), channel_id=1, source_target_pairs={{0,1},{1,2},{2,3},{3,0},{4,5},{5,6},{6,7},{7,4},{8,9},{9,10},{10,1... | collective-permute-start | bytes 49160 | tf_op jit(solution)/shard_map/ppermute | solution.py:521
  92.3 1.2 collective-permute-start.29
  93.5 4.8 %collective-permute-start.32 = (f32[32,128]{1,0:T(8,128)S(1)}, f32[32,128]{1,0:T(8,128)S(1)}, u32[]{:S(2)}, u32[]{:S(2)}) collective-permute-start(f32[32,128]{1,0:T(8,128)S(1)} %constant_dynamic-update-slice_fusion.2.refs_0_), channel_id=1, source_target_pairs={{0,24},{4,28},{8,16},{12,20},{16,8},{20,12},{24,0},{28,4},{1,25},{... | collective-permute-start | bytes 49160 | tf_op jit(solution)/shard_map/ppermute | solution.py:525
  94.7 3.7 %collective-permute-start.31 = (f32[32,128]{1,0:T(8,128)S(1)}, f32[32,128]{1,0:T(8,128)S(1)}, u32[]{:S(2)}, u32[]{:S(2)}) collective-permute-start(f32[32,128]{1,0:T(8,128)S(1)} %constant_dynamic-update-slice_fusion.2.refs_0_), channel_id=1, source_target_pairs={{0,16},{4,20},{8,24},{12,28},{16,0},{20,4},{24,8},{28,12},{1,17},{... | collective-permute-start | bytes 49160 | tf_op jit(solution)/shard_map/ppermute | solution.py:525
  94.7 4.0 %collective-permute-start.30 = (f32[32,128]{1,0:T(8,128)S(1)}, f32[32,128]{1,0:T(8,128)S(1)}, u32[]{:S(2)}, u32[]{:S(2)}) collective-permute-start(f32[32,128]{1,0:T(8,128)S(1)} %constant_dynamic-update-slice_fusion.2.refs_0_), channel_id=1, source_target_pairs={{0,8},{4,12},{8,0},{12,4},{16,24},{20,28},{24,16},{28,20},{1,9},{5... | collective-permute-start | bytes 49160 | tf_op jit(solution)/shard_map/ppermute | solution.py:525
  103.2 3.7 %collective-permute-start.35 = (f32[8,128]{1,0:T(8,128)S(1)}, f32[8,128]{1,0:T(8,128)S(1)}, u32[]{:S(2)}, u32[]{:S(2)}) collective-permute-start(f32[8,128]{1,0:T(8,128)S(1)} %get-tuple-element.69), channel_id=1, source_target_pairs={{0,3},{1,0},{2,1},{3,2},{4,7},{5,4},{6,5},{7,6},{8,11},{9,8},{10,9... | collective-permute-start | bytes 12296 | tf_op jit(solution)/shard_map/ppermute | solution.py:521
  103.5 4.5 %collective-permute-start.34 = (f32[8,128]{1,0:T(8,128)S(1)}, f32[8,128]{1,0:T(8,128)S(1)}, u32[]{:S(2)}, u32[]{:S(2)}) collective-permute-start(f32[8,128]{1,0:T(8,128)S(1)} %get-tuple-element.69), channel_id=1, source_target_pairs={{0,2},{1,3},{2,0},{3,1},{4,6},{5,7},{6,4},{7,5},{8,10},{9,11},{10,... | collective-permute-start | bytes 12296 | tf_op jit(solution)/shard_map/ppermute | solution.py:521
  104.6 5.4 %collective-permute-start.33 = (f32[8,128]{1,0:T(8,128)S(1)}, f32[8,128]{1,0:T(8,128)S(1)}, u32[]{:S(2)}, u32[]{:S(2)}) collective-permute-start(f32[8,128]{1,0:T(8,128)S(1)} %get-tuple-element.69), channel_id=1, source_target_pairs={{0,1},{1,2},{2,3},{3,0},{4,5},{5,6},{6,7},{7,4},{8,9},{9,10},{10,1... | collective-permute-start | bytes 12296 | tf_op jit(solution)/shard_map/ppermute | solution.py:521
  110.0 1.2 collective-permute-start.36
  111.2 4.5 %collective-permute-start.39 = (f32[8,128]{1,0:T(8,128)S(1)}, f32[8,128]{1,0:T(8,128)S(1)}, u32[]{:S(2)}, u32[]{:S(2)}) collective-permute-start(f32[8,128]{1,0:T(8,128)S(1)} %add.52), channel_id=1, source_target_pairs={{0,24},{4,28},{8,16},{12,20},{16,8},{20,12},{24,0},{28,4},{1,25},{... | collective-permute-start | bytes 12296 | tf_op jit(solution)/shard_map/ppermute | solution.py:525
  113.8 3.6 %collective-permute-start.38 = (f32[8,128]{1,0:T(8,128)S(1)}, f32[8,128]{1,0:T(8,128)S(1)}, u32[]{:S(2)}, u32[]{:S(2)}) collective-permute-start(f32[8,128]{1,0:T(8,128)S(1)} %add.52), channel_id=1, source_target_pairs={{0,16},{4,20},{8,24},{12,28},{16,0},{20,4},{24,8},{28,12},{1,17},{... | collective-permute-start | bytes 12296 | tf_op jit(solution)/shard_map/ppermute | solution.py:525
  114.0 4.5 %collective-permute-start.37 = (f32[8,128]{1,0:T(8,128)S(1)}, f32[8,128]{1,0:T(8,128)S(1)}, u32[]{:S(2)}, u32[]{:S(2)}) collective-permute-start(f32[8,128]{1,0:T(8,128)S(1)} %add.52), channel_id=1, source_target_pairs={{0,8},{4,12},{8,0},{12,4},{16,24},{20,28},{24,16},{28,20},{1,9},{5... | collective-permute-start | bytes 12296 | tf_op jit(solution)/shard_map/ppermute | solution.py:525
  114.7 4.6 %collective-permute-start.40 = (bf16[384,128]{1,0:T(8,128)(2,1)S(1)}, bf16[384,128]{1,0:T(8,128)(2,1)S(1)}, u32[]{:S(2)}, u32[]{:S(2)}) collective-permute-start(bf16[384,128]{1,0:T(8,128)(2,1)S(1)} %get-tuple-element.70), channel_id=1, source_target_pairs={{0,1},{1,0},{2,3},{3,2},{4,5},{5,4},{6,7},{7,6},{8,9},{9,8},{10,11... | collective-permute-start | bytes 294920 | tf_op jit(solution)/shard_map/ppermute | solution.py:511
  114.7 4.6 %collective-permute-start.41 = (bf16[384,128]{1,0:T(8,128)(2,1)S(1)}, bf16[384,128]{1,0:T(8,128)(2,1)S(1)}, u32[]{:S(2)}, u32[]{:S(2)}) collective-permute-start(bf16[384,128]{1,0:T(8,128)(2,1)S(1)} %get-tuple-element.71), channel_id=1, source_target_pairs={{1,2},{2,1},{5,6},{6,5},{9,10},{10,9},{13,14},{14,13},{17,18},{18,... | collective-permute-start | bytes 294920 | tf_op jit(solution)/shard_map/ppermute | solution.py:512
  115.7 3.6 %collective-permute-start.42 = (bf16[384,128]{1,0:T(8,128)(2,1)S(1)}, bf16[384,128]{1,0:T(8,128)(2,1)S(1)}, u32[]{:S(2)}, u32[]{:S(2)}) collective-permute-start(bf16[384,128]{1,0:T(8,128)(2,1)S(1)} %get-tuple-element.72), channel_id=1, source_target_pairs={{0,4},{4,0},{8,12},{12,8},{16,20},{20,16},{24,28},{28,24},{1,5},{5... | collective-permute-start | bytes 294920 | tf_op jit(solution)/shard_map/ppermute | solution.py:513
  117.4 5.5 %collective-permute-start.43 = (bf16[384,128]{1,0:T(8,128)(2,1)S(1)}, bf16[384,128]{1,0:T(8,128)(2,1)S(1)}, u32[]{:S(2)}, u32[]{:S(2)}) collective-permute-start(bf16[384,128]{1,0:T(8,128)(2,1)S(1)} %get-tuple-element.73), channel_id=1, source_target_pairs={{0,28},{4,8},{8,4},{12,16},{16,12},{20,24},{24,20},{28,0},{1,29},{... | collective-permute-start | bytes 294920 | tf_op jit(solution)/shard_map/ppermute | solution.py:514

commit v3 on v2

--- a/solution.py
+++ b/solution.py
@@ -8,6 +8,7 @@
 from jax.sharding import PartitionSpec as P
 
 precise = lax.Precision.HIGHEST
+COST = pl.CostEstimate(flops=1 << 30, bytes_accessed=0, transcendentals=0)
 F32 = jnp.float32
 BF16 = jnp.bfloat16
 VMEM = pl.BlockSpec(memory_space=pltpu.VMEM)
@@ -22,6 +23,7 @@
         out_shape=[jax.ShapeDtypeStruct(shape, dtype) for shape, dtype in outs],
         scratch_shapes=list(scratch),
         compiler_params=pltpu.CompilerParams(vmem_limit_bytes=16 * 1024 * 1024),
+        cost_estimate=COST,
     )(*scalars, *arrays)
 
 
@@ -103,26 +105,12 @@
     )
 
 
-def send_kernel(previous, deluxe, face_inverse, s0, s1, s2, s3, sems):
-    odd_n = lax.axis_index("narrow") % 2
-    odd_w = lax.axis_index("wide") % 2
-    slots, _, width, _ = previous.shape
-    copies = []
-    for send, face in ((s0, 1 - odd_n), (s1, odd_n), (s2, 3 - odd_w), (s3, 2 + odd_w)):
-        for part, source in enumerate((previous, deluxe, face_inverse)):
-            for slot in range(slots):
-                row = (part * slots + slot) * width
-                copies.append(
-                    pltpu.make_async_copy(
-                        source.at[slot, face],
-                        send.at[pl.ds(row, width)],
-                        sems.at[len(copies)],
-                    )
-                )
-    for copy in copies:
-        copy.start()
-    for copy in copies:
-        copy.wait()
+def send_kernel(*refs):
+    sources, sends = refs[:-4], refs[-4:]
+    slots = sources[0].shape[0]
+    for part, source in enumerate(sources):
+        for slot in range(slots):
+            send_faces(sends, part * slots + slot, [source[slot, face] for face in range(4)])
 
 
 def live_rows(count, size, slot, face, shape):
@@ -152,7 +140,7 @@
     pack.store((s0, s1, s2, s3), (weight, group, map_t, top))
     slots, faces, width, _ = previous.shape
 
-    def one_slot(slot, carry):
+    for slot in range(slots):
         for face in range(faces):
             other = partner[slot, face]
             mine = previous[slot, face].astype(F32)
@@ -170,31 +158,29 @@
             if face < 4:
                 sent.append(value)
         send_faces((s0, s1, s2, s3), slot, sent)
-        return carry
-
-    lax.fori_loop(0, slots, one_slot, 0)
 
 
 def scale_slot(slot, values, ids, deluxe, spread_weight, given, scaled, coarse_in):
     partner, count, size = ids
     rows = []
     faces = len(values)
-    slots, _, width, _ = deluxe.shape
+    _, _, width, _ = deluxe.shape
     for face, value in enumerate(values):
         half = value.astype(BF16)
         blocks = [deluxe[slot, face]]
         if face < 4:
             other = jnp.maximum(partner[slot, face], 0)
-            blocks.append(from_device(given, face, (slots + other) * width, width))
+            blocks.append(from_device(given, face, other * width, width))
         for side, block in enumerate(blocks):
             part = lax.dot_general(
                 block, half, (((0,), (0,)), ((), ())), preferred_element_type=F32
             )
             part = jnp.where(live_rows(count, size, slot, face, part.shape), part, 0.0)
             scaled[slot, face + side * faces] = part.astype(BF16)
-            if side == 0:
+            if side == 0 and coarse_in is not None:
                 rows.append(jnp.sum(spread_weight[slot, face] * part, axis=0, keepdims=True))
-    coarse_in[pl.ds(pl.multiple_of(slot * faces, 8), faces)] = jnp.concatenate(rows, axis=0)
+    if coarse_in is not None:
+        coarse_in[pl.ds(pl.multiple_of(slot * faces, 8), faces)] = jnp.concatenate(rows, axis=0)
 
 
 def restrict(coarse_map_t, coarse_in):
@@ -224,28 +210,38 @@
     restrict(coarse_map_t, coarse_in)
 
 
-def next_scale_kernel(partner, size, count, old_residual, image, sums, deluxe, spread_weight, coarse_map_t, *refs):
-    got, given = refs[:4], refs[4:8]
-    residual, full_image, scaled, coarse_in = refs[8:]
-    slots, faces = image.shape[:2]
-    totals = sums[...]
-    step = totals[0:1] / totals[1:2]
-
-    def one_slot(slot, carry):
-        values = []
-        for face in range(faces):
-            other = partner[slot, face]
-            theirs = from_face(image, got, jnp.maximum(other, 0), face).astype(F32)
-            full = image[slot, face] + jnp.where(other >= 0, theirs, 0.0)
-            full_image[slot, face] = full
-            value = old_residual[slot, face] - step * full
-            residual[slot, face] = value
-            values.append(value)
-        scale_slot(slot, values, (partner, count, size), deluxe, spread_weight, given, scaled, coarse_in)
-        return carry
-
-    lax.fori_loop(0, slots, one_slot, 0)
-    restrict(coarse_map_t, coarse_in)
+def make_next_scale_kernel(layout, halves):
+    def next_scale_kernel(partner, size, count, *refs):
+        pairs = refs[:halves]
+        old_residual, image, deluxe = refs[halves : halves + 3]
+        got, given = refs[halves + 3 : halves + 7], refs[halves + 7 : halves + 11]
+        residual, full_image, scaled, totals = refs[halves + 11 :]
+        slots, faces = image.shape[:2]
+        packed = pairs[0].shape[0] // 2
+        found = None
+        for rows in pairs:
+            for start in (layout.far_sums, packed + layout.far_sums):
+                part = rows[start : start + 8]
+                found = part if found is None else found + part
+        totals[...] = found
+        step = found[0:1] / found[1:2]
+
+        def one_slot(slot, carry):
+            values = []
+            for face in range(faces):
+                other = partner[slot, face]
+                theirs = from_face(image, got, jnp.maximum(other, 0), face).astype(F32)
+                full = image[slot, face] + jnp.where(other >= 0, theirs, 0.0)
+                full_image[slot, face] = full
+                value = old_residual[slot, face] - step * full
+                residual[slot, face] = value
+                values.append(value)
+            scale_slot(slot, values, (partner, count, size), deluxe, None, given, scaled, None)
+            return carry
+
+        lax.fori_loop(0, slots, one_slot, 0)
+
+    return next_scale_kernel
 
 
 def inverse_kernel(partner, scaled, face_inverse, g0, g1, g2, g3, local_part):
@@ -258,7 +254,7 @@
                 block = face_inverse[slot, face]
             else:
                 other = jnp.maximum(partner[slot, face - faces], 0)
-                block = from_device(given, face - faces, (2 * slots + other) * width, width)
+                block = from_device(given, face - faces, (slots + other) * width, width)
             local_part[slot, face] = jnp.dot(
                 block, scaled[slot, face], preferred_element_type=F32
             )
@@ -267,18 +263,32 @@
     lax.fori_loop(0, slots, one_slot, 0)
 
 
-def across_weight_kernel(pack, partner, g0, g1, g2, g3, spread):
-    got = (g0, g1, g2, g3)
-    slots, faces, width, columns = spread.shape
+def vector_kernel(pack, partner, size, count, deluxe, weight, *refs):
+    given, packs = refs[:4], refs[4:8]
+    spread, vectors = refs[8:]
+    slots, faces, width, columns = deluxe.shape
+    lanes = lax.broadcasted_iota(jnp.int32, (1, width), 1)
+
+    def vector(block, row, live):
+        row = jnp.where(lanes < live, row, 0.0)
+        value = jnp.sum(block.astype(F32) * row, axis=1, keepdims=True)
+        return jnp.broadcast_to(value, (width, columns))
+
     for face in range(faces):
-        rows = pack.read(got, face, 0)
+        rows = pack.read(packs, face, 0) if face < 4 else None
         for slot in range(slots):
-            other = partner[slot, face]
-            row = jnp.zeros((1, width), F32)
-            for place in range(slots):
-                number = place * (pack.sizes[0][0] // slots) + (face ^ 1)
-                row = jnp.where(other == place, rows[number : number + 1], row)
-            spread[slot, face] = jnp.broadcast_to(row, (columns, width)).T
+            live = jnp.where(slot < count[0, 0], size[slot, face], 0)
+            number = slot * faces + face
+            vectors[slot, face] = vector(deluxe[slot, face], weight[number : number + 1], live)
+            if face < 4:
+                other = partner[slot, face]
+                row = jnp.zeros((1, width), F32)
+                for place in range(slots):
+                    number = place * faces + (face ^ 1)
+                    row = jnp.where(other == place, rows[number : number + 1], row)
+                spread[slot, face] = jnp.broadcast_to(row, (columns, width)).T
+                block = from_device(given, face, jnp.maximum(other, 0) * width, width)
+                vectors[slot, faces + face] = vector(block, row, live)
 
 
 def make_group_kernel(pack, narrow, slots):
@@ -315,7 +325,62 @@
     return group_kernel
 
 
-def make_apply_kernel(pack, halves, later):
+class Layout:
+    def __init__(self, slots, faces, quotient, narrow):
+        self.each = slots * faces
+        self.beside = self.each
+        self.restricted = -(-(self.each + 4 * slots) // 8) * 8
+        self.sums = self.restricted + 3 * quotient
+        self.end = self.sums + 8
+        self.far_sums = 3 * quotient
+        self.far_group = self.far_sums + 8
+        self.far_beside = -(-(self.far_group + 2 * slots) // 8) * 8
+        self.far_end = -(-(self.far_beside + 2 * narrow * slots) // 8) * 8
+
+
+def make_next_group_kernel(pack, layout, narrow, slots):
+    def next_group_kernel(*refs):
+        rows_of = refs[:narrow]
+        coarse_group = refs[narrow]
+        got = refs[narrow + 1 : narrow + 5]
+        packed, group_part, group_vec = refs[narrow + 5 :]
+        each = layout.each
+        faces = each // slots
+        here = lax.axis_index("narrow")
+        packed[...] = jnp.zeros(packed.shape, F32)
+        carried = None
+        for back, rows in enumerate(rows_of):
+            place = (here + narrow - back) % narrow
+            group_vec[pl.ds(pl.multiple_of(place * each, 8), each)] = rows[:each]
+            part = rows[layout.restricted :]
+            carried = part if carried is None else carried + part
+        packed[: carried.shape[0]] = carried
+        for back, rows in enumerate(rows_of):
+            place = (here + narrow - back) % narrow
+            for slot in range(slots):
+                for face, shift in ((0, narrow - 1), (1, 1)):
+                    row = layout.beside + face * slots + slot
+                    target = (place + shift) % narrow * each + slot * faces + (face ^ 1)
+                    group_vec[pl.ds(target, 1)] += rows[row : row + 1]
+                for face in (2, 3):
+                    row = layout.beside + face * slots + slot
+                    target = layout.far_beside + ((face - 2) * narrow + place) * slots + slot
+                    packed[pl.ds(target, 1)] = rows[row : row + 1]
+        group = jnp.concatenate(
+            [coarse_group[...], pack.read(got, 0, 1), pack.read(got, 1, 1)], axis=0
+        )
+        part = exact(group, group_vec[...])
+        group_part[...] = part
+        for face in (2, 3):
+            for slot in range(slots):
+                row = layout.far_group + (face - 2) * slots + slot
+                number = slot * faces + face
+                packed[row : row + 1] = part[number : number + 1]
+
+    return next_group_kernel
+
+
+def make_apply_kernel(pack, layout, narrow, halves, later):
     def apply_kernel(partner, size, count, *refs):
         pairs = refs[:halves]
         refs = refs[halves:]
@@ -324,21 +389,34 @@
         residual, schur = refs[15:17]
         refs = refs[17:]
         if later:
-            old_direction, old_image = refs[:2]
-            refs = refs[2:]
-        direction, image, sums, s0, s1, s2, s3 = refs[:7]
-        weighted, everyone, every_pack, coarse_out, vec = refs[7:]
+            old_direction, old_image, coarse_group, totals, old_coarse = refs[:5]
+            direction, image, sums, s0, s1, s2, s3 = refs[5:12]
+            weighted, everyone, every_pack, coarse_out, vec, beside = refs[12:]
+        else:
+            vectors = refs[0]
+            direction, image, message, coarse_out, s0, s1, s2, s3 = refs[1:9]
+            weighted, everyone, every_pack, vec = refs[9:]
         slots, faces, width, columns = direction.shape
         quotient, each = map_t.shape
         here = lax.axis_index("wide")
         wide = 2 * halves
         packed = pairs[0].shape[0] // 2
+        far_group = layout.far_group if later else quotient
         for half, rows in enumerate(pairs):
             for other in range(2):
                 place = here ^ (2 * half + other)
-                block = rows[other * packed : (other + 1) * packed]
-                everyone[pl.ds(pl.multiple_of(place * quotient, 8), quotient)] = block[:quotient]
-                every_pack[pl.ds(pl.multiple_of(place * packed, 8), packed)] = block
+                every_pack[pl.ds(pl.multiple_of(place * packed, 8), packed)] = rows[
+                    other * packed : (other + 1) * packed
+                ]
+        for place in range(wide):
+            start = place * packed
+            value = every_pack[start : start + quotient]
+            if later:
+                above = (place + 1) % wide * packed + quotient
+                below = (place + wide - 1) % wide * packed + 2 * quotient
+                value = value + every_pack[above : above + quotient]
+                value = value + every_pack[below : below + quotient]
+            everyone[place * quotient : (place + 1) * quotient] = value
         tops = exact(
             jnp.concatenate(
                 [coarse_top[...], pack.read(packs, 2, 3), pack.read(packs, 3, 3)], axis=0
@@ -346,22 +424,49 @@
             everyone[...],
         )
         own_top = tops[:quotient]
-        coarse_out[:each] = group_part[:each] + exact_t(map_t[...], own_top)
+
+        def from_beside(shift, group):
+            beside[...] = jnp.zeros(beside.shape, F32)
+            for face, side in ((2, wide - 1), (3, 1)):
+                source = (here + shift + side) % wide * packed + layout.far_beside
+                source = source + (narrow * slots if face == 2 else 0)
+                for member in range(narrow):
+                    for slot in range(slots):
+                        target = member * each + slot * faces + face
+                        beside[target : target + 1] = every_pack[
+                            pl.ds(source + member * slots + slot, 1)
+                        ]
+            return exact(group, beside[...])
+
+        own_group = group_part[...]
+        if later:
+            group = jnp.concatenate(
+                [coarse_group[...], pack.read(packs, 0, 1), pack.read(packs, 1, 1)], axis=0
+            )
+            own_group = own_group + from_beside(0, group)
+        coarse_out[:each] = own_group[:each] + exact_t(map_t[...], own_top)
         for face in range(4):
             top = own_top if face < 2 else tops[(face - 1) * quotient : face * quotient]
             value = exact_t(pack.read(packs, face, 2), top)
             start = (face + 1) * each
             if face < 2:
-                value = value + group_part[start : start + each]
+                value = value + own_group[start : start + each]
+            elif later:
+                shift = wide - 1 if face == 2 else 1
+                value = value + from_beside(shift, pack.read(packs, face, 1))
             coarse_out[start : start + each] = value
+            if face >= 2:
+                side = (here + (wide - 1 if face == 2 else 1)) % wide
+                source = side * packed + far_group + (slots if face == 2 else 0)
+                for slot in range(slots):
+                    row = start + slot * faces + (face ^ 1)
+                    coarse_out[row : row + 1] += every_pack[pl.ds(source + slot, 1)]
+        if later:
+            step = totals[0:1] / totals[1:2]
+            coarse_out[...] = old_coarse[...] - step * coarse_out[...]
 
         def coarse_row(face, other):
-            row = coarse_out[pl.ds((face + 1) * each + other * faces + (face ^ 1), 1)]
-            if face < 2:
-                return row
-            side = here + wide - 1 if face == 2 else here + 1
-            start = (side % wide) * packed + quotient + (slots if face == 2 else 0)
-            return row + every_pack[pl.ds(start + other, 1)]
+            return coarse_out[pl.ds((face + 1) * each + other * faces + (face ^ 1), 1)]
 
         def weigh(part, weight, row, block, live):
             value = part + weight * row
@@ -386,7 +491,7 @@
                         local_part[slot, faces + face],
                         across_weight[slot, face],
                         coarse_row(face, place),
-                        from_device(given, face, (slots + place) * width, width),
+                        from_device(given, face, place * width, width),
                         live,
                     )
                     direction[slot, face] = jnp.where(other >= 0, theirs, 0.0)
@@ -405,13 +510,20 @@
                     theirs = weighted[jnp.maximum(other, 0), face ^ 1]
                     value = mine + jnp.where(other >= 0, theirs, 0.0)
                 direction[slot, face] = value
-                vec[face * width : (face + 1) * width] = value.astype(BF16)
+                half = value.astype(BF16)
+                rows = slice(face * width, (face + 1) * width)
+                vec[rows, :columns] = half
+                if later:
+                    vec[rows, columns:] = (value - half.astype(F32)).astype(BF16)
                 norm = norm + fold(residual[slot, face] * mine)
             products = multiply(schur, vec, slot, width)
             sent = []
             for face in range(faces):
-                live = live_rows(count, size, slot, face, products[face].shape)
-                value = jnp.where(live, products[face], 0.0)
+                live = live_rows(count, size, slot, face, (width, columns))
+                value = products[face]
+                if later:
+                    value = value[:, :columns] + value[:, columns:]
+                value = jnp.where(live, value, 0.0)
                 image[slot, face] = value
                 curve = curve + fold(direction[slot, face] * value)
                 if later:
@@ -428,7 +540,49 @@
         found = lax.fori_loop(0, slots, one_slot, (zero, zero, zero))
         rows = [jnp.sum(one, axis=0, keepdims=True) for one in found]
         rows.append(jnp.zeros((5, columns), F32))
-        sums[...] = jnp.concatenate(rows, axis=0)
+        local_sums = jnp.concatenate(rows, axis=0)
+        if later:
+            sums[...] = local_sums
+            return
+        message[...] = jnp.zeros(message.shape, F32)
+        message[layout.sums : layout.sums + 8] = local_sums
+
+        def coarse_slot(slot, carry):
+            rows = []
+            blocks = []
+            for face in range(faces):
+                other = partner[slot, face]
+                value = image[slot, face]
+                if face >= 4:
+                    theirs = image[jnp.maximum(other, 0), face ^ 1]
+                    value = value + jnp.where(other >= 0, theirs, 0.0)
+                rows.append(jnp.sum(vectors[slot, face] * value, axis=0, keepdims=True))
+                if face < 4:
+                    row = jnp.sum(vectors[slot, faces + face] * value, axis=0, keepdims=True)
+                    blocks += [jnp.where(other == place, row, 0.0) for place in range(slots)]
+            message[pl.ds(pl.multiple_of(slot * faces, 8), faces)] = jnp.concatenate(rows, axis=0)
+            return carry + jnp.concatenate(blocks, axis=0)
+
+        blocks = lax.fori_loop(0, slots, coarse_slot, jnp.zeros((4 * slots, columns), F32))
+        message[layout.beside : layout.beside + 4 * slots] = blocks
+        parts = [exact(map_t[...], message[:each])]
+        for face in range(4):
+            spread = []
+            for slot in range(slots):
+                before = face ^ 1
+                spread.append(jnp.zeros((before, columns), F32)) if before else None
+                row = face * slots + slot
+                spread.append(blocks[row : row + 1])
+                after = faces - 1 - before
+                spread.append(jnp.zeros((after, columns), F32))
+            value = exact(pack.read(packs, face, 2), jnp.concatenate(spread, axis=0))
+            if face < 2:
+                parts[0] = parts[0] + value
+            else:
+                parts.append(value)
+        message[layout.restricted : layout.restricted + 3 * quotient] = jnp.concatenate(
+            parts, axis=0
+        )
 
     return apply_kernel
 
@@ -524,63 +678,50 @@
     def across(rows, step):
         return lax.ppermute(rows, "wide", [(i, i ^ step) for i in range(wide)])
 
-    def total_and_swap(rows, sends):
-        rows = sum(of_group(rows))
-        got = swap(sends)
-        rows = rows + across(rows, 1)
-        rows = sum([rows] + [across(rows, step) for step in range(2, wide, 2)])
-        return rows, got
-
-    given = swap(
-        pl.pallas_call(
-            send_kernel,
-            name="send",
-            in_specs=[pl.BlockSpec(memory_space=pl.ANY)] * 3,
-            out_specs=[VMEM] * 4,
-            out_shape=[jax.ShapeDtypeStruct((3 * slots * width, columns), BF16)] * 4,
-            scratch_shapes=[pltpu.SemaphoreType.DMA((12 * slots,))],
-        )(previous, deluxe, face_inverse)
-    )
+    def spread_rows(rows):
+        pair = jnp.concatenate([rows, across(rows, 1)], axis=0)
+        return pair, [pair] + [across(pair, step) for step in range(2, wide, 2)]
+
+    def send(*sources):
+        rows = len(sources) * slots * width
+        return call(send_kernel, (), sources, [((rows, columns), BF16)] * 4)
+
+    got = swap(send(previous))
+    given = swap(send(deluxe, face_inverse))
     flat_weight = primal_weight[0, 0].reshape(each, width)
     spread_weight = jnp.broadcast_to(primal_weight[0, 0][..., None], shape)
     coarse_map_t = coarse_map.T
     ids = (partner, face_size, slot_count)
     vec = pltpu.VMEM((order, columns), BF16)
-    averaged, local, *sends = call(
+    run_start = functools.partial(
+        call,
         functools.partial(start_kernel, pack),
         ids,
         (previous, load_vector, schur_matrix, flat_weight, coarse_group, coarse_map_t, coarse_top)
-        + given,
+        + got,
         [(shape, F32), (shape, F32)] + [((pack.end, columns), F32)] * 4,
         [vec],
     )
+    averaged, local, *sends = run_start()
     wider = (slots, faces + 4, width, columns)
     scale_outs = [(wider, BF16), ((each + quotient, columns), F32)]
     packed_rows = -(-(quotient + 2 * slots) // 8) * 8
     packs = swap(sends)
-    (across_weight,) = call(
-        functools.partial(across_weight_kernel, pack),
-        (partner,),
-        packs,
-        [((slots, 4, width, columns), F32)],
-    )
-
-    def apply_to(later, scaled, coarse_in, more, send_type):
-        rows_of = of_group(coarse_in)
-        (local_part,) = call(
-            inverse_kernel, (partner,), (scaled, face_inverse) + given, [(wider, F32)]
-        )
-        packed, group_part = call(
-            make_group_kernel(pack, narrow, slots),
-            (),
-            (*rows_of, coarse_group) + packs,
-            [((packed_rows, columns), F32), ((3 * each, columns), F32)],
-            [pltpu.VMEM((narrow * each, columns), F32)],
-        )
-        pair = jnp.concatenate([packed, across(packed, 1)], axis=0)
-        pairs = [pair] + [across(pair, step) for step in range(2, wide, 2)]
+    layout = Layout(slots, faces, quotient, narrow)
+    across_weight, vectors = call(
+        functools.partial(vector_kernel, pack),
+        ids,
+        (deluxe, flat_weight) + given + packs,
+        [((slots, 4, width, columns), F32), (wider, F32)],
+    )
+
+    def invert(scaled):
+        return call(inverse_kernel, (partner,), (scaled, face_inverse) + given, [(wider, F32)])[0]
+
+    def apply_to(later, pairs, group_part, local_part, more, outs, send_type, scratch):
+        packed = pairs[0].shape[0] // 2
         return call(
-            make_apply_kernel(pack, wide // 2, later),
+            make_apply_kernel(pack, layout, narrow, wide // 2, later),
             ids,
             (
                 *pairs,
@@ -595,14 +736,13 @@
             + given
             + packs
             + more,
-            [(shape, F32), (shape, F32), ((8, columns), F32)] + [(one_face, send_type)] * 4,
+            [(shape, F32), (shape, F32)] + outs + [(one_face, send_type)] * 4,
             [
                 pltpu.VMEM(shape, F32),
                 pltpu.VMEM((wide * quotient, columns), F32),
-                pltpu.VMEM((wide * packed_rows, columns), F32),
-                pltpu.VMEM((5 * each, columns), F32),
-                vec,
-            ],
+                pltpu.VMEM((wide * packed, columns), F32),
+            ]
+            + scratch,
         )
 
     residual, scaled, coarse_in = call(
@@ -611,20 +751,61 @@
         (local, deluxe, spread_weight, coarse_map_t) + packs + given,
         [(shape, F32)] + scale_outs,
     )
-    direction, image, first_sums, *sends = apply_to(
-        False, scaled, coarse_in, (residual, schur_matrix), F32
-    )
-    first_sums, got = total_and_swap(first_sums, sends)
-    residual, full_image, scaled, coarse_in = call(
-        next_scale_kernel,
+    group_outs = [((3 * each, columns), F32)]
+    group_scratch = [pltpu.VMEM((narrow * each, columns), F32)]
+    packed, group_part = call(
+        make_group_kernel(pack, narrow, slots),
+        (),
+        (*of_group(coarse_in), coarse_group) + packs,
+        [((packed_rows, columns), F32)] + group_outs,
+        group_scratch,
+    )
+    pair, pairs = spread_rows(packed)
+    direction, image, message, coarse_out, *sends = apply_to(
+        False,
+        pairs,
+        group_part,
+        invert(scaled),
+        (residual, schur_matrix, vectors),
+        [((layout.end, columns), F32), ((5 * each, columns), F32)],
+        F32,
+        [vec],
+    )
+    rows_of = of_group(message)
+    got = swap(sends)
+    packed, group_part = call(
+        make_next_group_kernel(pack, layout, narrow, slots),
+        (),
+        (*rows_of, coarse_group) + packs,
+        [((layout.far_end, columns), F32)] + group_outs,
+        group_scratch,
+    )
+    pair = jnp.concatenate([packed, across(packed, 1)], axis=0)
+    pairs = [pair] + [across(pair, step) for step in range(2, wide, 2)]
+    residual, full_image, scaled, first_sums = call(
+        make_next_scale_kernel(layout, wide // 2),
         ids,
-        (residual, image, first_sums, deluxe, spread_weight, coarse_map_t) + got + given,
-        [(shape, F32), (shape, F32)] + scale_outs,
+        (*pairs, residual, image, deluxe) + got + given,
+        [(shape, F32), (shape, F32), (wider, BF16), ((8, columns), F32)],
     )
     precond, later_image, later_sums, *sends = apply_to(
-        True, scaled, coarse_in, (residual, schur_matrix, direction, image), BF16
-    )
-    later_sums, got = total_and_swap(later_sums, sends)
+        True,
+        pairs,
+        group_part,
+        invert(scaled),
+        (residual, schur_matrix, direction, image, coarse_group, first_sums, coarse_out),
+        [((8, columns), F32)],
+        BF16,
+        [
+            pltpu.VMEM((5 * each, columns), F32),
+            pltpu.VMEM((order, 2 * columns), BF16),
+            pltpu.VMEM((narrow * each, columns), F32),
+        ],
+    )
+    later_sums = sum(of_group(later_sums))
+    got = swap(sends)
+    later_sums = later_sums + across(later_sums, 1)
+    later_sums = sum([later_sums] + [across(later_sums, step) for step in range(2, wide, 2)])
     solution, residual = call(
         finish_kernel,
         (partner,),

time: 126 us -> 115 us (0.913)
  waiting for transfers between devices: 50.8 us -> 40.3 us
    ppermute x4 -> x5, waiting for transfers between devices: 9.98 us -> 0.87 us  [swap(): lax.ppermute(sends[0], 'narrow', narrow_near)]
    ppermute x12 -> x9, waiting for transfers between devices: 17.4 us -> 12.3 us  [of_group(): got.append(lax.ppermute(rows, 'narrow', ring))]
    ppermute x16 -> x12, waiting for transfers between devices: 9.9 us -> 14.1 us  [across(): return lax.ppermute(rows, 'wide', [(i, i ^ step) for i in range(wide)])]
    ppermute x16 -> x12, starting transfers between devices: 14.2 us -> 11.5 us  [across(): return lax.ppermute(rows, 'wide', [(i, i ^ step) for i in range(wide)])]
    pallas_call x1 -> x0, Pallas kernels: 2.63 us -> none  [body(): pl.pallas_call(send_kernel, name='send', in_specs=[pl.BlockSpec(memory_sp...]
    ppermute x4 -> x5, starting transfers between devices: 7.65 us -> 9.23 us  [swap(): lax.ppermute(sends[0], 'narrow', narrow_near)]
    pallas_call x11 -> x13, Pallas kernels: 22.5 us -> 23.9 us  [call(): pl.pallas_call(kernel, in_specs=[SMEM] * len(scalars) + [VMEM] * len(arra...]
    ppermute x4 -> x5, starting transfers between devices: 6.34 us -> 7.47 us  [swap(): lax.ppermute(sends[3], 'wide', wide_far)]
  transfers between devices with their start and end apart: 44 -> 41, of which waited for: 28 -> 19; matrix products, arithmetic and copies ran while one was open for 0% -> 0% of each run, Pallas kernels for 3% -> 5%
where the time goes in v3:
time: 115 us
  starting transfers between devices  44.9 us (39%)
  waiting for transfers between devices  40.3 us (35%)
  Pallas kernels  23.9 us (21%)
  local copies, waits for them, and re-layouts  3.93 us (3%)
  between operations  1.71 us (1%)
    pallas_call x13, Pallas kernels, call(): pl.pallas_call(kernel, in_specs=[SMEM] * len(scalars) + [VMEM] * len(arra...  23.9 us
    ppermute x12, waiting for transfers between devices, across(): return lax.ppermute(rows, 'wide', [(i, i ^ step) for i in range(wide)])  14.1 us
    ppermute x5, waiting for transfers between devices, swap(): lax.ppermute(sends[3], 'wide', wide_far)  13.1 us
    ppermute x9, starting transfers between devices, of_group(): got.append(lax.ppermute(rows, 'narrow', ring))  13 us
    ppermute x9, waiting for transfers between devices, of_group(): got.append(lax.ppermute(rows, 'narrow', ring))  12.3 us
    ppermute x12, starting transfers between devices, across(): return lax.ppermute(rows, 'wide', [(i, i ^ step) for i in range(wide)])  11.5 us
    ppermute x5, starting transfers between devices, swap(): lax.ppermute(sends[0], 'narrow', narrow_near)  9.23 us
    ppermute x5, starting transfers between devices, swap(): lax.ppermute(sends[3], 'wide', wide_far)  7.47 us
  transfers between devices with their start and end apart: 41, of which 19 were waited for; matrix products, arithmetic and copies ran while one was open for 0% of the time, Pallas kernels for 5%

profile of v3, /device:TPU:0, one launch (start us, length us, event | category | flops | bytes accessed | tf_op | source)
XLA Modules:
  0.0 114.9 jit_solution(15014101080654594633)
XLA Ops:
  0.6 1.1 copy-done.5
  1.9 3.1 %collective-permute-start = (bf16[384,128]{1,0:T(8,128)(2,1)S(1)}, bf16[384,128]{1,0:T(8,128)(2,1)S(1)}, u32[]{:S(2)}, u32[]{:S(2)}) collective-permute-start(bf16[384,128]{1,0:T(8,128)(2,1)S(1)} %get-tuple-element.46), channel_id=1, source_target_pairs={{0,1},{1,0},{2,3},{3,2},{4,5},{5,4},{6,7},{7,6},{8,9},{9,8},{10,11... | collective-permute-start | bytes 294920 | tf_op jit(solution)/shard_map/ppermute | solution.py:665
  5.0 0.7 collective-permute-start.1
  5.7 2.7 %collective-permute-start.3 = (bf16[384,128]{1,0:T(8,128)(2,1)S(1)}, bf16[384,128]{1,0:T(8,128)(2,1)S(1)}, u32[]{:S(2)}, u32[]{:S(2)}) collective-permute-start(bf16[384,128]{1,0:T(8,128)(2,1)S(1)} %get-tuple-element.49), channel_id=1, source_target_pairs={{0,28},{4,8},{8,4},{12,16},{16,12},{20,24},{24,20},{28,0},{1,29},{... | collective-permute-start | bytes 294920 | tf_op jit(solution)/shard_map/ppermute | solution.py:668
  8.4 1.1 copy-done.1
  9.5 1.1 copy-done.3
  10.9 4.5 %collective-permute-start.8 = (bf16[768,128]{1,0:T(8,128)(2,1)S(1)}, bf16[768,128]{1,0:T(8,128)(2,1)S(1)}, u32[]{:S(2)}, u32[]{:S(2)}) collective-permute-start(bf16[768,128]{1,0:T(8,128)(2,1)S(1)} %get-tuple-element.56), channel_id=1, source_target_pairs={{0,1},{1,0},{2,3},{3,2},{4,5},{5,4},{6,7},{7,6},{8,9},{9,8},{10,11... | collective-permute-start | bytes 589832 | tf_op jit(solution)/shard_map/ppermute | solution.py:665
  15.3 0.7 collective-permute-start.9
  16.9 2.8 %shard_map.132 = (f32[3,8,128,128]{3,2,1,0:T(8,128)S(1)}, f32[3,8,128,128]{3,2,1,0:T(8,128)S(1)}, f32[448,128]{1,0:T(8,128)S(1)}, f32[448,128]{1,0:T(8,128)S(1)}...) custom-call(s32[3,8]{1,0:T(4,128)S(1)} %get-tuple-element.91.partner, s32[3,8]{1,0:T(4,128)S(1)} %get-tuple-element.90.size, ...), custom_call_target="tpu_custom_call" | custom-call | flops 1073741824 | tf_op jit(solution)/shard_map/pallas_call | solution.py:19
  19.7 1.5 %collective-permute-start.4 = (f32[448,128]{1,0:T(8,128)S(1)}, f32[448,128]{1,0:T(8,128)S(1)}, u32[]{:S(2)}, u32[]{:S(2)}) collective-permute-start(f32[448,128]{1,0:T(8,128)S(1)} %get-tuple-element.52), channel_id=1, source_target_pairs={{0,1},{1,0},{2,3},{3,2},{4,5},{5,4},{6,7},{7,6},{8,9},{9,8},{10,11... | collective-permute-start | bytes 688136 | tf_op jit(solution)/shard_map/ppermute | solution.py:665
  21.2 0.7 collective-permute-start.5
  21.9 0.3 collective-permute-start.6
  22.2 0.5 collective-permute-start.7
  22.6 2.2 %collective-permute-start.11 = (bf16[768,128]{1,0:T(8,128)(2,1)S(1)}, bf16[768,128]{1,0:T(8,128)(2,1)S(1)}, u32[]{:S(2)}, u32[]{:S(2)}) collective-permute-start(bf16[768,128]{1,0:T(8,128)(2,1)S(1)} %get-tuple-element.59), channel_id=1, source_target_pairs={{0,28},{4,8},{8,4},{12,16},{16,12},{20,24},{24,20},{28,0},{1,29},{... | collective-permute-start | bytes 589832 | tf_op jit(solution)/shard_map/ppermute | solution.py:668
  24.8 10.0 %collective-permute-done.11.refs_7_.g3.refs_3_.refs_14_ = bf16[768,128]{1,0:T(8,128)(2,1)S(1)} collective-permute-done((bf16[768,128]{1,0:T(8,128)(2,1)S(1)}, bf16[768,128]{1,0:T(8,128)(2,1)S(1)}, u32[]{:S(2)}, u32[]{:S(2)}) %collective-permute-start.11) | collective-permute-done | bytes 196640 | tf_op jit(solution)/shard_map/ppermute | solution.py:668
  34.8 0.5 broadcast_in_dim.14.spread_weight.refs_8_
  35.3 1.7 %shard_map.134 = (f32[3,8,128,128]{3,2,1,0:T(8,128)S(1)}, bf16[3,12,128,128]{3,2,1,0:T(8,128)(2,1)S(1)}, f32[32,128]{1,0:T(8,128)S(1)}) custom-call(s32[3,8]{1,0:T(4,128)S(1)} %get-tuple-element.91.partner, s32[3,8]{1,0:T(4,128)S(1)} %get-tuple-element.90.size, s32[1,1]{1,0:T(1,128)S(6)} %copy.20.count, f32[3,8,128,128]{3,2,1,0:T(8,128)S(1)} %get-tuple-element.51.local, ...), custom_call_target="tpu_custom_call" | custom-call | flops 1073741824 | tf_op jit(solution)/shard_map/pallas_call | solution.py:19
  37.0 2.8 %collective-permute-start.14 = (f32[32,128]{1,0:T(8,128)S(1)}, f32[32,128]{1,0:T(8,128)S(1)}, u32[]{:S(2)}, u32[]{:S(2)}) collective-permute-start(f32[32,128]{1,0:T(8,128)S(1)} %get-tuple-element.60.refs_0_), channel_id=1, source_target_pairs={{0,3},{1,0},{2,1},{3,2},{4,7},{5,4},{6,5},{7,6},{8,11},{9,8},{10,9... | collective-permute-start | bytes 49160 | tf_op jit(solution)/shard_map/ppermute | solution.py:675
  39.8 2.0 %collective-permute-start.13 = (f32[32,128]{1,0:T(8,128)S(1)}, f32[32,128]{1,0:T(8,128)S(1)}, u32[]{:S(2)}, u32[]{:S(2)}) collective-permute-start(f32[32,128]{1,0:T(8,128)S(1)} %get-tuple-element.60.refs_0_), channel_id=1, source_target_pairs={{0,2},{1,3},{2,0},{3,1},{4,6},{5,7},{6,4},{7,5},{8,10},{9,11},{10,... | collective-permute-start | bytes 49160 | tf_op jit(solution)/shard_map/ppermute | solution.py:675
  41.8 0.5 collective-permute-start.12
  42.2 1.5 %shard_map.137 = (f32[3,4,128,128]{3,2,1,0:T(8,128)S(1)}, f32[3,12,128,128]{3,2,1,0:T(8,128)S(1)}) custom-call(s32[3,8]{1,0:T(4,128)S(1)} %get-tuple-element.91.partner, s32[3,8]{1,0:T(4,128)S(1)} %get-tuple-element.90.size, s32[1,1]{1,0:T(1,128)S(6)} %copy.20.count, bf16[3,8,128,128]{3,2,1,0:T(8,128)(2,1)S(1)} %bitcast.22, f32[24,128]{1,0:T(8,128)S(1)} %bitcast.38, ...), custom_call_target="tpu_custom_call" | custom-call | flops 1073741824 | tf_op jit(solution)/shard_map/pallas_call | solution.py:19
  43.8 0.8 collective-permute-done.13.refs_2_
  44.6 2.7 %collective-permute-done.12.refs_1_ = f32[32,128]{1,0:T(8,128)S(1)} collective-permute-done((f32[32,128]{1,0:T(8,128)S(1)}, f32[32,128]{1,0:T(8,128)S(1)}, u32[]{:S(2)}, u32[]{:S(2)}) %collective-permute-start.12) | collective-permute-done | bytes 16416 | tf_op jit(solution)/shard_map/ppermute | solution.py:675
  47.3 0.2 shard_map.135
  47.6 1.1 collective-permute-done.15
  48.8 0.5 collective-permute-start.17
  49.3 3.0 %collective-permute-start.16 = (f32[32,128]{1,0:T(8,128)S(1)}, f32[32,128]{1,0:T(8,128)S(1)}, u32[]{:S(2)}, u32[]{:S(2)}) collective-permute-start(f32[32,128]{1,0:T(8,128)S(1)} %constant_dynamic-update-slice_fusion.refs_0_), channel_id=1, source_target_pairs={{0,8},{4,12},{8,0},{12,4},{16,24},{20,28},{24,16},{28,20},{1,9},{5... | collective-permute-start | bytes 49160 | tf_op jit(solution)/shard_map/ppermute | solution.py:679
  52.3 1.4 %shard_map.136.refs_7_ = f32[3,12,128,128]{3,2,1,0:T(8,128)S(1)} custom-call(s32[3,8]{1,0:T(4,128)S(1)} %get-tuple-element.91.partner, bf16[3,12,128,128]{3,2,1,0:T(8,128)(2,1)S(1)} %get-tuple-element.63.scaled, bf16[3,8,128,128]{3,2,1,0:T(8,128)(2,1)S(1)} %bitcast.27, bf16[768,128]{1,0:T(8,128)(2,1)S(1)} %collective-permute-done.8.refs_4_.g0.refs_0_.refs_11_, ...), custom_call_target="tpu_custom_call" | custom-call | flops 1073741824 | tf_op jit(solution)/shard_map/pallas_call | solution.py:19
  53.6 0.3 collective-permute-done.16.refs_1_
  54.0 4.9 %shard_map.138 = (f32[3,8,128,128]{3,2,1,0:T(8,128)S(1)}, f32[3,8,128,128]{3,2,1,0:T(8,128)S(1)}, f32[72,128]{1,0:T(8,128)S(1)}, f32[120,128]{1,0:T(8,128)S(1)},...) custom-call(s32[3,8]{1,0:T(4,128)S(1)} %get-tuple-element.91.partner, ...), custom_call_target="tpu_custom_call" | custom-call | flops 1073741824 | tf_op jit(solution)/shard_map/pallas_call | solution.py:19
  58.9 0.2 collective-permute-start.20
  59.1 1.9 %collective-permute-start.19 = (f32[72,128]{1,0:T(8,128)S(1)}, f32[72,128]{1,0:T(8,128)S(1)}, u32[]{:S(2)}, u32[]{:S(2)}) collective-permute-start(f32[72,128]{1,0:T(8,128)S(1)} %get-tuple-element.68.refs_0_), channel_id=1, source_target_pairs={{0,1},{1,2},{2,3},{3,0},{4,5},{5,6},{6,7},{7,4},{8,9},{9,10},{10,1... | collective-permute-start | bytes 110600 | tf_op jit(solution)/shard_map/ppermute | solution.py:675
  61.0 1.9 %collective-permute-done.21.refs_3_ = f32[72,128]{1,0:T(8,128)S(1)} collective-permute-done((f32[72,128]{1,0:T(8,128)S(1)}, f32[72,128]{1,0:T(8,128)S(1)}, u32[]{:S(2)}, u32[]{:S(2)}) %collective-permute-start.21) | collective-permute-done | bytes 36896 | tf_op jit(solution)/shard_map/ppermute | solution.py:675
  62.9 0.9 collective-permute-done.20.refs_2_
  63.9 1.8 %collective-permute-done.19.refs_1_ = f32[72,128]{1,0:T(8,128)S(1)} collective-permute-done((f32[72,128]{1,0:T(8,128)S(1)}, f32[72,128]{1,0:T(8,128)S(1)}, u32[]{:S(2)}, u32[]{:S(2)}) %collective-permute-start.19) | collective-permute-done | bytes 36896 | tf_op jit(solution)/shard_map/ppermute | solution.py:675
  65.7 0.3 shard_map.139
  66.1 1.2 %collective-permute-done.22 = f32[64,128]{1,0:T(8,128)S(1)} collective-permute-done((f32[64,128]{1,0:T(8,128)S(1)}, f32[64,128]{1,0:T(8,128)S(1)}, u32[]{:S(2)}, u32[]{:S(2)}) %collective-permute-start.22) | collective-permute-done | bytes 32800 | tf_op jit(solution)/shard_map/ppermute | solution.py:679
  67.2 1.9 %collective-permute-start.25 = (f32[128,128]{1,0:T(8,128)S(1)}, f32[128,128]{1,0:T(8,128)S(1)}, u32[]{:S(2)}, u32[]{:S(2)}) collective-permute-start(f32[128,128]{1,0:T(8,128)S(1)} %constant_dynamic-update-slice_fusion.2.refs_0_), channel_id=1, source_target_pairs={{0,24},{4,28},{8,16},{12,20},{16,8},{20,12},{24,0},{28,4},{1,25},{... | collective-permute-start | bytes 196616 | tf_op jit(solution)/shard_map/ppermute | solution.py:679
  69.3 0.7 collective-permute-start.27
  70.1 1.1 collective-permute-start.29
  71.2 1.2 %collective-permute-done.25.refs_3_ = f32[128,128]{1,0:T(8,128)S(1)} collective-permute-done((f32[128,128]{1,0:T(8,128)S(1)}, f32[128,128]{1,0:T(8,128)S(1)}, u32[]{:S(2)}, u32[]{:S(2)}) %collective-permute-start.25) | collective-permute-done | bytes 65568 | tf_op jit(solution)/shard_map/ppermute | solution.py:679
  72.4 0.7 collective-permute-start.24
  73.1 4.4 %collective-permute-done.24.refs_2_ = f32[128,128]{1,0:T(8,128)S(1)} collective-permute-done((f32[128,128]{1,0:T(8,128)S(1)}, f32[128,128]{1,0:T(8,128)S(1)}, u32[]{:S(2)}, u32[]{:S(2)}) %collective-permute-start.24) | collective-permute-done | bytes 65568 | tf_op jit(solution)/shard_map/ppermute | solution.py:679
  77.5 1.7 %collective-permute-start.23 = (f32[128,128]{1,0:T(8,128)S(1)}, f32[128,128]{1,0:T(8,128)S(1)}, u32[]{:S(2)}, u32[]{:S(2)}) collective-permute-start(f32[128,128]{1,0:T(8,128)S(1)} %constant_dynamic-update-slice_fusion.2.refs_0_), channel_id=1, source_target_pairs={{0,8},{4,12},{8,0},{12,4},{16,24},{20,28},{24,16},{28,20},{1,9},{5... | collective-permute-start | bytes 196616 | tf_op jit(solution)/shard_map/ppermute | solution.py:679
  79.2 2.6 %collective-permute-done.23.refs_1_ = f32[128,128]{1,0:T(8,128)S(1)} collective-permute-done((f32[128,128]{1,0:T(8,128)S(1)}, f32[128,128]{1,0:T(8,128)S(1)}, u32[]{:S(2)}, u32[]{:S(2)}) %collective-permute-start.23) | collective-permute-done | bytes 65568 | tf_op jit(solution)/shard_map/ppermute | solution.py:679
  81.8 1.6 %shard_map.140 = (f32[3,8,128,128]{3,2,1,0:T(8,128)S(1)}, f32[3,8,128,128]{3,2,1,0:T(8,128)S(1)}, bf16[3,12,128,128]{3,2,1,0:T(8,128)(2,1)S(1)}, f32[8,128]{1,0:T(8,128)S(1)}) custom-call(s32[3,8]{1,0:T(4,128)S(1)} %get-tuple-element.91.partner, s32[3,8]{1,0:T(4,128)S(1)} %get-tuple-element.90.size, s32[1,1]{1,0:T(1,128)S(6)} %copy.20.count, ...), custom_call_target="tpu_custom_call" | custom-call | flops 1073741824 | tf_op jit(solution)/shard_map/pallas_call | solution.py:19
  83.4 1.3 %shard_map.141.refs_7_ = f32[3,12,128,128]{3,2,1,0:T(8,128)S(1)} custom-call(s32[3,8]{1,0:T(4,128)S(1)} %get-tuple-element.91.partner, bf16[3,12,128,128]{3,2,1,0:T(8,128)(2,1)S(1)} %get-tuple-element.76.scaled, bf16[3,8,128,128]{3,2,1,0:T(8,128)(2,1)S(1)} %bitcast.28, bf16[768,128]{1,0:T(8,128)(2,1)S(1)} %collective-permute-done.8.refs_4_.g0.refs_0_.refs_11_, ...), custom_call_target="tpu_custom_call" | custom-call | flops 1073741824 | tf_op jit(solution)/shard_map/pallas_call | solution.py:19
  84.7 4.9 %shard_map.142 = (f32[3,8,128,128]{3,2,1,0:T(8,128)S(1)}, f32[3,8,128,128]{3,2,1,0:T(8,128)S(1)}, f32[8,128]{1,0:T(8,128)S(1)}, bf16[384,128]{1,0:T(8,128)(2,1)S...) custom-call(s32[3,8]{1,0:T(4,128)S(1)} %get-tuple-element.91.partner, ...), custom_call_target="tpu_custom_call" | custom-call | flops 1073741824 | tf_op jit(solution)/shard_map/pallas_call | solution.py:19
  89.6 1.5 %collective-permute-start.32 = (f32[8,128]{1,0:T(8,128)S(1)}, f32[8,128]{1,0:T(8,128)S(1)}, u32[]{:S(2)}, u32[]{:S(2)}) collective-permute-start(f32[8,128]{1,0:T(8,128)S(1)} %get-tuple-element.83), channel_id=1, source_target_pairs={{0,3},{1,0},{2,1},{3,2},{4,7},{5,4},{6,5},{7,6},{8,11},{9,8},{10,9... | collective-permute-start | bytes 12296 | tf_op jit(solution)/shard_map/ppermute | solution.py:675
  91.1 2.9 %collective-permute-start.31 = (f32[8,128]{1,0:T(8,128)S(1)}, f32[8,128]{1,0:T(8,128)S(1)}, u32[]{:S(2)}, u32[]{:S(2)}) collective-permute-start(f32[8,128]{1,0:T(8,128)S(1)} %get-tuple-element.83), channel_id=1, source_target_pairs={{0,2},{1,3},{2,0},{3,1},{4,6},{5,7},{6,4},{7,5},{8,10},{9,11},{10,... | collective-permute-start | bytes 12296 | tf_op jit(solution)/shard_map/ppermute | solution.py:675
  94.0 1.3 %collective-permute-start.30 = (f32[8,128]{1,0:T(8,128)S(1)}, f32[8,128]{1,0:T(8,128)S(1)}, u32[]{:S(2)}, u32[]{:S(2)}) collective-permute-start(f32[8,128]{1,0:T(8,128)S(1)} %get-tuple-element.83), channel_id=1, source_target_pairs={{0,1},{1,2},{2,3},{3,0},{4,5},{5,6},{6,7},{7,4},{8,9},{9,10},{10,1... | collective-permute-start | bytes 12296 | tf_op jit(solution)/shard_map/ppermute | solution.py:675
  95.3 0.3 collective-permute-done.31
  95.6 3.8 %collective-permute-done.30 = f32[8,128]{1,0:T(8,128)S(1)} collective-permute-done((f32[8,128]{1,0:T(8,128)S(1)}, f32[8,128]{1,0:T(8,128)S(1)}, u32[]{:S(2)}, u32[]{:S(2)}) %collective-permute-start.30) | collective-permute-done | bytes 4128 | tf_op jit(solution)/shard_map/ppermute | solution.py:675
  99.4 1.2 %collective-permute-done.33 = f32[8,128]{1,0:T(8,128)S(1)} collective-permute-done((f32[8,128]{1,0:T(8,128)S(1)}, f32[8,128]{1,0:T(8,128)S(1)}, u32[]{:S(2)}, u32[]{:S(2)}) %collective-permute-start.33) | collective-permute-done | bytes 4128 | tf_op jit(solution)/shard_map/ppermute | solution.py:679
  100.6 2.6 %collective-permute-start.36 = (f32[8,128]{1,0:T(8,128)S(1)}, f32[8,128]{1,0:T(8,128)S(1)}, u32[]{:S(2)}, u32[]{:S(2)}) collective-permute-start(f32[8,128]{1,0:T(8,128)S(1)} %add.24), channel_id=1, source_target_pairs={{0,24},{4,28},{8,16},{12,20},{16,8},{20,12},{24,0},{28,4},{1,25},{... | collective-permute-start | bytes 12296 | tf_op jit(solution)/shard_map/ppermute | solution.py:679
  103.2 0.6 collective-permute-start.35
  103.8 0.2 collective-permute-start.34
  104.1 0.7 collective-permute-start.38
  104.8 0.3 collective-permute-done.36
  105.1 1.7 %collective-permute-done.35 = f32[8,128]{1,0:T(8,128)S(1)} collective-permute-done((f32[8,128]{1,0:T(8,128)S(1)}, f32[8,128]{1,0:T(8,128)S(1)}, u32[]{:S(2)}, u32[]{:S(2)}) %collective-permute-start.35) | collective-permute-done | bytes 4128 | tf_op jit(solution)/shard_map/ppermute | solution.py:679
  106.8 1.0 collective-permute-start.40
  107.9 0.9 collective-permute-done.37.g0
  108.7 3.0 %collective-permute-done.40.g3 = bf16[384,128]{1,0:T(8,128)(2,1)S(1)} collective-permute-done((bf16[384,128]{1,0:T(8,128)(2,1)S(1)}, bf16[384,128]{1,0:T(8,128)(2,1)S(1)}, u32[]{:S(2)}, u32[]{:S(2)}) %collective-permute-start.40) | collective-permute-done | bytes 98336 | tf_op jit(solution)/shard_map/ppermute | solution.py:668
  111.8 3.1 %shard_map.143 = (f32[3,8,128,128]{3,2,1,0:T(8,128)}, f32[3,8,128,128]{3,2,1,0:T(8,128)}) custom-call(s32[3,8]{1,0:T(4,128)S(1)} %get-tuple-element.91.partner, f32[3,8,128,128]{3,2,1,0:T(8,128)S(1)} %get-tuple-element.50.averaged, f32[3,8,128,128]{3,2,1,0:T(8,128)S(1)} %get-tuple-element.67.refs_21_.direction, ...), custom_call_target="tpu_custom_call" | custom-call | flops 1073741824 | tf_op jit(solution)/shard_map/pallas_call | solution.py:19
  (68 shorter events, 0.9 us)
Async XLA Ops:
  0.6 1.1 copy-start.5
  1.8 15.0 %copy-start = (bf16[1,1,3,1024,1024]{4,3,2,1,0:T(8,128)(2,1)S(1)}, bf16[1,1,3,1024,1024]{4,3,2,1,0:T(8,128)(2,1)}, u32[]{:S(2)}) copy-start(bf16[1,1,3,1024,1024]{4,3,2,1,0:T(8,128)(2,1)} %param.12) | copy-start | bytes 18874372
  1.9 13.5 %collective-permute-start = (bf16[384,128]{1,0:T(8,128)(2,1)S(1)}, bf16[384,128]{1,0:T(8,128)(2,1)S(1)}, u32[]{:S(2)}, u32[]{:S(2)}) collective-permute-start(bf16[384,128]{1,0:T(8,128)(2,1)S(1)} %get-tuple-element.46), channel_id=1, source_target_pairs={{0,1},{1,0},{2,3},{3,2},{4,5},{5,4},{6,7},{7,6},{8,9},{9,8},{10,11... | collective-permute-start | bytes 294920 | tf_op jit(solution)/shard_map/ppermute | solution.py:665
  5.0 11.0 %collective-permute-start.1 = (bf16[384,128]{1,0:T(8,128)(2,1)S(1)}, bf16[384,128]{1,0:T(8,128)(2,1)S(1)}, u32[]{:S(2)}, u32[]{:S(2)}) collective-permute-start(bf16[384,128]{1,0:T(8,128)(2,1)S(1)} %get-tuple-element.47), channel_id=1, source_target_pairs={{1,2},{2,1},{5,6},{6,5},{9,10},{10,9},{13,14},{14,13},{17,18},{18,... | collective-permute-start | bytes 294920 | tf_op jit(solution)/shard_map/ppermute | solution.py:666
  5.6 11.1 %collective-permute-start.2 = (bf16[384,128]{1,0:T(8,128)(2,1)S(1)}, bf16[384,128]{1,0:T(8,128)(2,1)S(1)}, u32[]{:S(2)}, u32[]{:S(2)}) collective-permute-start(bf16[384,128]{1,0:T(8,128)(2,1)S(1)} %get-tuple-element.48), channel_id=1, source_target_pairs={{0,4},{4,0},{8,12},{12,8},{16,20},{20,16},{24,28},{28,24},{1,5},{5... | collective-permute-start | bytes 294920 | tf_op jit(solution)/shard_map/ppermute | solution.py:667
  5.7 11.1 %collective-permute-start.3 = (bf16[384,128]{1,0:T(8,128)(2,1)S(1)}, bf16[384,128]{1,0:T(8,128)(2,1)S(1)}, u32[]{:S(2)}, u32[]{:S(2)}) collective-permute-start(bf16[384,128]{1,0:T(8,128)(2,1)S(1)} %get-tuple-element.49), channel_id=1, source_target_pairs={{0,28},{4,8},{8,4},{12,16},{16,12},{20,24},{24,20},{28,0},{1,29},{... | collective-permute-start | bytes 294920 | tf_op jit(solution)/shard_map/ppermute | solution.py:668
  8.4 1.1 copy-start.1
  9.5 1.1 copy-start.3
  10.7 5.4 %copy-start.12 = (s32[1,1,3,8]{3,1,2,0:T(1,128)S(1)}, s32[1,1,3,8]{3,1,2,0:T(1,128)}, u32[]{:S(2)}) copy-start(s32[1,1,3,8]{3,1,2,0:T(1,128)} %param.23) | copy-start | bytes 292
  10.7 5.4 %copy-start.13 = (s32[1,1,3,8]{3,1,2,0:T(1,128)S(1)}, s32[1,1,3,8]{3,1,2,0:T(1,128)}, u32[]{:S(2)}) copy-start(s32[1,1,3,8]{3,1,2,0:T(1,128)} %param.22) | copy-start | bytes 292
  10.7 6.1 %copy-start.6 = (bf16[1,1,3,8,128,128]{5,4,3,2,1,0:T(8,128)(2,1)S(1)}, bf16[1,1,3,8,128,128]{5,4,3,2,1,0:T(8,128)(2,1)}, u32[]{:S(2)}) copy-start(bf16[1,1,3,8,128,128]{5,4,3,2,1,0:T(8,128)(2,1)} %param.20) | copy-start | bytes 2359300
  10.7 6.2 %copy-start.7 = (bf16[1,1,3,8,128,128]{5,4,3,2,1,0:T(8,128)(2,1)S(1)}, bf16[1,1,3,8,128,128]{5,4,3,2,1,0:T(8,128)(2,1)}, u32[]{:S(2)}) copy-start(bf16[1,1,3,8,128,128]{5,4,3,2,1,0:T(8,128)(2,1)} %param.19) | copy-start | bytes 2359300
  10.7 6.2 %copy-start.8 = (f32[1,24,8]{1,2,0:T(8,128)S(1)}, f32[1,24,8]{1,2,0:T(8,128)}, u32[]{:S(2)}) copy-start(f32[1,24,8]{1,2,0:T(8,128)} %param.17) | copy-start | bytes 2308
  10.7 6.2 %copy-start.9 = (f32[1,1,3,8,128]{4,3,2,1,0:T(8,128)S(1)}, f32[1,1,3,8,128]{4,3,2,1,0:T(8,128)}, u32[]{:S(2)}) copy-start(f32[1,1,3,8,128]{4,3,2,1,0:T(8,128)} %param.15) | copy-start | bytes 36868
  10.7 6.2 %copy-start.10 = (f32[1,24,96]{2,1,0:T(8,128)S(1)}, f32[1,24,96]{2,1,0:T(8,128)}, u32[]{:S(2)}) copy-start(f32[1,24,96]{2,1,0:T(8,128)} %param.16) | copy-start | bytes 27652
  10.7 6.2 %copy-start.11 = (f32[8,64]{1,0:T(8,128)S(1)}, f32[8,64]{1,0:T(8,128)}, u32[]{:S(2)}) copy-start(f32[8,64]{1,0:T(8,128)} %refs_6_.3) | copy-start | bytes 6148
  10.9 11.0 %collective-permute-start.8 = (bf16[768,128]{1,0:T(8,128)(2,1)S(1)}, bf16[768,128]{1,0:T(8,128)(2,1)S(1)}, u32[]{:S(2)}, u32[]{:S(2)}) collective-permute-start(bf16[768,128]{1,0:T(8,128)(2,1)S(1)} %get-tuple-element.56), channel_id=1, source_target_pairs={{0,1},{1,0},{2,3},{3,2},{4,5},{5,4},{6,7},{7,6},{8,9},{9,8},{10,11... | collective-permute-start | bytes 589832 | tf_op jit(solution)/shard_map/ppermute | solution.py:665
  15.3 6.8 %collective-permute-start.9 = (bf16[768,128]{1,0:T(8,128)(2,1)S(1)}, bf16[768,128]{1,0:T(8,128)(2,1)S(1)}, u32[]{:S(2)}, u32[]{:S(2)}) collective-permute-start(bf16[768,128]{1,0:T(8,128)(2,1)S(1)} %get-tuple-element.57), channel_id=1, source_target_pairs={{1,2},{2,1},{5,6},{6,5},{9,10},{10,9},{13,14},{14,13},{17,18},{18,... | collective-permute-start | bytes 589832 | tf_op jit(solution)/shard_map/ppermute | solution.py:666
  16.0 6.6 %collective-permute-start.10 = (bf16[768,128]{1,0:T(8,128)(2,1)S(1)}, bf16[768,128]{1,0:T(8,128)(2,1)S(1)}, u32[]{:S(2)}, u32[]{:S(2)}) collective-permute-start(bf16[768,128]{1,0:T(8,128)(2,1)S(1)} %get-tuple-element.58), channel_id=1, source_target_pairs={{0,4},{4,0},{8,12},{12,8},{16,20},{20,16},{24,28},{28,24},{1,5},{5... | collective-permute-start | bytes 589832 | tf_op jit(solution)/shard_map/ppermute | solution.py:667
  19.7 15.6 %copy-start.2 = (bf16[1,1,3,8,128,128]{5,4,3,2,1,0:T(8,128)(2,1)S(1)}, bf16[1,1,3,8,128,128]{5,4,3,2,1,0:T(8,128)(2,1)}, u32[]{:S(2)}) copy-start(bf16[1,1,3,8,128,128]{5,4,3,2,1,0:T(8,128)(2,1)} %param.14) | copy-start | bytes 2359300
  19.7 15.1 %collective-permute-start.4 = (f32[448,128]{1,0:T(8,128)S(1)}, f32[448,128]{1,0:T(8,128)S(1)}, u32[]{:S(2)}, u32[]{:S(2)}) collective-permute-start(f32[448,128]{1,0:T(8,128)S(1)} %get-tuple-element.52), channel_id=1, source_target_pairs={{0,1},{1,0},{2,3},{3,2},{4,5},{5,4},{6,7},{7,6},{8,9},{9,8},{10,11... | collective-permute-start | bytes 688136 | tf_op jit(solution)/shard_map/ppermute | solution.py:665
  21.2 13.6 %collective-permute-start.5 = (f32[448,128]{1,0:T(8,128)S(1)}, f32[448,128]{1,0:T(8,128)S(1)}, u32[]{:S(2)}, u32[]{:S(2)}) collective-permute-start(f32[448,128]{1,0:T(8,128)S(1)} %get-tuple-element.53), channel_id=1, source_target_pairs={{1,2},{2,1},{5,6},{6,5},{9,10},{10,9},{13,14},{14,13},{17,18},{18,... | collective-permute-start | bytes 688136 | tf_op jit(solution)/shard_map/ppermute | solution.py:666
  21.9 12.9 %collective-permute-start.6 = (f32[448,128]{1,0:T(8,128)S(1)}, f32[448,128]{1,0:T(8,128)S(1)}, u32[]{:S(2)}, u32[]{:S(2)}) collective-permute-start(f32[448,128]{1,0:T(8,128)S(1)} %get-tuple-element.54), channel_id=1, source_target_pairs={{0,4},{4,0},{8,12},{12,8},{16,20},{20,16},{24,28},{28,24},{1,5},{5... | collective-permute-start | bytes 688136 | tf_op jit(solution)/shard_map/ppermute | solution.py:667
  22.2 12.7 %collective-permute-start.7 = (f32[448,128]{1,0:T(8,128)S(1)}, f32[448,128]{1,0:T(8,128)S(1)}, u32[]{:S(2)}, u32[]{:S(2)}) collective-permute-start(f32[448,128]{1,0:T(8,128)S(1)} %get-tuple-element.55), channel_id=1, source_target_pairs={{0,28},{4,8},{8,4},{12,16},{16,12},{20,24},{24,20},{28,0},{1,29},{... | collective-permute-start | bytes 688136 | tf_op jit(solution)/shard_map/ppermute | solution.py:668
  22.6 12.2 %collective-permute-start.11 = (bf16[768,128]{1,0:T(8,128)(2,1)S(1)}, bf16[768,128]{1,0:T(8,128)(2,1)S(1)}, u32[]{:S(2)}, u32[]{:S(2)}) collective-permute-start(bf16[768,128]{1,0:T(8,128)(2,1)S(1)} %get-tuple-element.59), channel_id=1, source_target_pairs={{0,28},{4,8},{8,4},{12,16},{16,12},{20,24},{24,20},{28,0},{1,29},{... | collective-permute-start | bytes 589832 | tf_op jit(solution)/shard_map/ppermute | solution.py:668
  37.0 6.8 %collective-permute-start.14 = (f32[32,128]{1,0:T(8,128)S(1)}, f32[32,128]{1,0:T(8,128)S(1)}, u32[]{:S(2)}, u32[]{:S(2)}) collective-permute-start(f32[32,128]{1,0:T(8,128)S(1)} %get-tuple-element.60.refs_0_), channel_id=1, source_target_pairs={{0,3},{1,0},{2,1},{3,2},{4,7},{5,4},{6,5},{7,6},{8,11},{9,8},{10,9... | collective-permute-start | bytes 49160 | tf_op jit(solution)/shard_map/ppermute | solution.py:675
  39.8 4.8 %collective-permute-start.13 = (f32[32,128]{1,0:T(8,128)S(1)}, f32[32,128]{1,0:T(8,128)S(1)}, u32[]{:S(2)}, u32[]{:S(2)}) collective-permute-start(f32[32,128]{1,0:T(8,128)S(1)} %get-tuple-element.60.refs_0_), channel_id=1, source_target_pairs={{0,2},{1,3},{2,0},{3,1},{4,6},{5,7},{6,4},{7,5},{8,10},{9,11},{10,... | collective-permute-start | bytes 49160 | tf_op jit(solution)/shard_map/ppermute | solution.py:675
  41.8 5.5 %collective-permute-start.12 = (f32[32,128]{1,0:T(8,128)S(1)}, f32[32,128]{1,0:T(8,128)S(1)}, u32[]{:S(2)}, u32[]{:S(2)}) collective-permute-start(f32[32,128]{1,0:T(8,128)S(1)} %get-tuple-element.60.refs_0_), channel_id=1, source_target_pairs={{0,1},{1,2},{2,3},{3,0},{4,5},{5,6},{6,7},{7,4},{8,9},{9,10},{10,1... | collective-permute-start | bytes 49160 | tf_op jit(solution)/shard_map/ppermute | solution.py:675
  43.8 8.5 %copy-start.4 = (bf16[1,1,3,8,128,128]{5,4,3,2,1,0:T(8,128)(2,1)S(1)}, bf16[1,1,3,8,128,128]{5,4,3,2,1,0:T(8,128)(2,1)}, u32[]{:S(2)}) copy-start(bf16[1,1,3,8,128,128]{5,4,3,2,1,0:T(8,128)(2,1)} %param.13) | copy-start | bytes 2359300
  47.5 1.2 %collective-permute-start.15 = (f32[16,128]{1,0:T(8,128)S(1)}, f32[16,128]{1,0:T(8,128)S(1)}, u32[]{:S(2)}, u32[]{:S(2)}) collective-permute-start(f32[16,128]{1,0:T(8,128)S(1)} %get-tuple-element.61), channel_id=1, source_target_pairs={{0,4},{4,0},{8,12},{12,8},{16,20},{20,16},{24,28},{28,24},{1,5},{5... | collective-permute-start | bytes 24584 | tf_op jit(solution)/shard_map/ppermute | solution.py:679
  48.8 4.9 %collective-permute-start.18 = (f32[32,128]{1,0:T(8,128)S(1)}, f32[32,128]{1,0:T(8,128)S(1)}, u32[]{:S(2)}, u32[]{:S(2)}) collective-permute-start(f32[32,128]{1,0:T(8,128)S(1)} %constant_dynamic-update-slice_fusion.refs_0_), channel_id=1, source_target_pairs={{0,24},{4,28},{8,16},{12,20},{16,8},{20,12},{24,0},{28,4},{1,25},{... | collective-permute-start | bytes 49160 | tf_op jit(solution)/shard_map/ppermute | solution.py:679
  48.8 4.9 %collective-permute-start.17 = (f32[32,128]{1,0:T(8,128)S(1)}, f32[32,128]{1,0:T(8,128)S(1)}, u32[]{:S(2)}, u32[]{:S(2)}) collective-permute-start(f32[32,128]{1,0:T(8,128)S(1)} %constant_dynamic-update-slice_fusion.refs_0_), channel_id=1, source_target_pairs={{0,16},{4,20},{8,24},{12,28},{16,0},{20,4},{24,8},{28,12},{1,17},{... | collective-permute-start | bytes 49160 | tf_op jit(solution)/shard_map/ppermute | solution.py:679
  49.3 4.7 %collective-permute-start.16 = (f32[32,128]{1,0:T(8,128)S(1)}, f32[32,128]{1,0:T(8,128)S(1)}, u32[]{:S(2)}, u32[]{:S(2)}) collective-permute-start(f32[32,128]{1,0:T(8,128)S(1)} %constant_dynamic-update-slice_fusion.refs_0_), channel_id=1, source_target_pairs={{0,8},{4,12},{8,0},{12,4},{16,24},{20,28},{24,16},{28,20},{1,9},{5... | collective-permute-start | bytes 49160 | tf_op jit(solution)/shard_map/ppermute | solution.py:679
  58.9 4.0 %collective-permute-start.21 = (f32[72,128]{1,0:T(8,128)S(1)}, f32[72,128]{1,0:T(8,128)S(1)}, u32[]{:S(2)}, u32[]{:S(2)}) collective-permute-start(f32[72,128]{1,0:T(8,128)S(1)} %get-tuple-element.68.refs_0_), channel_id=1, source_target_pairs={{0,3},{1,0},{2,1},{3,2},{4,7},{5,4},{6,5},{7,6},{8,11},{9,8},{10,9... | collective-permute-start | bytes 110600 | tf_op jit(solution)/shard_map/ppermute | solution.py:675
  58.9 5.0 %collective-permute-start.20 = (f32[72,128]{1,0:T(8,128)S(1)}, f32[72,128]{1,0:T(8,128)S(1)}, u32[]{:S(2)}, u32[]{:S(2)}) collective-permute-start(f32[72,128]{1,0:T(8,128)S(1)} %get-tuple-element.68.refs_0_), channel_id=1, source_target_pairs={{0,2},{1,3},{2,0},{3,1},{4,6},{5,7},{6,4},{7,5},{8,10},{9,11},{10,... | collective-permute-start | bytes 110600 | tf_op jit(solution)/shard_map/ppermute | solution.py:675
  59.1 6.6 %collective-permute-start.19 = (f32[72,128]{1,0:T(8,128)S(1)}, f32[72,128]{1,0:T(8,128)S(1)}, u32[]{:S(2)}, u32[]{:S(2)}) collective-permute-start(f32[72,128]{1,0:T(8,128)S(1)} %get-tuple-element.68.refs_0_), channel_id=1, source_target_pairs={{0,1},{1,2},{2,3},{3,0},{4,5},{5,6},{6,7},{7,4},{8,9},{9,10},{10,1... | collective-permute-start | bytes 110600 | tf_op jit(solution)/shard_map/ppermute | solution.py:675
  66.0 1.3 %collective-permute-start.22 = (f32[64,128]{1,0:T(8,128)S(1)}, f32[64,128]{1,0:T(8,128)S(1)}, u32[]{:S(2)}, u32[]{:S(2)}) collective-permute-start(f32[64,128]{1,0:T(8,128)S(1)} %get-tuple-element.69), channel_id=1, source_target_pairs={{0,4},{4,0},{8,12},{12,8},{16,20},{20,16},{24,28},{28,24},{1,5},{5... | collective-permute-start | bytes 98312 | tf_op jit(solution)/shard_map/ppermute | solution.py:679
  67.2 5.2 %collective-permute-start.25 = (f32[128,128]{1,0:T(8,128)S(1)}, f32[128,128]{1,0:T(8,128)S(1)}, u32[]{:S(2)}, u32[]{:S(2)}) collective-permute-start(f32[128,128]{1,0:T(8,128)S(1)} %constant_dynamic-update-slice_fusion.2.refs_0_), channel_id=1, source_target_pairs={{0,24},{4,28},{8,16},{12,20},{16,8},{20,12},{24,0},{28,4},{1,25},{... | collective-permute-start | bytes 196616 | tf_op jit(solution)/shard_map/ppermute | solution.py:679
  69.1 12.7 %collective-permute-start.26 = (f32[384,128]{1,0:T(8,128)S(1)}, f32[384,128]{1,0:T(8,128)S(1)}, u32[]{:S(2)}, u32[]{:S(2)}) collective-permute-start(f32[384,128]{1,0:T(8,128)S(1)} %get-tuple-element.72), channel_id=1, source_target_pairs={{0,1},{1,0},{2,3},{3,2},{4,5},{5,4},{6,7},{7,6},{8,9},{9,8},{10,11... | collective-permute-start | bytes 589832 | tf_op jit(solution)/shard_map/ppermute | solution.py:665
  69.3 12.5 %collective-permute-start.27 = (f32[384,128]{1,0:T(8,128)S(1)}, f32[384,128]{1,0:T(8,128)S(1)}, u32[]{:S(2)}, u32[]{:S(2)}) collective-permute-start(f32[384,128]{1,0:T(8,128)S(1)} %get-tuple-element.73), channel_id=1, source_target_pairs={{1,2},{2,1},{5,6},{6,5},{9,10},{10,9},{13,14},{14,13},{17,18},{18,... | collective-permute-start | bytes 589832 | tf_op jit(solution)/shard_map/ppermute | solution.py:666
  70.0 11.8 %collective-permute-start.28 = (f32[384,128]{1,0:T(8,128)S(1)}, f32[384,128]{1,0:T(8,128)S(1)}, u32[]{:S(2)}, u32[]{:S(2)}) collective-permute-start(f32[384,128]{1,0:T(8,128)S(1)} %get-tuple-element.74), channel_id=1, source_target_pairs={{0,4},{4,0},{8,12},{12,8},{16,20},{20,16},{24,28},{28,24},{1,5},{5... | collective-permute-start | bytes 589832 | tf_op jit(solution)/shard_map/ppermute | solution.py:667
  70.1 11.7 %collective-permute-start.29 = (f32[384,128]{1,0:T(8,128)S(1)}, f32[384,128]{1,0:T(8,128)S(1)}, u32[]{:S(2)}, u32[]{:S(2)}) collective-permute-start(f32[384,128]{1,0:T(8,128)S(1)} %get-tuple-element.75), channel_id=1, source_target_pairs={{0,28},{4,8},{8,4},{12,16},{16,12},{20,24},{24,20},{28,0},{1,29},{... | collective-permute-start | bytes 589832 | tf_op jit(solution)/shard_map/ppermute | solution.py:668
  72.4 5.1 %collective-permute-start.24 = (f32[128,128]{1,0:T(8,128)S(1)}, f32[128,128]{1,0:T(8,128)S(1)}, u32[]{:S(2)}, u32[]{:S(2)}) collective-permute-start(f32[128,128]{1,0:T(8,128)S(1)} %constant_dynamic-update-slice_fusion.2.refs_0_), channel_id=1, source_target_pairs={{0,16},{4,20},{8,24},{12,28},{16,0},{20,4},{24,8},{28,12},{1,17},{... | collective-permute-start | bytes 196616 | tf_op jit(solution)/shard_map/ppermute | solution.py:679
  77.5 4.3 %collective-permute-start.23 = (f32[128,128]{1,0:T(8,128)S(1)}, f32[128,128]{1,0:T(8,128)S(1)}, u32[]{:S(2)}, u32[]{:S(2)}) collective-permute-start(f32[128,128]{1,0:T(8,128)S(1)} %constant_dynamic-update-slice_fusion.2.refs_0_), channel_id=1, source_target_pairs={{0,8},{4,12},{8,0},{12,4},{16,24},{20,28},{24,16},{28,20},{1,9},{5... | collective-permute-start | bytes 196616 | tf_op jit(solution)/shard_map/ppermute | solution.py:679
  89.6 5.7 %collective-permute-start.32 = (f32[8,128]{1,0:T(8,128)S(1)}, f32[8,128]{1,0:T(8,128)S(1)}, u32[]{:S(2)}, u32[]{:S(2)}) collective-permute-start(f32[8,128]{1,0:T(8,128)S(1)} %get-tuple-element.83), channel_id=1, source_target_pairs={{0,3},{1,0},{2,1},{3,2},{4,7},{5,4},{6,5},{7,6},{8,11},{9,8},{10,9... | collective-permute-start | bytes 12296 | tf_op jit(solution)/shard_map/ppermute | solution.py:675
  91.1 4.5 %collective-permute-start.31 = (f32[8,128]{1,0:T(8,128)S(1)}, f32[8,128]{1,0:T(8,128)S(1)}, u32[]{:S(2)}, u32[]{:S(2)}) collective-permute-start(f32[8,128]{1,0:T(8,128)S(1)} %get-tuple-element.83), channel_id=1, source_target_pairs={{0,2},{1,3},{2,0},{3,1},{4,6},{5,7},{6,4},{7,5},{8,10},{9,11},{10,... | collective-permute-start | bytes 12296 | tf_op jit(solution)/shard_map/ppermute | solution.py:675
  94.0 5.4 %collective-permute-start.30 = (f32[8,128]{1,0:T(8,128)S(1)}, f32[8,128]{1,0:T(8,128)S(1)}, u32[]{:S(2)}, u32[]{:S(2)}) collective-permute-start(f32[8,128]{1,0:T(8,128)S(1)} %get-tuple-element.83), channel_id=1, source_target_pairs={{0,1},{1,2},{2,3},{3,0},{4,5},{5,6},{6,7},{7,4},{8,9},{9,10},{10,1... | collective-permute-start | bytes 12296 | tf_op jit(solution)/shard_map/ppermute | solution.py:675
  99.4 1.2 %collective-permute-start.33 = (f32[8,128]{1,0:T(8,128)S(1)}, f32[8,128]{1,0:T(8,128)S(1)}, u32[]{:S(2)}, u32[]{:S(2)}) collective-permute-start(f32[8,128]{1,0:T(8,128)S(1)} %add_add_fusion.1), channel_id=1, source_target_pairs={{0,4},{4,0},{8,12},{12,8},{16,20},{20,16},{24,28},{28,24},{1,5},{5... | collective-permute-start | bytes 12296 | tf_op jit(solution)/shard_map/ppermute | solution.py:679
  100.6 4.5 %collective-permute-start.36 = (f32[8,128]{1,0:T(8,128)S(1)}, f32[8,128]{1,0:T(8,128)S(1)}, u32[]{:S(2)}, u32[]{:S(2)}) collective-permute-start(f32[8,128]{1,0:T(8,128)S(1)} %add.24), channel_id=1, source_target_pairs={{0,24},{4,28},{8,16},{12,20},{16,8},{20,12},{24,0},{28,4},{1,25},{... | collective-permute-start | bytes 12296 | tf_op jit(solution)/shard_map/ppermute | solution.py:679
  103.2 3.6 %collective-permute-start.35 = (f32[8,128]{1,0:T(8,128)S(1)}, f32[8,128]{1,0:T(8,128)S(1)}, u32[]{:S(2)}, u32[]{:S(2)}) collective-permute-start(f32[8,128]{1,0:T(8,128)S(1)} %add.24), channel_id=1, source_target_pairs={{0,16},{4,20},{8,24},{12,28},{16,0},{20,4},{24,8},{28,12},{1,17},{... | collective-permute-start | bytes 12296 | tf_op jit(solution)/shard_map/ppermute | solution.py:679
  103.8 4.0 %collective-permute-start.34 = (f32[8,128]{1,0:T(8,128)S(1)}, f32[8,128]{1,0:T(8,128)S(1)}, u32[]{:S(2)}, u32[]{:S(2)}) collective-permute-start(f32[8,128]{1,0:T(8,128)S(1)} %add.24), channel_id=1, source_target_pairs={{0,8},{4,12},{8,0},{12,4},{16,24},{20,28},{24,16},{28,20},{1,9},{5... | collective-permute-start | bytes 12296 | tf_op jit(solution)/shard_map/ppermute | solution.py:679
  104.1 4.6 %collective-permute-start.37 = (bf16[384,128]{1,0:T(8,128)(2,1)S(1)}, bf16[384,128]{1,0:T(8,128)(2,1)S(1)}, u32[]{:S(2)}, u32[]{:S(2)}) collective-permute-start(bf16[384,128]{1,0:T(8,128)(2,1)S(1)} %get-tuple-element.84), channel_id=1, source_target_pairs={{0,1},{1,0},{2,3},{3,2},{4,5},{5,4},{6,7},{7,6},{8,9},{9,8},{10,11... | collective-permute-start | bytes 294920 | tf_op jit(solution)/shard_map/ppermute | solution.py:665
  104.1 4.6 %collective-permute-start.38 = (bf16[384,128]{1,0:T(8,128)(2,1)S(1)}, bf16[384,128]{1,0:T(8,128)(2,1)S(1)}, u32[]{:S(2)}, u32[]{:S(2)}) collective-permute-start(bf16[384,128]{1,0:T(8,128)(2,1)S(1)} %get-tuple-element.85), channel_id=1, source_target_pairs={{1,2},{2,1},{5,6},{6,5},{9,10},{10,9},{13,14},{14,13},{17,18},{18,... | collective-permute-start | bytes 294920 | tf_op jit(solution)/shard_map/ppermute | solution.py:666
  105.1 3.6 %collective-permute-start.39 = (bf16[384,128]{1,0:T(8,128)(2,1)S(1)}, bf16[384,128]{1,0:T(8,128)(2,1)S(1)}, u32[]{:S(2)}, u32[]{:S(2)}) collective-permute-start(bf16[384,128]{1,0:T(8,128)(2,1)S(1)} %get-tuple-element.86), channel_id=1, source_target_pairs={{0,4},{4,0},{8,12},{12,8},{16,20},{20,16},{24,28},{28,24},{1,5},{5... | collective-permute-start | bytes 294920 | tf_op jit(solution)/shard_map/ppermute | solution.py:667
  106.8 4.9 %collective-permute-start.40 = (bf16[384,128]{1,0:T(8,128)(2,1)S(1)}, bf16[384,128]{1,0:T(8,128)(2,1)S(1)}, u32[]{:S(2)}, u32[]{:S(2)}) collective-permute-start(bf16[384,128]{1,0:T(8,128)(2,1)S(1)} %get-tuple-element.87), channel_id=1, source_target_pairs={{0,28},{4,8},{8,4},{12,16},{16,12},{20,24},{24,20},{28,0},{1,29},{... | collective-permute-start | bytes 294920 | tf_op jit(solution)/shard_map/ppermute | solution.py:668
